TPU v7x, 128 devices: a whole 4x4x4 slice. The times are simulated.
128 devices in a mesh: rep: 1, dp: 128 (over x, y, z, core).
Axes of the slice: x: 4, y: 4, z: 4, core: 2. Of those that a mesh axis runs over, the one named last changes fastest.
Arguments:
- x: bfloat16 [128, 1024, 1536], P(('rep', 'dp'))
- dy: bfloat16 [128, 1024, 1536], P(('rep', 'dp'))
- w_gate: bfloat16 [2, 1536, 4224], replicated
- w_up: bfloat16 [2, 1536, 4224], replicated
- w_down: bfloat16 [2, 4224, 1536], replicated
- m_w_gate: float32 [2, 1536, 4224], P(None, 'dp')
- m_w_up: float32 [2, 1536, 4224], P(None, 'dp')
- m_w_down: float32 [2, 4224, 1536], P(None, 'dp')
- v_w_gate: float32 [2, 1536, 4224], P(None, 'dp')
- v_w_up: float32 [2, 1536, 4224], P(None, 'dp')
- v_w_down: float32 [2, 4224, 1536], P(None, 'dp')
Outputs:
- output 1: bfloat16 [2, 1536, 4224], P('rep')
- output 2: bfloat16 [2, 1536, 4224], P('rep')
- output 3: bfloat16 [2, 4224, 1536], P('rep')
- output 4: float32 [2, 1536, 4224], P('rep', 'dp')
- output 5: float32 [2, 1536, 4224], P('rep', 'dp')
- output 6: float32 [2, 4224, 1536], P('rep', 'dp')
- output 7: float32 [2, 1536, 4224], P('rep', 'dp')
- output 8: float32 [2, 1536, 4224], P('rep', 'dp')
- output 9: float32 [2, 4224, 1536], P('rep', 'dp')
All inputs are finite; a program needn't handle non-finite values.
Results may differ from a plain program's by a relative error of at most 0.022.
Values are sent between devices in bfloat16 or wider.
A program may use at most 1.5 GiB of HBM per device.

v0:
```python
import jax
import jax.numpy as jnp
from jax import lax

NAMES = ("w_gate", "w_up", "w_down")


def matmul(a, w):
    return jnp.dot(a, w, preferred_element_type=jnp.float32).astype(jnp.bfloat16)


def normed(h):
    wide = h.astype(jnp.float32)
    scale = lax.rsqrt(jnp.mean(wide**2, -1, keepdims=True) + 1e-6)
    return (wide * scale).astype(jnp.bfloat16)


def layer(h, w):
    a = normed(h)
    gate = jnp.dot(a, w["w_gate"], preferred_element_type=jnp.float32)
    up = jnp.dot(a, w["w_up"], preferred_element_type=jnp.float32)
    return h + matmul((jax.nn.silu(gate) * up).astype(jnp.bfloat16), w["w_down"])


def adamw(w, m, v, g):
    m = 0.9 * m + 0.1 * g
    v = 0.95 * v + 0.05 * g * g
    step = m * lax.rsqrt(v + 1e-8) + 0.1 * w
    return (w - 0.02 * step).astype(jnp.bfloat16), m, v


def clipped(gradients, sum_of_squares, count):
    factor = jnp.minimum(1.0, 0.5 * lax.rsqrt(sum_of_squares / count + 1e-30))
    return [g * factor for g in gradients]


def stack(weights, h):
    for number in range(weights["w_gate"].shape[0]):
        h = layer(h, {name: w[number] for name, w in weights.items()})
    return h


def solution(mesh):
    groups = mesh.shape["rep"]

    def step(x, dy, *arrays):
        weights, m, v = (arrays[i : i + 3] for i in (0, 3, 6))
        x, dy = (t.reshape(groups, -1, *t.shape[1:]) for t in (x, dy))

        def of_a_group(x, dy):
            _, back = jax.vjp(lambda w: stack(w, x), dict(zip(NAMES, weights, strict=True)))
            by_weights = back(dy)[0]
            gradients = [by_weights[name].astype(jnp.float32) for name in NAMES]
            gradients = clipped(gradients, sum(jnp.sum(g * g) for g in gradients), sum(g.size for g in gradients))
            new = [adamw(w.astype(jnp.float32), m, v, g) for w, m, v, g in zip(weights, m, v, gradients, strict=True)]
            return tuple(one[which] for which in range(3) for one in new)

        return tuple(t.reshape(-1, *t.shape[2:]) for t in jax.vmap(of_a_group)(x, dy))

    return step
```

profile of v0, /device:TPU:1, one launch (start us, length us, event | category | flops | bytes accessed | tf_op | source)
XLA Modules:
  0.0 4151.5 jit_solution(11817466275495519514)
XLA Ops:
  28.5 23.3 fusion.40
  123.6 28.1 fusion.66
  151.6 363.0 %fusion.4 = f32[40,1536]{1,0:T(8,128)S(1)} fusion(f32[4224,1536]{1,0:T(8,128)} %fusion.66), kind=kCustom, calls=%all-reduce-scatter.4 | all-reduce-scatter fusion | flops 7864321 | bytes 26198016
  579.9 24.4 fusion.79
  627.2 365.9 %fusion.5 = f32[1536,40]{0,1:T(8,128)S(1)} fusion(f32[1536,4224]{0,1:T(8,128)} %fusion.167), kind=kCustom, calls=%all-reduce-scatter.5 | all-reduce-scatter fusion | flops 7864321 | bytes 26198016
  995.6 26.0 fusion.49
  1067.1 407.3 %fusion.2 = f32[4224,16]{0,1:T(8,128)S(1)} fusion(f32[4224,1536]{0,1:T(8,128)} %fusion.49), kind=kCustom, calls=%all-reduce-scatter.2 | all-reduce-scatter fusion | flops 8650753 | bytes 26222592
  1474.4 26.0 fusion.8
  1500.4 407.3 %fusion.3 = f32[4224,16]{0,1:T(8,128)S(1)} fusion(f32[4224,1536]{0,1:T(8,128)} %fusion.8), kind=kCustom, calls=%all-reduce-scatter.3 | all-reduce-scatter fusion | flops 8650753 | bytes 26222592
  1907.7 407.3 %fusion = f32[4224,16]{0,1:T(8,128)S(1)} fusion(f32[4224,1536]{0,1:T(8,128)} %fusion.157), kind=kCustom, calls=%all-reduce-scatter | all-reduce-scatter fusion | flops 8650753 | bytes 26222592
  2315.0 33.8 fusion.16
  2351.6 407.3 %fusion.1 = f32[4224,16]{0,1:T(8,128)S(1)} fusion(f32[4224,1536]{0,1:T(8,128)} %fusion.16), kind=kCustom, calls=%all-reduce-scatter.1 | all-reduce-scatter fusion | flops 8650753 | bytes 26222592
  3224.3 39.2 concatenate.4
  3263.5 39.2 concatenate.5
  3337.8 96.8 %concatenate.2 = bf16[4224,524]{0,1:T(8,128)(2,1)} concatenate(bf16[4224,12]{0,1:T(8,128)(2,1)S(1)} %collective-permute-done.95, bf16[4224,16]{0,1:T(8,128)(2,1)} %collective-permute-done.94, bf16[4224,16]{0,1:T(8,128)(2,1)} %collective-permute-done.93, bf16[4224,16]{0,1:T(8,128)(2,1)} %copy-done.30, bf16[4224,16]{0,1:T(8,128)(2,1)} %copy-done.28, bf16[4224,16]{0,1:T(8,128)(2,1)} %copy-done.26, ...), dimensions={1} | concatenate | bytes 8988672
  3445.6 98.3 %concatenate.3 = bf16[4224,524]{0,1:T(8,128)(2,1)} concatenate(bf16[4224,12]{0,1:T(8,128)(2,1)S(1)} %collective-permute-done.127, bf16[4224,16]{0,1:T(8,128)(2,1)} %copy-done.55, bf16[4224,16]{0,1:T(8,128)(2,1)} %copy-done.53, bf16[4224,16]{0,1:T(8,128)(2,1)} %copy-done.51, bf16[4224,16]{0,1:T(8,128)(2,1)} %copy-done.50, bf16[4224,16]{0,1:T(8,128)(2,1)} %copy-done.49, ...), dimensions={1} | concatenate | bytes 8988672
  3554.7 98.3 %concatenate = bf16[4224,524]{0,1:T(8,128)(2,1)} concatenate(bf16[4224,12]{0,1:T(8,128)(2,1)S(1)} %collective-permute-done.31, bf16[4224,16]{0,1:T(8,128)(2,1)} %copy-done.82, bf16[4224,16]{0,1:T(8,128)(2,1)} %copy-done.80, bf16[4224,16]{0,1:T(8,128)(2,1)} %copy-done.77, bf16[4224,16]{0,1:T(8,128)(2,1)} %copy-done.76, bf16[4224,16]{0,1:T(8,128)(2,1)} %copy-done.75, ...), dimensions={1} | concatenate | bytes 8988672
  3667.3 96.1 %concatenate.1 = bf16[4224,524]{0,1:T(8,128)(2,1)} concatenate(bf16[4224,12]{0,1:T(8,128)(2,1)S(1)} %collective-permute-done.63, bf16[4224,16]{0,1:T(8,128)(2,1)} %collective-permute-done.62, bf16[4224,16]{0,1:T(8,128)(2,1)} %copy-done.99, bf16[4224,16]{0,1:T(8,128)(2,1)S(1)} %collective-permute-done.60, bf16[4224,16]{0,1:T(8,128)(2,1)S(1)} %collective-permute-done.59, ...), dimensions={1} | concatenate | bytes 8988672
  3767.1 66.0 %all-reduce.10 = f32[]{:T(128)} all-reduce(f32[]{:T(128)S(6)} %add.102), channel_id=3, replica_groups=mesh['rep'=1,'dp'=128] {'dp'}, use_global_device_ids=true, to_apply=%region_3.4.clone | all-reduce | flops 1 | bytes 8 | tf_op jit(solution)/vmap()/reduce_sum | solution.py:54
  3847.3 80.6 %all-gather.14.cloned.1.call-done = bf16[1,2,4224,1536]{3,1,0,2:T(2,128)(2,1)} async-done(((bf16[1,2,33,1536]{3,1,0,2:T(2,128)(2,1)}), bf16[1,2,4224,1536]{3,1,0,2:T(2,128)(2,1)}) %all-gather.14.cloned.1.call-update) | async-done | bytes 25952272 | tf_op jit(solution)/reshape | solution.py:58
  3927.9 24.0 copy.23
  3951.8 72.9 %all-gather.12.cloned.1.call-done = bf16[1,2,1536,4224]{3,1,0,2:T(2,128)(2,1)} async-done(((bf16[1,2,12,4224]{3,1,0,2:T(2,128)(2,1)}), bf16[1,2,1536,4224]{3,1,0,2:T(2,128)(2,1)}) %all-gather.12.cloned.1.call-update) | async-done | bytes 25952272 | tf_op jit(solution)/reshape | solution.py:58
  4024.8 23.1 copy.22
  4047.9 73.8 %all-gather.10.cloned.1.call-done = bf16[1,2,1536,4224]{3,1,0,2:T(2,128)(2,1)} async-done(((bf16[1,2,12,4224]{3,1,0,2:T(2,128)(2,1)}), bf16[1,2,1536,4224]{3,1,0,2:T(2,128)(2,1)}) %all-gather.10.cloned.1.call-update) | async-done | bytes 25952272 | tf_op jit(solution)/reshape | solution.py:58
  (682 shorter events, 803.0 us)
Async XLA Ops:
  7.2 3920.7 %all-gather.14.cloned.1.call-start = ((), (), s32[]{:S(2)}) async-start(), calls=%async_computation.2 | async-start | bytes 26155008 | tf_op jit(solution)/reshape | solution.py:58
  515.4 2251.0 %collective-permute-start.128 = (bf16[40,1536]{1,0:T(8,128)(2,1)}, bf16[40,1536]{1,0:T(8,128)(2,1)}, u32[]{:S(2)}, u32[]{:S(2)}) collective-permute-start(bf16[40,1536]{1,0:T(8,128)(2,1)} %convert.381), channel_id=1, source_target_pairs={{0,1},{1,2},{2,3},{3,4},{4,5},{5,6},{6,7},{7,8},{8,9},{9,10},{10,1... | collective-permute-start | bytes 368648
  518.4 2249.9 %collective-permute-start.129 = (bf16[40,1536]{1,0:T(8,128)(2,1)}, bf16[40,1536]{1,0:T(8,128)(2,1)}, u32[]{:S(2)}, u32[]{:S(2)}) collective-permute-start(bf16[40,1536]{1,0:T(8,128)(2,1)} %convert.381), channel_id=1, source_target_pairs={{0,2},{1,3},{2,4},{3,5},{4,6},{5,7},{6,8},{7,9},{8,10},{9,11},{10,... | collective-permute-start | bytes 368648
  520.3 2249.9 %collective-permute-start.130 = (bf16[40,1536]{1,0:T(8,128)(2,1)}, bf16[40,1536]{1,0:T(8,128)(2,1)}, u32[]{:S(2)}, u32[]{:S(2)}) collective-permute-start(bf16[40,1536]{1,0:T(8,128)(2,1)} %convert.381), channel_id=1, source_target_pairs={{0,3},{1,4},{2,5},{3,6},{4,7},{5,8},{6,9},{7,10},{8,11},{9,12},{10... | collective-permute-start | bytes 368648
  522.9 1826.0 %collective-permute-start.150 = (bf16[9,1536]{1,0:T(8,128)(2,1)}, bf16[9,1536]{1,0:T(8,128)(2,1)}, u32[]{:S(2)}, u32[]{:S(2)}) collective-permute-start(bf16[9,1536]{1,0:T(8,128)(2,1)} %slice.28), channel_id=1, source_target_pairs={{0,23},{1,24},{2,25},{3,26},{4,27},{5,28},{6,29},{7,30},{8,31},{9,... | collective-permute-start | bytes 82952
  993.7 1356.6 %collective-permute-start.173 = (bf16[1536,9]{0,1:T(8,128)(2,1)}, bf16[1536,9]{0,1:T(8,128)(2,1)}, u32[]{:S(2)}, u32[]{:S(2)}) collective-permute-start(bf16[1536,9]{0,1:T(8,128)(2,1)} %slice.29), channel_id=1, source_target_pairs={{0,23},{1,24},{2,25},{3,26},{4,27},{5,28},{6,29},{7,30},{8,31},{9,... | collective-permute-start | bytes 82952
  2348.9 410.1 %collective-permute-start.95 = (bf16[4224,12]{0,1:T(8,128)(2,1)S(1)}, bf16[4224,12]{0,1:T(8,128)(2,1)S(1)}, u32[]{:S(2)}, u32[]{:S(2)}) collective-permute-start(bf16[4224,12]{0,1:T(8,128)(2,1)S(1)} %slice.26), channel_id=1, source_target_pairs={{0,32},{1,33},{2,34},{3,35},{4,36},{5,37},{6,38},{7,39},{8,40},{9,... | collective-permute-start | bytes 304136
  2350.3 410.0 %collective-permute-start.127 = (bf16[4224,12]{0,1:T(8,128)(2,1)S(1)}, bf16[4224,12]{0,1:T(8,128)(2,1)S(1)}, u32[]{:S(2)}, u32[]{:S(2)}) collective-permute-start(bf16[4224,12]{0,1:T(8,128)(2,1)S(1)} %slice.27), channel_id=1, source_target_pairs={{0,32},{1,33},{2,34},{3,35},{4,36},{5,37},{6,38},{7,39},{8,40},{9,... | collective-permute-start | bytes 304136
  3321.4 113.3 %collective-permute-start.43 = (bf16[4224,16]{0,1:T(8,128)(2,1)S(1)}, bf16[4224,16]{0,1:T(8,128)(2,1)}, u32[]{:S(2)}, u32[]{:S(2)}) collective-permute-start(bf16[4224,16]{0,1:T(8,128)(2,1)S(1)} %convert.380), channel_id=1, source_target_pairs={{0,12},{1,13},{2,14},{3,15},{4,16},{5,17},{6,18},{7,19},{8,20},{9,... | collective-permute-start | bytes 405512
  3325.5 110.7 %collective-permute-start.44 = (bf16[4224,16]{0,1:T(8,128)(2,1)S(1)}, bf16[4224,16]{0,1:T(8,128)(2,1)}, u32[]{:S(2)}, u32[]{:S(2)}) collective-permute-start(bf16[4224,16]{0,1:T(8,128)(2,1)S(1)} %convert.380), channel_id=1, source_target_pairs={{0,13},{1,14},{2,15},{3,16},{4,17},{5,18},{6,19},{7,20},{8,21},{9,... | collective-permute-start | bytes 405512
  3329.1 108.8 %collective-permute-start.45 = (bf16[4224,16]{0,1:T(8,128)(2,1)S(1)}, bf16[4224,16]{0,1:T(8,128)(2,1)}, u32[]{:S(2)}, u32[]{:S(2)}) collective-permute-start(bf16[4224,16]{0,1:T(8,128)(2,1)S(1)} %convert.380), channel_id=1, source_target_pairs={{0,14},{1,15},{2,16},{3,17},{4,18},{5,19},{6,20},{7,21},{8,22},{9,... | collective-permute-start | bytes 405512
  3331.8 109.4 %collective-permute-start.46 = (bf16[4224,16]{0,1:T(8,128)(2,1)S(1)}, bf16[4224,16]{0,1:T(8,128)(2,1)}, u32[]{:S(2)}, u32[]{:S(2)}) collective-permute-start(bf16[4224,16]{0,1:T(8,128)(2,1)S(1)} %convert.380), channel_id=1, source_target_pairs={{0,15},{1,16},{2,17},{3,18},{4,19},{5,20},{6,21},{7,22},{8,23},{9,... | collective-permute-start | bytes 405512
  3333.7 108.9 %collective-permute-start.47 = (bf16[4224,16]{0,1:T(8,128)(2,1)S(1)}, bf16[4224,16]{0,1:T(8,128)(2,1)}, u32[]{:S(2)}, u32[]{:S(2)}) collective-permute-start(bf16[4224,16]{0,1:T(8,128)(2,1)S(1)} %convert.380), channel_id=1, source_target_pairs={{0,16},{1,17},{2,18},{3,19},{4,20},{5,21},{6,22},{7,23},{8,24},{9,... | collective-permute-start | bytes 405512
  3434.7 109.2 %collective-permute-start.48 = (bf16[4224,16]{0,1:T(8,128)(2,1)S(1)}, bf16[4224,16]{0,1:T(8,128)(2,1)S(1)}, u32[]{:S(2)}, u32[]{:S(2)}) collective-permute-start(bf16[4224,16]{0,1:T(8,128)(2,1)S(1)} %convert.380), channel_id=1, source_target_pairs={{0,17},{1,18},{2,19},{3,20},{4,21},{5,22},{6,23},{7,24},{8,25},{9,... | collective-permute-start | bytes 405512
  3436.2 109.1 %collective-permute-start.49 = (bf16[4224,16]{0,1:T(8,128)(2,1)S(1)}, bf16[4224,16]{0,1:T(8,128)(2,1)S(1)}, u32[]{:S(2)}, u32[]{:S(2)}) collective-permute-start(bf16[4224,16]{0,1:T(8,128)(2,1)S(1)} %convert.380), channel_id=1, source_target_pairs={{0,18},{1,19},{2,20},{3,21},{4,22},{5,23},{6,24},{7,25},{8,26},{9,... | collective-permute-start | bytes 405512
  3437.8 109.4 %collective-permute-start.50 = (bf16[4224,16]{0,1:T(8,128)(2,1)S(1)}, bf16[4224,16]{0,1:T(8,128)(2,1)S(1)}, u32[]{:S(2)}, u32[]{:S(2)}) collective-permute-start(bf16[4224,16]{0,1:T(8,128)(2,1)S(1)} %convert.380), channel_id=1, source_target_pairs={{0,19},{1,20},{2,21},{3,22},{4,23},{5,24},{6,25},{7,26},{8,27},{9,... | collective-permute-start | bytes 405512
  3441.2 108.3 %collective-permute-start.51 = (bf16[4224,16]{0,1:T(8,128)(2,1)S(1)}, bf16[4224,16]{0,1:T(8,128)(2,1)S(1)}, u32[]{:S(2)}, u32[]{:S(2)}) collective-permute-start(bf16[4224,16]{0,1:T(8,128)(2,1)S(1)} %convert.380), channel_id=1, source_target_pairs={{0,20},{1,21},{2,22},{3,23},{4,24},{5,25},{6,26},{7,27},{8,28},{9,... | collective-permute-start | bytes 405512
  3442.6 109.2 %collective-permute-start.52 = (bf16[4224,16]{0,1:T(8,128)(2,1)S(1)}, bf16[4224,16]{0,1:T(8,128)(2,1)S(1)}, u32[]{:S(2)}, u32[]{:S(2)}) collective-permute-start(bf16[4224,16]{0,1:T(8,128)(2,1)S(1)} %convert.380), channel_id=1, source_target_pairs={{0,21},{1,22},{2,23},{3,24},{4,25},{5,26},{6,27},{7,28},{8,29},{9,... | collective-permute-start | bytes 405512
  3543.9 109.1 %collective-permute-start.53 = (bf16[4224,16]{0,1:T(8,128)(2,1)S(1)}, bf16[4224,16]{0,1:T(8,128)(2,1)S(1)}, u32[]{:S(2)}, u32[]{:S(2)}) collective-permute-start(bf16[4224,16]{0,1:T(8,128)(2,1)S(1)} %convert.380), channel_id=1, source_target_pairs={{0,22},{1,23},{2,24},{3,25},{4,26},{5,27},{6,28},{7,29},{8,30},{9,... | collective-permute-start | bytes 405512
  3545.3 109.4 %collective-permute-start.54 = (bf16[4224,16]{0,1:T(8,128)(2,1)S(1)}, bf16[4224,16]{0,1:T(8,128)(2,1)S(1)}, u32[]{:S(2)}, u32[]{:S(2)}) collective-permute-start(bf16[4224,16]{0,1:T(8,128)(2,1)S(1)} %convert.380), channel_id=1, source_target_pairs={{0,23},{1,24},{2,25},{3,26},{4,27},{5,28},{6,29},{7,30},{8,31},{9,... | collective-permute-start | bytes 405512
  3547.3 109.2 %collective-permute-start.55 = (bf16[4224,16]{0,1:T(8,128)(2,1)S(1)}, bf16[4224,16]{0,1:T(8,128)(2,1)}, u32[]{:S(2)}, u32[]{:S(2)}) collective-permute-start(bf16[4224,16]{0,1:T(8,128)(2,1)S(1)} %convert.380), channel_id=1, source_target_pairs={{0,24},{1,25},{2,26},{3,27},{4,28},{5,29},{6,30},{7,31},{8,32},{9,... | collective-permute-start | bytes 405512
  3549.6 108.2 %collective-permute-start.56 = (bf16[4224,16]{0,1:T(8,128)(2,1)S(1)}, bf16[4224,16]{0,1:T(8,128)(2,1)}, u32[]{:S(2)}, u32[]{:S(2)}) collective-permute-start(bf16[4224,16]{0,1:T(8,128)(2,1)S(1)} %convert.380), channel_id=1, source_target_pairs={{0,25},{1,26},{2,27},{3,28},{4,29},{5,30},{6,31},{7,32},{8,33},{9,... | collective-permute-start | bytes 405512
  3836.1 188.7 %all-gather.12.cloned.1.call-start = ((), (), s32[]{:S(2)}) async-start(), calls=%async_computation.1 | async-start | bytes 26155008 | tf_op jit(solution)/reshape | solution.py:58
  3838.6 283.1 %all-gather.10.cloned.1.call-start = ((), (), s32[]{:S(2)}) async-start(), calls=%async_computation | async-start | bytes 26155008 | tf_op jit(solution)/reshape | solution.py:58
  (292 other events, 12041.0 us)
Sparse Core Ops, SparseCore 0:
  3836.2 91.6 all-gather.13
  3931.4 93.3 all-gather.11
  4028.3 93.3 all-gather.9
where the time goes:
time: 4200 us; the launch traced here: 4150 us
  blocking collectives  2420 us (58%)
  local copies, waits for them, and re-layouts  558 us (13%)
  starting transfers between devices  527 us (13%)
  matrix products  349 us (8%)
  waiting for transfers between devices  238 us (6%)
    unnamed x6, blocking collectives  2360 us
    unnamed x299, local copies, waits for them, and re-layouts  550 us
    unnamed x174, starting transfers between devices  527 us
    reshape x3, waiting for transfers between devices, step(): t.reshape(-1, *t.shape[2:])  227 us
    dot_general x5, matrix products, layer(): up = jnp.dot(a, w['w_up'], preferred_element_type=jnp.float32)  120 us
    dot_general x5, matrix products, layer(): gate = jnp.dot(a, w['w_gate'], preferred_element_type=jnp.float32)  115 us
    dot_general x5, matrix products, matmul(): jnp.dot(a, w, preferred_element_type=jnp.float32).astype(jnp.bfloat16)  114 us
  transfers between devices with their start and end apart: 177, of which 10 were waited for; matrix products, arithmetic and copies ran while one was open for 64% of the time, Pallas kernels for 0%

commit v1 on v0

v1 whole, which is shorter than its diff:
```python
import jax
import jax.numpy as jnp
from jax import lax
from jax.sharding import PartitionSpec as P

F32, BF16 = jnp.float32, jnp.bfloat16
CLIP_EPS = 1e-30


def dot(a, b, dims):
    return lax.dot_general(a, b, (dims, ((), ())), preferred_element_type=F32)


def norm_scale(h):
    wide = h.astype(F32)
    return wide, lax.rsqrt(jnp.mean(wide * wide, -1, keepdims=True) + 1e-6)


def normed(h):
    wide, scale = norm_scale(h)
    return (wide * scale).astype(BF16)


def hidden_back(gate, up, dp):
    dp = dp.astype(F32)
    s = jax.nn.sigmoid(gate)
    act = gate * s
    return (dp * up * (s + act * (1.0 - s))).astype(BF16), (dp * act).astype(BF16)


def norm_back(h, da):
    wide, scale = norm_scale(h)
    da = da.astype(F32)
    return (scale * da - wide * (scale * scale * scale * jnp.mean(da * wide, -1, keepdims=True))).astype(BF16)


def adamw(w, m, v, g):
    w = w.astype(F32)
    m = 0.9 * m + 0.1 * g
    v = 0.95 * v + 0.05 * g * g
    step = m * lax.rsqrt(v + 1e-8) + 0.1 * w
    return (w - 0.02 * step).astype(BF16), m, v


def solution(mesh):
    n = mesh.shape["dp"]

    pairs = [[2 * i, 2 * i + 1] for i in range(n // 2)]
    alike = [list(range(c, n, 2)) for c in range(2)]

    def body(x, dy, wg, wu, wd, mg, mu, md, vg, vu, vd):
        x, dy = x[0], dy[0]
        d, ff = wg.shape[1:]
        half = d // 2

        def summed(two, rows):
            mine = lax.psum_scatter(two, "dp", scatter_dimension=0, axis_index_groups=pairs)
            mine = mine.reshape(n // 2, rows, mine.shape[-1])
            return lax.psum_scatter(mine, "dp", scatter_dimension=0, axis_index_groups=alike)

        def down_sum(p, dy):
            two = [dot(p, dy[:, i * half : (i + 1) * half], ((0,), (0,))).astype(BF16) for i in range(2)]
            return summed(jnp.stack(two), 2 * ff // n)

        def gate_up_sum(a, dg, du):
            two = [dot(a, t, ((0,), (0,))).astype(BF16) for t in (dg, du)]
            return summed(jnp.stack(two), 2 * d // n)

        a0 = normed(x)
        gate0, up0 = dot(a0, wg[0], ((1,), (0,))), dot(a0, wu[0], ((1,), (0,)))
        p0 = (jax.nn.silu(gate0) * up0).astype(BF16)
        h1 = x + dot(p0, wd[0], ((1,), (0,))).astype(BF16)
        a1 = normed(h1)
        gate1, up1 = dot(a1, wg[1], ((1,), (0,))), dot(a1, wu[1], ((1,), (0,)))
        p1 = (jax.nn.silu(gate1) * up1).astype(BF16)
        sd1 = down_sum(p1, dy)
        dp1 = dot(dy, wd[1], ((1,), (1,))).astype(BF16)
        dg1, du1 = hidden_back(gate1, up1, dp1)
        sgu1 = gate_up_sum(a1, dg1, du1)
        da1 = dot(dg1, wg[1], ((1,), (1,))).astype(BF16) + dot(du1, wu[1], ((1,), (1,))).astype(BF16)
        dh1 = dy + norm_back(h1, da1)
        dp0 = dot(dh1, wd[0], ((1,), (1,))).astype(BF16)
        dg0, du0 = hidden_back(gate0, up0, dp0)
        sd0 = down_sum(p0, dh1)
        sgu0 = gate_up_sum(a0, dg0, du0)

        count = 3 * 2 * d * ff
        squares = sum(jnp.sum(g.astype(F32) ** 2) for g in (sd1, sgu1, sd0, sgu0))
        total = lax.psum(squares, "dp")
        factor = jnp.minimum(1.0, 0.5 * lax.rsqrt(total / count + CLIP_EPS))
        core = lax.axis_index("dp") % 2

        def own_rows(s):
            both = lax.all_gather(s, "dp", axis_index_groups=pairs)
            rows = s.shape[0] // 2
            return lax.dynamic_slice_in_dim(both, core * rows, rows, 1).astype(F32)

        gu = [own_rows(s) for s in (sgu0, sgu1)]
        down = [own_rows(s) for s in (sd0, sd1)]
        grads = [[t[0] for t in gu], [t[1] for t in gu], [jnp.concatenate([t[0], t[1]], -1) for t in down]]
        me = lax.axis_index("dp")
        ws, ms, vs = [], [], []
        for pair, w, m, v in zip(grads, (wg, wu, wd), (mg, mu, md), (vg, vu, vd), strict=True):
            rows = m.shape[1]
            own = lax.dynamic_slice_in_dim(w, me * rows, rows, 1)
            new = [adamw(own[i], m[i], v[i], pair[i] * factor) for i in range(2)]
            ws.append(jnp.stack([lax.all_gather(new[i][0], "dp", axis=0, tiled=True) for i in range(2)]))
            ms.append(jnp.stack([new[i][1] for i in range(2)]))
            vs.append(jnp.stack([new[i][2] for i in range(2)]))
        return (*ws, *ms, *vs)

    shard = P(None, "dp", None)
    return jax.shard_map(
        body,
        mesh=mesh,
        in_specs=(P(("rep", "dp")), P(("rep", "dp")), P(), P(), P(), *[shard] * 6),
        out_specs=(P("rep"), P("rep"), P("rep"), *[P("rep", "dp", None)] * 6),
        check_vma=False,
    )
```

time: 4200 us -> 1980 us (0.47)
  blocking collectives: 2420 us -> 78.2 us
  waiting for transfers between devices: 238 us -> 1280 us
  starting transfers between devices: 527 us -> 0.56 us
  local copies, waits for them, and re-layouts: 558 us -> 136 us
  other arithmetic: 35.1 us -> 123 us
    unnamed x6 -> x0, blocking collectives: 2360 us -> none
    unnamed x299 -> x44, local copies, waits for them, and re-layouts: 550 us -> 6.06 us
    unnamed x174 -> x2, starting transfers between devices: 527 us -> 0.08 us
    reduce_scatter x0 -> x6, waiting for transfers between devices: none -> 475 us  [the longest x2 456 us: summed(): lax.psum_scatter(mine, 'dp', scatter_dimension=0, axis_index_groups=alike)]
    unnamed x177 -> x16, waiting for transfers between devices: 10.4 us -> 467 us
    all_gather x0 -> x6, waiting for transfers between devices: none -> 339 us  [body(): lax.all_gather(new[i][0], 'dp', axis=0, tiled=True)]
    reshape x3 -> x0, waiting for transfers between devices: 227 us -> none  [step(): t.reshape(-1, *t.shape[2:])]
    another operation x0 -> x8, local copies, waits for them, and re-layouts: none -> 125 us  [the longest x6 108 us: body(): jnp.stack([lax.all_gather(new[i][0], 'dp', axis=0, tiled=True) for i in r...]
  transfers between devices with their start and end apart: 177 -> 14, of which waited for: 10 -> 11; matrix products, arithmetic and copies ran while one was open for 64% -> 17% of each run, Pallas kernels for 0% -> 0%
where the time goes in v1:
time: 1980 us; the launch traced here: 1970 us
  waiting for transfers between devices  1280 us (65%)
  matrix products  332 us (17%)
  local copies, waits for them, and re-layouts  136 us (7%)
  other arithmetic  123 us (6%)
  blocking collectives  78.2 us (4%)
    unnamed x16, waiting for transfers between devices  467 us
    reduce_scatter x2, waiting for transfers between devices, summed(): lax.psum_scatter(mine, 'dp', scatter_dimension=0, axis_index_groups=alike)  456 us
    all_gather x6, waiting for transfers between devices, body(): lax.all_gather(new[i][0], 'dp', axis=0, tiled=True)  339 us
    dot_general x17, matrix products, dot(): return lax.dot_general(a, b, (dims, ((), ())), preferred_element_type=F32)  332 us
    another operation x6, local copies, waits for them, and re-layouts, body(): jnp.stack([lax.all_gather(new[i][0], 'dp', axis=0, tiled=True) for i in r...  108 us
    psum x1, blocking collectives, body(): total = lax.psum(squares, 'dp')  64.5 us
    another operation x3, other arithmetic, body(): jnp.stack([lax.all_gather(new[i][0], 'dp', axis=0, tiled=True) for i in r...  58.2 us
  transfers between devices with their start and end apart: 14, of which 11 were waited for; matrix products, arithmetic and copies ran while one was open for 17% of the time, Pallas kernels for 0%

profile of v1, /device:TPU:1, one launch (start us, length us, event | category | flops | bytes accessed | tf_op | source)
XLA Modules:
  0.0 1968.5 jit_solution(14989066886184830858)
XLA Ops:
  9.8 20.2 %fusion.42 = bf16[1024,4224]{1,0:T(8,128)(2,1)} fusion(bf16[2,4224,1536]{2,1,0:T(8,128)(2,1)} %param.15, bf16[1,1024,1536]{2,1,0:T(8,128)(2,1)} %param.12), kind=kOutput, calls=%fused_computation.63 | convolution fusion | flops 13291880448 | bytes 24772608 | tf_op jit(solution)/shard_map/dot_general | solution.py:11
  30.1 20.0 %fusion.26 = f32[1024,4224]{1,0:T(8,128)} fusion(bf16[2,1536,4224]{2,1,0:T(8,128)(2,1)} %param.13, bf16[1,1024,1536]{2,1,0:T(8,128)(2,1)S(1)} %copy-done.1, f32[1024]{0:T(1024)S(1)} %add_rsqrt_fusion.1), kind=kOutput, calls=%fused_computation.45 | convolution fusion | flops 13292273664 | bytes 33427456 | tf_op jit(solution)/shard_map/dot_general | solution.py:11
  50.1 27.7 %multiply_convert_fusion.1 = (bf16[1024,4224]{1,0:T(8,128)(2,1)}, f32[1024,4224]{1,0:T(8,128)}) fusion(f32[1024,4224]{1,0:T(8,128)} %fusion.26, bf16[2,1536,4224]{2,1,0:T(8,128)(2,1)} %param.14, bf16[1,1024,1536]{2,1,0:T(8,128)(2,1)S(1)} %copy-done.1, f32[1024]{0:T(1024)S(1)} %add_rsqrt_fusion.1), kind=kOutput, calls=%fused_computation.21 | convolution fusion | flops 13318225920 | bytes 59379712 | tf_op jit(solution)/shard_map/dot_general | solution.py:11
  97.2 21.1 %fusion.12 = f32[1024,4224]{1,0:T(8,128)} fusion(bf16[2,1536,4224]{2,1,0:T(8,128)(2,1)} %param.13, bf16[1024,1536]{1,0:T(8,128)(2,1)S(1)} %get-tuple-element.81, f32[1024]{0:T(1024)S(1)} %add_rsqrt_fusion), kind=kOutput, calls=%fused_computation.31 | convolution fusion | flops 13292273664 | bytes 33427456 | tf_op jit(solution)/shard_map/dot_general | solution.py:11
  118.4 22.1 %fusion.61 = bf16[1024,1536]{1,0:T(8,128)(2,1)} fusion(bf16[2,1536,4224]{2,1,0:T(8,128)(2,1)} %param.14, bf16[1024,4224]{1,0:T(8,128)(2,1)} %fusion.42, f32[1024,4224]{1,0:T(8,128)} %fusion.12), kind=kOutput, calls=%fused_computation.84 | convolution fusion | flops 13319405568 | bytes 42074112 | tf_op jit(solution)/shard_map/dot_general | solution.py:11
  140.5 28.6 %fusion.1 = (bf16[1024,4224]{1,0:T(8,128)(2,1)}, bf16[1024,4224]{1,0:T(8,128)(2,1)}) fusion(bf16[1024,4224]{1,0:T(8,128)(2,1)} %fusion.42, f32[1024,4224]{1,0:T(8,128)} %fusion.12, bf16[2,1536,4224]{2,1,0:T(8,128)(2,1)} %param.14, bf16[1024,1536]{1,0:T(8,128)(2,1)S(1)} %get-tuple-element.81, f32[1024]{0:T(1024)S(1)} %add_rsqrt_fusion), kind=kOutput, calls=%fused_computation.14 | convolution fusion | flops 13348503552 | bytes 59379712 | tf_op jit(solution)/shard_map/dot_general | solution.py:11
  169.1 21.0 %fusion.57 = (f32[1024]{0:T(1024)S(1)}, bf16[1024,1536]{1,0:T(8,128)(2,1)S(1)}) fusion(bf16[1024,1536]{1,0:T(8,128)(2,1)} %copy-done.5, bf16[1024,1536]{1,0:T(8,128)(2,1)} %fusion.61, bf16[1024,4224]{1,0:T(8,128)(2,1)} %get-tuple-element.36, bf16[2,1536,4224]{2,1,0:T(8,128)(2,1)} %param.13), kind=kOutput, calls=%fused_computation.81 | convolution fusion | flops 13296991232 | bytes 31068160 | tf_op jit(solution)/shard_map/dot_general | solution.py:11
  263.8 22.7 %fusion.9 = bf16[1,1536,4224]{2,1,0:T(8,128)(2,1)} fusion(bf16[1024,4224]{1,0:T(8,128)(2,1)} %fusion.42, bf16[1024,1536]{1,0:T(8,128)(2,1)} %copy-done.5, f32[1024]{0:T(1024)S(1)} %add_rsqrt_fusion, f32[1024,4224]{1,0:T(8,128)} %fusion.12), kind=kOutput, calls=%fused_computation.26 | convolution fusion | flops 13329039360 | bytes 42078208 | tf_op jit(solution)/shard_map/dot_general | solution.py:11
  320.6 24.1 %fusion.7 = bf16[1,1536,4224]{2,1,0:T(8,128)(2,1)} fusion(bf16[1024,4224]{1,0:T(8,128)(2,1)S(1)} %fusion.39, bf16[1,1024,1536]{2,1,0:T(8,128)(2,1)S(1)} %copy-done.2, f32[1024]{0:T(1024)S(1)} %copy-done.14, f32[1024,4224]{1,0:T(8,128)} %fusion.26), kind=kOutput, calls=%fused_computation.24 | convolution fusion | flops 13329039360 | bytes 42078208 | tf_op jit(solution)/shard_map/dot_general | solution.py:11
  344.8 25.6 %fusion.6 = bf16[1,1536,4224]{2,1,0:T(8,128)(2,1)} fusion(f32[1024,4224]{1,0:T(8,128)} %get-tuple-element.79, bf16[1024,4224]{1,0:T(8,128)(2,1)} %copy-done.15, f32[1024,4224]{1,0:T(8,128)} %fusion.26, bf16[1,1024,1536]{2,1,0:T(8,128)(2,1)S(1)} %copy-done.2, f32[1024]{0:T(1024)S(1)} %copy-done.14), kind=kOutput, calls=%fused_computation.23 | convolution fusion | flops 13346340864 | bytes 59379712 | tf_op jit(solution)/shard_map/dot_general | solution.py:11
  370.4 21.1 %pad_maximum_fusion = bf16[2,1536,4224]{2,1,0:T(8,128)(2,1)} fusion(bf16[1,1536,4224]{2,1,0:T(8,128)(2,1)} %fusion.7, bf16[1,1536,4224]{2,1,0:T(8,128)(2,1)} %fusion.6), kind=kLoop, calls=%fused_computation | loop fusion | flops 12976128 | bytes 51904512 | tf_op jit(solution)/shard_map/stack | solution.py:67
  428.8 230.4 %reduce-scatter.23.cloned.1.call-done = bf16[1,66,768]{2,1,0:T(8,128)(2,1)} async-done(((bf16[64,66,768]{2,1,0:T(8,128)(2,1)}), bf16[1,66,768]{2,1,0:T(8,128)(2,1)}) %reduce-scatter.23.cloned.1.call-update) | async-done | bytes 101392 | tf_op jit(solution)/shard_map/reduce_scatter | solution.py:59
  663.5 226.0 %reduce-scatter.17.cloned.1.call-done = bf16[1,66,768]{2,1,0:T(8,128)(2,1)} async-done(((bf16[64,66,768]{2,1,0:T(8,128)(2,1)}), bf16[1,66,768]{2,1,0:T(8,128)(2,1)}) %reduce-scatter.17.cloned.1.call-update) | async-done | bytes 101392 | tf_op jit(solution)/shard_map/reduce_scatter | solution.py:59
  897.6 229.4 %reduce-scatter.27.cloned.1.call-done = bf16[1,24,4224]{2,1,0:T(8,128)(2,1)} async-done(((bf16[64,24,4224]{2,1,0:T(8,128)(2,1)}), bf16[1,24,4224]{2,1,0:T(8,128)(2,1)}) %reduce-scatter.27.cloned.1.call-update) | async-done | bytes 202768
  1130.6 234.2 %reduce-scatter.25.cloned.1.call-done = bf16[1,24,4224]{2,1,0:T(8,128)(2,1)} async-done(((bf16[64,24,4224]{2,1,0:T(8,128)(2,1)}), bf16[1,24,4224]{2,1,0:T(8,128)(2,1)}) %reduce-scatter.25.cloned.1.call-update) | async-done | bytes 202768
  1367.8 64.5 %psum.7 = f32[]{:T(128)} all-reduce(f32[]{:T(128)S(6)} %add.215), channel_id=1, replica_groups=mesh['rep'=1,'dp'=128] {'dp'}, use_global_device_ids=true, to_apply=%region_15.16 | all-reduce | flops 1 | bytes 8 | tf_op jit(solution)/shard_map/psum | solution.py:89
  1456.3 53.4 %all-gather.21.cloned.1.call-done = bf16[128,33,1536]{2,1,0:T(8,128)(2,1)} async-done(((bf16[1,33,1536]{2,1,0:T(8,128)(2,1)}), bf16[128,33,1536]{2,1,0:T(8,128)(2,1)}) %all-gather.21.cloned.1.call-update) | async-done | bytes 12976144 | tf_op jit(solution)/shard_map/all_gather | solution.py:107
  1527.0 62.8 %all-gather.23.cloned.1.call-done = bf16[128,33,1536]{2,1,0:T(8,128)(2,1)} async-done(((bf16[1,33,1536]{2,1,0:T(8,128)(2,1)}), bf16[128,33,1536]{2,1,0:T(8,128)(2,1)}) %all-gather.23.cloned.1.call-update) | async-done | bytes 12976144 | tf_op jit(solution)/shard_map/all_gather | solution.py:107
  1607.1 66.2 %all-gather.13.cloned.1.call-done = bf16[128,12,4224]{2,1,0:T(8,128)(2,1)} async-done(((bf16[1,12,4224]{2,1,0:T(8,128)(2,1)}), bf16[128,12,4224]{2,1,0:T(8,128)(2,1)}) %all-gather.13.cloned.1.call-update) | async-done | bytes 12976144 | tf_op jit(solution)/shard_map/all_gather | solution.py:107
  1691.6 64.9 %all-gather.15.cloned.1.call-done = bf16[128,12,4224]{2,1,0:T(8,128)(2,1)} async-done(((bf16[1,12,4224]{2,1,0:T(8,128)(2,1)}), bf16[128,12,4224]{2,1,0:T(8,128)(2,1)}) %all-gather.15.cloned.1.call-update) | async-done | bytes 12976144 | tf_op jit(solution)/shard_map/all_gather | solution.py:107
  1775.0 64.4 %all-gather.19.cloned.1.call-done = bf16[128,12,4224]{2,1,0:T(8,128)(2,1)} async-done(((bf16[1,12,4224]{2,1,0:T(8,128)(2,1)}), bf16[128,12,4224]{2,1,0:T(8,128)(2,1)}) %all-gather.19.cloned.1.call-update) | async-done | bytes 12976144 | tf_op jit(solution)/shard_map/all_gather | solution.py:107
  1857.9 21.9 %pad_maximum_fusion.4 = bf16[2,4224,1536]{2,1,0:T(8,128)(2,1)} fusion(bf16[1,4224,1536]{2,1,0:T(8,128)(2,1)} %stack.112, bf16[1,4224,1536]{2,1,0:T(8,128)(2,1)} %stack.111), kind=kLoop, calls=%fused_computation.4 | loop fusion | flops 12976128 | bytes 51904512 | tf_op jit(solution)/shard_map/stack | solution.py:107
  1895.0 27.0 %all-gather.17.cloned.1.call-done = bf16[128,12,4224]{2,1,0:T(8,128)(2,1)} async-done(((bf16[1,12,4224]{2,1,0:T(8,128)(2,1)}), bf16[128,12,4224]{2,1,0:T(8,128)(2,1)}) %all-gather.17.cloned.1.call-update) | async-done | bytes 12976144 | tf_op jit(solution)/shard_map/all_gather | solution.py:107
  1940.4 21.1 %pad_maximum_fusion.3 = bf16[2,1536,4224]{2,1,0:T(8,128)(2,1)} fusion(bf16[1,1536,4224]{2,1,0:T(8,128)(2,1)} %stack.109, bf16[1,1536,4224]{2,1,0:T(8,128)(2,1)} %stack.108), kind=kLoop, calls=%fused_computation.3 | loop fusion | flops 12976128 | bytes 51904512 | tf_op jit(solution)/shard_map/stack | solution.py:107
  (130 shorter events, 329.9 us)
Async XLA Ops:
  7.2 384.4 %reduce-scatter.21.cloned.1.call-start = ((), (), s32[]{:S(2)}) async-start(), calls=%async_computation.12 | async-start | bytes 19464192 | tf_op jit(solution)/shard_map/reduce_scatter | solution.py:57
  9.8 40.3 %copy-start.13 = (f32[1024]{0:T(1024)}, f32[1024]{0:T(1024)S(1)}, u32[]{:S(2)}) copy-start(f32[1024]{0:T(1024)S(1)} %add_rsqrt_fusion.1) | copy-start | bytes 12292
  97.2 21.2 %copy-start.11 = (f32[1024]{0:T(1024)}, f32[1024]{0:T(1024)S(1)}, u32[]{:S(2)}) copy-start(f32[1024]{0:T(1024)S(1)} %get-tuple-element.80) | copy-start | bytes 12292
  97.2 43.3 %copy-start.5 = (bf16[1024,1536]{1,0:T(8,128)(2,1)}, bf16[1024,1536]{1,0:T(8,128)(2,1)S(1)}, u32[]{:S(2)}) copy-start(bf16[1024,1536]{1,0:T(8,128)(2,1)S(1)} %get-tuple-element.81) | copy-start | bytes 9437188
  169.1 21.0 %copy-start.12 = (f32[1024]{0:T(1024)S(1)}, f32[1024]{0:T(1024)}, u32[]{:S(2)}) copy-start(f32[1024]{0:T(1024)} %copy-done.11) | copy-start | bytes 12292
  169.1 21.0 %copy-start.3 = (bf16[1,1024,1536]{2,1,0:T(8,128)(2,1)S(1)}, bf16[1,1024,1536]{2,1,0:T(8,128)(2,1)}, u32[]{:S(2)}) copy-start(bf16[1,1024,1536]{2,1,0:T(8,128)(2,1)} %param.12) | copy-start | bytes 9437188
  169.1 21.0 %copy-start.6 = (bf16[1024,1536]{1,0:T(8,128)(2,1)S(1)}, bf16[1024,1536]{1,0:T(8,128)(2,1)}, u32[]{:S(2)}) copy-start(bf16[1024,1536]{1,0:T(8,128)(2,1)} %copy-done.5) | copy-start | bytes 9437188
  217.2 183.0 %reduce-scatter.15.cloned.1.call-start = ((), (), s32[]{:S(2)}) async-start(), calls=%async_computation.9 | async-start | bytes 19464192 | tf_op jit(solution)/shard_map/reduce_scatter | solution.py:57
  244.6 164.3 %reduce-scatter.19.cloned.1.call-start = ((), (), s32[]{:S(2)}) async-start(), calls=%async_computation.11 | async-start | bytes 38928384 | tf_op jit(solution)/shard_map/reduce_scatter | solution.py:57
  301.8 126.2 %reduce-scatter.13.cloned.1.call-start = ((), (), s32[]{:S(2)}) async-start(), calls=%async_computation.8 | async-start | bytes 38928384 | tf_op jit(solution)/shard_map/reduce_scatter | solution.py:57
  320.6 24.1 %copy-start.15 = (bf16[1024,4224]{1,0:T(8,128)(2,1)}, bf16[1024,4224]{1,0:T(8,128)(2,1)S(1)}, u32[]{:S(2)}) copy-start(bf16[1024,4224]{1,0:T(8,128)(2,1)S(1)} %fusion.39) | copy-start | bytes 25952260
  391.5 267.7 %reduce-scatter.23.cloned.1.call-start = ((), (), s32[]{:S(2)}) async-start(), calls=%async_computation.13 | async-start | bytes 7188480 | tf_op jit(solution)/shard_map/reduce_scatter | solution.py:59
  400.2 489.3 %reduce-scatter.17.cloned.1.call-start = ((), (), s32[]{:S(2)}) async-start(), calls=%async_computation.10 | async-start | bytes 7188480 | tf_op jit(solution)/shard_map/reduce_scatter | solution.py:59
  408.8 718.2 %reduce-scatter.27.cloned.1.call-start = ((), (), s32[]{:S(2)}) async-start(), calls=%async_computation.21 | async-start | bytes 13178880
  409.6 1026.1 %copy-start.9 = (f32[2,12,4224]{2,0,1:T(2,128)S(1)}, f32[2,12,4224]{2,0,1:T(2,128)}, u32[]{:S(2)}) copy-start(f32[2,12,4224]{2,0,1:T(2,128)} %param.16) | copy-start | bytes 1216516
  409.6 1026.1 %copy-start.10 = (f32[2,12,4224]{2,0,1:T(2,128)S(1)}, f32[2,12,4224]{2,0,1:T(2,128)}, u32[]{:S(2)}) copy-start(f32[2,12,4224]{2,0,1:T(2,128)} %param.19) | copy-start | bytes 1216516
  409.6 955.2 %reduce-scatter.25.cloned.1.call-start = ((), (), s32[]{:S(2)}) async-start(), calls=%async_computation.20 | async-start | bytes 13178880
  428.1 1081.7 %all-gather.21.cloned.1.call-start = ((), (), s32[]{:S(2)}) async-start(), calls=%async_computation.18 | async-start | bytes 15851520 | tf_op jit(solution)/shard_map/all_gather | solution.py:107
  1435.0 154.8 %all-gather.23.cloned.1.call-start = ((), (), s32[]{:S(2)}) async-start(), calls=%async_computation.19 | async-start | bytes 15851520 | tf_op jit(solution)/shard_map/all_gather | solution.py:107
  1435.6 237.6 %all-gather.13.cloned.1.call-start = ((), (), s32[]{:S(2)}) async-start(), calls=%async_computation.14 | async-start | bytes 17436672 | tf_op jit(solution)/shard_map/all_gather | solution.py:107
  1446.5 310.1 %all-gather.15.cloned.1.call-start = ((), (), s32[]{:S(2)}) async-start(), calls=%async_computation.15 | async-start | bytes 17436672 | tf_op jit(solution)/shard_map/all_gather | solution.py:107
  1447.1 392.3 %all-gather.19.cloned.1.call-start = ((), (), s32[]{:S(2)}) async-start(), calls=%async_computation.17 | async-start | bytes 17436672 | tf_op jit(solution)/shard_map/all_gather | solution.py:107
  1447.8 474.3 %all-gather.17.cloned.1.call-start = ((), (), s32[]{:S(2)}) async-start(), calls=%async_computation.16 | async-start | bytes 17436672 | tf_op jit(solution)/shard_map/all_gather | solution.py:107
  1857.9 21.9 %copy-start = (bf16[1,1536,4224]{2,1,0:T(8,128)(2,1)S(1)}, bf16[1,1536,4224]{2,1,0:T(8,128)(2,1)}, u32[]{:S(2)}) copy-start(bf16[1,1536,4224]{2,1,0:T(8,128)(2,1)} %stack.106) | copy-start | bytes 38928388
  (9 other events, 147.2 us)
Sparse Core Ops, SparseCore 0:
  217.3 25.1 reduce-scatter.20
  244.9 24.9 reduce-scatter.14
  301.9 36.3 reduce-scatter.18
  391.6 36.3 reduce-scatter.12
  432.4 226.7 reduce-scatter.22
  664.1 225.2 reduce-scatter.16
  894.2 232.7 reduce-scatter.26
  1131.8 232.9 reduce-scatter.24
  1435.2 74.5 all-gather.20
  1512.6 77.1 all-gather.22
  1593.4 79.7 all-gather.12
  1676.7 79.7 all-gather.14
  1759.5 79.7 all-gather.18
  1842.2 79.7 all-gather.16

commit v2 on v0

v2 whole, which is shorter than its diff:
```python
import functools

import jax
import jax.numpy as jnp
from jax import lax
from jax.experimental import pallas as pl
from jax.experimental.layout import Layout, with_layout_constraint
from jax.experimental.pallas import tpu as pltpu
from jax.sharding import PartitionSpec as P

F32, BF16 = jnp.float32, jnp.bfloat16
CLIP_EPS = 1e-30
LANES = 128
SIDE = 4
ORDERS = ((0, 1, 2), (1, 2, 0), (2, 0, 1))
VMEM_LIMIT = 63 * 1024 * 1024


class Place:
    def __init__(self):
        me = lax.axis_index("dp")
        self.core = lax.rem(me, 2)
        chip = lax.div(me, 2)
        self.at = (lax.div(chip, SIDE * SIDE), lax.rem(lax.div(chip, SIDE), SIDE), lax.rem(chip, SIDE))

    def device(self, axis=None, off=0, core=None):
        at = list(self.at)
        if axis is not None:
            at[axis] = lax.rem(at[axis] + off, SIDE)
        core = self.core if core is None else core
        return {"dp": ((at[0] * SIDE + at[1]) * SIDE + at[2]) * 2 + core}

    def partner(self):
        return self.device(core=1 - self.core)

    def onward(self, way):
        return 1 + 2 * lax.rem(way + self.core, 2)

    def block(self, axis, way, hops):
        return lax.rem(self.at[axis] + hops * (SIDE - self.onward(way)), SIDE)


def signal_all(devices):
    barrier = pltpu.get_barrier_semaphore()
    for d in devices:
        pl.semaphore_signal(barrier, inc=1, device_id=d, device_id_type=pl.DeviceIdType.MESH)
    pl.semaphore_wait(barrier, len(devices))


def near(place):
    return [place.partner()] + [place.device(axis, off) for axis in range(3) for off in (1, SIDE - 1)]


def put(src, dst, send, recv, device):
    return pltpu.make_async_remote_copy(
        src_ref=src, dst_ref=dst, send_sem=send, recv_sem=recv, device_id=device, device_id_type=pl.DeviceIdType.MESH
    )


def ways_of(cols):
    tiles = cols // LANES
    first = (tiles + 1) // 2 * LANES
    return ((0, first), (first, cols - first))


def index(order, values):
    out = [None] * 3
    for axis, value in zip(order, values, strict=True):
        out[axis] = value
    return tuple(out)


ALL = slice(None)


class Rings:
    def __init__(self, place, rows, cols, slots, sems):
        self.place, self.rows, self.slots, self.sems = place, rows // 3, slots, sems
        self.ways = ways_of(cols)

    def part(self, t, way):
        start, width = self.ways[way]
        return pl.ds(t * self.rows, self.rows), pl.ds(start, width)

    @staticmethod
    def pairs():
        return [(t, way) for t in range(3) for way in range(2)]

    def send(self, axis, way, src, landing, key, sems):
        src = landing if src is None else src
        return put(src, landing, sems[0].at[key], sems[1].at[key], self.place.device(axis, self.place.onward(way)))


class First(Rings):
    @staticmethod
    def scratch(rows, cols):
        third, dma = rows // 3, pltpu.SemaphoreType.DMA
        slots = [pltpu.VMEM((3, 3, SIDE, SIDE, third, width), BF16) for _, width in ways_of(cols)]
        return [pltpu.VMEM((SIDE, SIDE, SIDE, rows, cols), BF16), *slots, dma((3, 2, 3, SIDE)), dma((3, 2, 3, SIDE))]

    @classmethod
    def of(cls, place, rows, cols, refs):
        one = cls(place, rows, cols, refs[1:3], refs[3:5])
        one.held = refs[0]
        return one

    def block(self, t, way, hops, k, c=ALL):
        order = ORDERS[t]
        return self.held.at[(*index(order, (self.place.block(order[0], way, hops), k, c)), *self.part(t, way))]

    def message(self, t, way, n, k, arriving=False):
        src = None
        if not arriving:
            src = self.block(t, way, 1, k) if isinstance(n, int) and n == 0 else self.slots[way].at[t, n - 1, k]
        return self.send(ORDERS[t][0], way, src, self.slots[way].at[t, n, k], (t, way, n, k), self.sems)

    def start(self, k):
        for t, way in self.pairs():
            self.message(t, way, 0, k).start()

    def step(self, n, k):
        for t, way in self.pairs():
            self.message(t, way, n - 1, k, arriving=True).wait_recv()
            slots = self.slots[way]
            for c in range(SIDE):
                own = self.block(t, way, n + 1, k, c)
                slots[t, n - 1, k, c] = (slots[t, n - 1, k, c].astype(F32) + own[...].astype(F32)).astype(BF16)
            pl.when(n < 3)(lambda t=t, way=way: self.message(t, way, n, k).start())

    def tick(self, i):
        pl.when(i < SIDE)(lambda: self.start(i))
        pl.when(i >= SIDE)(lambda: self.step(lax.div(i, SIDE), lax.rem(i, SIDE)))

    def results(self):
        return [slots.at[:, 2] for slots in self.slots]

    def drain(self):
        def sent(k, _):
            for t, way in self.pairs():
                self.message(t, way, 0, k).wait_send()
                lax.fori_loop(1, 3, lambda n, _: (self.message(t, way, n, k).wait_send(), 0)[1], 0)
            return 0

        lax.fori_loop(0, SIDE, sent, 0)


class Rest(Rings):
    @staticmethod
    def scratch(rows, cols):
        third, dma = rows // 3, pltpu.SemaphoreType.DMA
        shapes = [pltpu.VMEM((*lead, third, width), BF16) for lead in ((3, 3, SIDE), (3, 3)) for _, width in ways_of(cols)]
        return shapes + [dma((3, 2, 3))] * 4

    @classmethod
    def of(cls, place, rows, cols, before, refs):
        one = cls(place, rows, cols, refs[:4], refs[4:8])
        one.before = before
        return one

    def message(self, phase, t, way, n, arriving=False):
        slots = self.slots[2 * phase - 2 + way]
        axis = ORDERS[t][phase]
        if arriving:
            src = None
        elif isinstance(n, int) and n == 0:
            v = self.place.block(axis, way, 1)
            src = self.before[way].at[t, v] if phase == 1 else self.slots[way].at[t, 2, v]
        else:
            src = slots.at[t, n - 1]
        return self.send(axis, way, src, slots.at[t, n], (t, way, n), self.sems[2 * phase - 2 : 2 * phase])

    def start(self, phase):
        for t, way in self.pairs():
            self.message(phase, t, way, 0).start()

    def step1(self, n):
        for t, way in self.pairs():
            self.message(1, t, way, n - 1, arriving=True).wait_recv()
            v = self.place.block(ORDERS[t][1], way, n + 1)
            before, slots = self.before[way], self.slots[way]
            for c in range(SIDE):
                slots[t, n - 1, c] = (slots[t, n - 1, c].astype(F32) + before[t, v, c].astype(F32)).astype(BF16)
            pl.when(n < 3)(lambda t=t, way=way: self.message(1, t, way, n).start())

    def step2(self, n):
        for t, way in self.pairs():
            self.message(2, t, way, n - 1, arriving=True).wait_recv()
            v = self.place.block(ORDERS[t][2], way, n + 1)
            before, slots = self.slots[way], self.slots[2 + way]
            slots[t, n - 1] = (slots[t, n - 1].astype(F32) + before[t, 2, v].astype(F32)).astype(BF16)
            pl.when(n < 3)(lambda t=t, way=way: self.message(2, t, way, n).start())

    def tick(self, i):
        pl.when(i == 0)(lambda: self.start(1))
        pl.when((i >= 1) & (i <= 3))(lambda: self.step1(i))
        pl.when(i == 3)(lambda: self.start(2))
        pl.when((i >= 4) & (i <= 6))(lambda: self.step2(i - 3))

    def result(self, out):
        for t, way in self.pairs():
            out[self.part(t, way)] = self.slots[2 + way][t, 2]

    def drain(self):
        for t, way in self.pairs():
            for phase in (1, 2):
                for n in range(3):
                    self.message(phase, t, way, n).wait_send()


def loads_down(source, first, sems):
    return [pltpu.make_async_copy(source.at[:, :, pl.ds(64 * z, 72)], first.held.at[:, :, z], sems.at[z]) for z in range(SIDE)]


def spread(j, steps, count, tick):
    low, high = lax.div(count * j, steps), lax.div(count * (j + 1), steps)
    lax.fori_loop(low, high, lambda i, _: (tick(i), 0)[1], 0)


def copies(sources, targets, sems):
    return [pltpu.make_async_copy(s, t, sems.at[i]) for i, (s, t) in enumerate(zip(sources, targets, strict=True))]


def begin(all_copies):
    for copy in all_copies:
        copy.start()


def end(all_copies):
    for copy in all_copies:
        copy.wait()


def half_sums(rows, cols):
    return [(3, SIDE, SIDE, rows // 3, width) for _, width in ways_of(cols)]


PREV = 6
DOWN_ROWS = 33


class Gather:
    def __init__(self, place, bufs, sems, outs, copy_sems):
        self.place, self.bufs, self.sems, self.outs, self.copy_sems = place, bufs, sems, outs, copy_sems

    @staticmethod
    def scratch(gate_cols, down_cols):
        bufs = [pltpu.VMEM((2, SIDE, SIDE, SIDE, 24, gate_cols), BF16), pltpu.VMEM((2, SIDE, SIDE, SIDE, 72, down_cols), BF16)]
        return bufs + [pltpu.SemaphoreType.DMA((2, 3, 2, 3, 3))] * 4 + [pltpu.SemaphoreType.DMA((2,))] * 3

    def part(self, kind, t, way):
        rows, cols = self.bufs[kind].shape[-2:]
        start, width = ways_of(cols)[way]
        return pl.ds(t * (rows // 3), rows // 3), pl.ds(start, width)

    def message(self, kind, l, t, way, phase, n, hops):
        order, place = ORDERS[t], self.place
        v = place.block(order[phase], way, hops)
        values = [ALL] * phase + [v] + [place.at[axis] for axis in order[phase + 1 :]]
        ref = self.bufs[kind].at[(l, *index(order, values), *self.part(kind, t, way))]
        key = (l, t, way, phase, n)
        axis = order[phase]
        return put(ref, ref, self.sems[2 * kind].at[key], self.sems[2 * kind + 1].at[key], place.device(axis, place.onward(way)))

    def copies(self, kind, l, t, way, v):
        order = ORDERS[t]
        rows, cols = self.part(kind, t, way)
        if kind == 0:
            at = (l, *index(order, (ALL, ALL, v)), rows, cols)
            return [(lambda out, at=at: (self.bufs[0].at[at], out.at[at]))]
        half = self.bufs[1].shape[-1]
        start, width = ways_of(half)[way]
        columns = pl.ds(pl.multiple_of(self.place.core * half + start, LANES), width)

        def pair(out, z, count):
            x, y, _ = index(order, (ALL, ALL, v))
            src = self.bufs[1].at[l, x, y, z, pl.ds(24 * t, count), cols]
            return src, out.at[l, x, y, pl.ds(64 * z + 24 * t, count), columns]

        if order[2] == 2:
            return [lambda out: pair(out, v, 24)]
        return [lambda out, z=z: pair(out, z, 16 if t == 2 and z < SIDE - 1 else 24) for z in range(SIDE)]

    def copy_out(self, kind, l, t, way, v):
        local, send, recv = self.copy_sems

        def both(out):
            for pair in self.copies(kind, l, t, way, v):
                src, dst = pair(out)
                pltpu.make_async_copy(src, dst, local.at[kind]).start()
                put(src, dst, send.at[kind], recv.at[kind], self.place.partner()).start()

        if kind:
            both(self.outs[2])
        else:
            for core in range(2):
                pl.when(self.place.core == core)(lambda core=core: both(self.outs[core]))

    def parts(self):
        return [(kind, t, way) for kind in range(2) for t in range(3) for way in range(2)]

    def own(self, l):
        for kind, t, way in self.parts():
            self.message(kind, l, t, way, 0, 0, 0).start()

    def phase(self, phase):
        def step(i, _):
            n, l = 1 + lax.div(i, 2), lax.rem(i, 2)
            for kind, t, way in self.parts():
                self.message(kind, l, t, way, phase, n - 1, n).wait_recv()
                pl.when(n < 3)(lambda kind=kind, t=t, way=way: self.message(kind, l, t, way, phase, n, n).start())
                if phase < 2:

                    @pl.when(n == 3)
                    def _(kind=kind, t=t, way=way):
                        self.message(kind, l, t, way, phase + 1, 0, 0).start()
                        if phase == 1:
                            self.copy_out(kind, l, t, way, self.place.at[ORDERS[t][2]])

                else:
                    self.copy_out(kind, l, t, way, self.place.block(ORDERS[t][2], way, n))
            return 0

        lax.fori_loop(0, 6, step, 0)

    def drain(self):
        local, send, recv = self.copy_sems
        half = self.bufs[1].shape[-1]
        columns = self.outs[2].at[:, :, :, :, pl.ds(0, half)]
        for kind, whole in ((0, self.outs[0]), (1, columns)):
            pltpu.make_async_copy(whole, whole, local.at[kind]).wait()
            copy = put(whole, whole, send.at[kind], recv.at[kind], self.place.partner())
            copy.wait_send()
            copy.wait_recv()

        def sent(i, _):
            l, n = lax.div(i, 3), lax.rem(i, 3)
            for phase in range(3):
                for kind, t, way in self.parts():
                    self.message(kind, l, t, way, phase, n, n).wait_send()
            return 0

        lax.fori_loop(0, 6, sent, 0)


def finish_kernel(count, *refs):
    sums_gu, sums_d, m_in, v_in, w_in = refs[0:2], refs[2:4], refs[4:7], refs[7:10], refs[10:13]
    w_out, m_out, v_out = refs[13:16], refs[16:19], refs[19:22]
    moments_gu, moments_d, old_gu, old_d, other_d, tiles = refs[22:28]
    load_sem, early_send, early_recv, norm_send, norm_recv, late_local, late_send, late_recv = refs[28:36]
    gather_refs = refs[36:]
    place = Place()
    x, y, z = place.at
    core = place.core
    gather = Gather(place, gather_refs[:2], gather_refs[2:6], w_out, gather_refs[6:9])
    partner = place.partner()
    gate_tiles, down_tiles = sums_gu[0].shape[1] // LANES, sums_d[0].shape[1] // LANES
    gate_stride, down_stride = 2 * gate_tiles, 4 * down_tiles
    gate_size, down_size = 12 * gate_stride, DOWN_ROWS * down_stride

    def blank(i, _):
        for which in range(2):
            moments_d[which, pl.ds(pl.multiple_of(8 * i, 8), 8), :] = jnp.zeros((8, LANES), F32)
        return 0

    lax.fori_loop(0, moments_d.shape[1] // 8, blank, 0)
    following = [place.device(2, 1, core=c) for c in range(2)]
    others = [place.device(axis, 2) for axis in range(3)] + [place.device(2, off, core=1 - core) for off in (1, SIDE - 1)]
    signal_all(near(place) + others)

    def gate_rows(i, which):
        return moments_gu.at[i, pl.ds(pl.multiple_of(which * gate_size, 8), gate_size)]

    def down_rows(i, first, rows):
        return moments_d.at[i, pl.ds(pl.multiple_of(first * down_stride, 8), rows * down_stride)]

    def columns(ref):
        half = down_tiles * LANES
        return ref.at[:, x, y, pl.ds(pl.multiple_of(64 * z, 8), 72), pl.ds(pl.multiple_of(core * half, LANES), half)]

    own_rows = PREV + 2 * z + DOWN_ROWS * core
    loads, sends = [], []
    for i, moment in enumerate((m_in, v_in)):
        for c in range(2):

            @pl.when(core == c)
            def _(i=i, moment=moment, c=c):
                pltpu.make_async_copy(moment[c], gate_rows(i, core), load_sem.at[i]).start()
                put(moment[1 - c], gate_rows(i, core), early_send.at[i], early_recv.at[i], partner).start()

        loads.append(pltpu.make_async_copy(moment[0], gate_rows(i, core), load_sem.at[i]))
        sends.append(put(moment[0], gate_rows(i, core), early_send.at[i], early_recv.at[i], partner))
        loads.append(pltpu.make_async_copy(moment[2], down_rows(i, own_rows, DOWN_ROWS), load_sem.at[2 + i]))
        loads[-1].start()
        sends.append(put(moment[2], down_rows(i, own_rows, DOWN_ROWS), early_send.at[2 + i], early_recv.at[2 + i], partner))
        sends[-1].start()
        last = moment[2].at[pl.ds((DOWN_ROWS - PREV) * down_stride, PREV * down_stride)]
        landing = down_rows(i, 2 * lax.rem(z + 1, SIDE), PREV)

        @pl.when(core == 1)
        def _(i=i, last=last, landing=landing):
            for c in range(2):
                put(last, landing, early_send.at[4 + 2 * i + c], early_recv.at[4 + i], following[c]).start()

    for l in range(2):
        sends.append(put(sums_d[l], other_d.at[l], early_send.at[8 + l], early_recv.at[6 + l], partner))
        sends[-1].start()
    for c in range(2):

        @pl.when(core == c)
        def _(c=c):
            pltpu.make_async_copy(w_in[c].at[:, x, y, z], old_gu, load_sem.at[4]).start()

    loads.append(pltpu.make_async_copy(w_in[0].at[:, x, y, z], old_gu, load_sem.at[4]))
    loads.append(pltpu.make_async_copy(columns(w_in[2]), old_d, load_sem.at[5]))
    loads[-1].start()

    squares = jnp.zeros((8, LANES), F32)
    for l in range(2):

        def of_gate_up(j, total, l=l):
            for t in range(3):
                g = sums_gu[l][pl.ds(8 * t, 8), pl.ds(pl.multiple_of(j * LANES, LANES), LANES)].astype(F32)
                total += g * g
            return total

        squares = lax.fori_loop(0, gate_tiles, of_gate_up, squares)

        def of_down(i, total, l=l):
            row = 8 * i + lax.broadcasted_iota(jnp.int32, (8, LANES), 0)
            mine = (row >= 2 * z) & (row < 2 * z + 2 * DOWN_ROWS)
            for j in range(down_tiles):
                g = sums_d[l][pl.ds(pl.multiple_of(8 * i, 8), 8), pl.ds(j * LANES, LANES)].astype(F32)
                total += jnp.where(mine, g * g, 0.0)
            return total

        squares = lax.fori_loop(0, 9, of_down, squares)
    for stage, (coordinate, size) in enumerate(((core, 2), (x, SIDE), (y, SIDE), (z, SIDE))):
        tiles[stage, coordinate] = squares
        exchanges = []
        for off in range(1, size):
            target = partner if stage == 0 else place.device(stage - 1, off)
            key = 3 * stage + off - 1
            here = tiles.at[stage, coordinate]
            exchanges.append(put(here, here, norm_send.at[key], norm_recv.at[key], target))
            exchanges[-1].start()
        for exchange in exchanges:
            exchange.wait_recv()
        for exchange in exchanges:
            exchange.wait_send()
        squares = tiles[stage, 0]
        for other in range(1, size):
            squares += tiles[stage, other]
    total = jnp.sum(jnp.sum(squares, 0, keepdims=True), 1, keepdims=True)
    factor = jnp.minimum(1.0, 0.5 * lax.rsqrt(total / count + CLIP_EPS))

    for copy in loads:
        copy.wait()
    for copy in sends:
        copy.wait_recv()
    for i in range(2):
        put(down_rows(i, 0, PREV), down_rows(i, 0, PREV), early_send.at[0], early_recv.at[4 + i], partner).wait_recv()

    def moments(ref, start, stride, g):
        rows = pl.ds(start, 8, stride=stride)
        m = 0.9 * ref[0, rows, :] + 0.1 * g
        v = 0.95 * ref[1, rows, :] + 0.05 * g * g
        ref[0, rows, :] = m
        ref[1, rows, :] = v
        return m * lax.rsqrt(v + 1e-8)

    def weight(w, step):
        w = w.astype(F32)
        return (w - 0.02 * (step + 0.1 * w)).astype(BF16)

    for l in range(2):

        def gate_up(j, _, l=l):
            lanes = pl.ds(pl.multiple_of(j * LANES, LANES), LANES)
            for t in range(3):
                rows = pl.ds(8 * t, 8)
                g = sums_gu[l][rows, lanes].astype(F32) * factor
                step = moments(moments_gu, 8 * t * gate_stride + 2 * j + l, gate_stride, g)
                gather.bufs[0][l, x, y, z, rows, lanes] = weight(old_gu[l, rows, lanes], step)
            return 0

        lax.fori_loop(0, gate_tiles, gate_up, 0)

        def down(i, _, l=l):
            rows = pl.ds(pl.multiple_of(8 * i, 8), 8)
            for j in range(down_tiles):
                lanes = pl.ds(j * LANES, LANES)
                start = (PREV + 8 * i) * down_stride + 2 * j + l
                g = sums_d[l][rows, lanes].astype(F32) * factor
                step = moments(moments_d, start + 2 * down_tiles * core, down_stride, g)
                gather.bufs[1][l, x, y, z, rows, lanes] = weight(old_d[l, rows, lanes], step)
                g = other_d[l, rows, lanes].astype(F32) * factor
                moments(moments_d, start + 2 * down_tiles * (1 - core), down_stride, g)
            return 0

        lax.fori_loop(0, 9, down, 0)
        gather.own(l)

    late = []
    for i, out in enumerate((m_out, v_out)):
        for c in range(2):

            @pl.when(core == c)
            def _(i=i, out=out, c=c):
                pltpu.make_async_copy(gate_rows(i, core), out[c], late_local.at[i]).start()
                put(gate_rows(i, 1 - core), out[c], late_send.at[i], late_recv.at[i], partner).start()

        pltpu.make_async_copy(down_rows(i, own_rows, DOWN_ROWS), out[2], late_local.at[2 + i]).start()
    for phase in range(3):
        gather.phase(phase)
    for i, out in enumerate((m_out, v_out)):
        pltpu.make_async_copy(gate_rows(i, core), out[0], late_local.at[i]).wait()
        pltpu.make_async_copy(down_rows(i, own_rows, DOWN_ROWS), out[2], late_local.at[2 + i]).wait()
        copy = put(gate_rows(i, 1 - core), out[0], late_send.at[i], late_recv.at[i], partner)
        copy.wait_recv()
        copy.wait_send()
    for copy in sends:
        copy.wait_send()
    for i in range(2):
        for c in range(2):

            @pl.when(core == 1)
            def _(i=i, c=c):
                rows = down_rows(i, 0, PREV)
                put(rows, rows, early_send.at[4 + 2 * i + c], early_recv.at[4 + i], following[c]).wait_send()

    gather.drain()


def finish_call(count, collective_id, sums_gu, sums_d, m, v, w):
    gate_cols, down_half = sums_gu[0].shape[1], sums_d[0].shape[1]
    operands = [*sums_gu, *sums_d, *m, *v, *w]
    hbm, vmem = pl.BlockSpec(memory_space=pltpu.HBM), pl.BlockSpec(memory_space=pltpu.VMEM)
    dma = pltpu.SemaphoreType.DMA
    gate_stride, down_stride = gate_cols // 64, down_half // 32
    scratch = [
        pltpu.VMEM((2, 24 * gate_stride, LANES), F32),
        pltpu.VMEM((2, (PREV + 72) * down_stride, LANES), F32),
        pltpu.VMEM((2, 24, gate_cols), BF16),
        pltpu.VMEM((2, 72, down_half), BF16),
        pltpu.VMEM((2, 72, down_half), BF16),
        pltpu.VMEM((4, SIDE, 8, LANES), F32),
        dma((6,)), dma((10,)), dma((8,)), dma((12,)), dma((12,)), dma((4,)), dma((2,)), dma((2,)),
    ]
    return pl.pallas_call(
        functools.partial(finish_kernel, count),
        name="finish",
        out_shape=[jax.ShapeDtypeStruct(t.shape, t.dtype) for t in (*w, *m, *v)],
        in_specs=[vmem] * 4 + [hbm] * 9,
        out_specs=[hbm] * 9,
        scratch_shapes=scratch + Gather.scratch(gate_cols, down_half),
        compiler_params=pltpu.CompilerParams(collective_id=collective_id, has_side_effects=True, vmem_limit_bytes=VMEM_LIMIT),
        cost_estimate=pl.CostEstimate(flops=10**9, bytes_accessed=10**8, transcendentals=0),
    )(*operands)


TILE = 384
ROWS = 256
TIGHT = pl.Buffered(buffer_count=1)


def dot(a, b, dims):
    return lax.dot_general(a, b, (dims, ((), ())), preferred_element_type=F32)


NN, NT, TN = ((1,), (0,)), ((1,), (1,)), ((0,), (0,))


def norm_scale(wide):
    return lax.rsqrt(jnp.mean(wide * wide, -1, keepdims=True) + 1e-6)


def in_rows(total, step, body):
    def one(i, _):
        body(pl.ds(pl.multiple_of(i * step, step), step))
        return 0

    lax.fori_loop(0, total // step, one, 0)


def clear(acc):
    def rows(r):
        acc[r, :] = jnp.zeros((8, acc.shape[1]), F32)

    in_rows(acc.shape[0], 8, rows)


def spec(shape, index_map, tight=False):
    return pl.BlockSpec(shape, index_map, pipeline_mode=TIGHT) if tight else pl.BlockSpec(shape, index_map)


def whole(shape, tight=True):
    return spec(shape, lambda j: (0,) * len(shape), tight)


HBM = pl.BlockSpec(memory_space=pltpu.HBM)


def params(collective_id=None, semantics=("arbitrary",)):
    more = {} if collective_id is None else {"collective_id": collective_id, "has_side_effects": True}
    return pltpu.CompilerParams(dimension_semantics=semantics, vmem_limit_bytes=VMEM_LIMIT, **more)


def transpose_piece(j, last, src, dst):
    def piece(i):
        at = pl.ds(pl.multiple_of(i * LANES, LANES), LANES)
        dst[at, :] = src[:, at].T

    piece(j)
    pl.when(j == last)(lambda: piece(last + 1))


def forward_kernel(tiles, x, wg, wu, wd, gate, up, h_out, a_out, at, a, acc):
    j = pl.program_id(0)

    @pl.when(j == 0)
    def _():
        def rows(r):
            wide = x[r, :].astype(F32)
            a[r, :] = (wide * norm_scale(wide)).astype(BF16)

        in_rows(x.shape[0], 128, rows)
        clear(acc)

    transpose_piece(j, tiles - 1, a, at)
    for m in range(x.shape[0] // ROWS):
        r = pl.ds(m * ROWS, ROWS)
        g = dot(a[r, :], wg[0], NN)
        u = dot(a[r, :], wu[0], NN)
        gate[r, :] = g
        up[r, :] = u
        p = (g * lax.logistic(g) * u).astype(BF16)
        acc[r, :] += dot(p, wd[0], NN)

    @pl.when(j == tiles - 1)
    def _():
        def rows(r):
            h = (x[r, :].astype(F32) + acc[r, :].astype(BF16).astype(F32)).astype(BF16)
            h_out[r, :] = h
            wide = h.astype(F32)
            a_out[r, :] = (wide * norm_scale(wide)).astype(BF16)

        in_rows(x.shape[0], 128, rows)


def forward_call(x, wg, wu, wd):
    tokens, d = x.shape
    ff = wg.shape[2]
    tiles = ff // TILE
    w_in = spec((1, d, TILE), lambda j: (0, 0, j))
    return pl.pallas_call(
        functools.partial(forward_kernel, tiles),
        name="forward_0",
        grid=(tiles,),
        in_specs=[whole((tokens, d)), w_in, w_in, spec((1, TILE, d), lambda j: (0, j, 0))],
        out_specs=[spec((tokens, TILE), lambda j: (0, j))] * 2 + [whole((tokens, d))] * 2 + [whole((d, tokens))],
        out_shape=[jax.ShapeDtypeStruct((tokens, ff), F32)] * 2
        + [jax.ShapeDtypeStruct((tokens, d), BF16)] * 2
        + [jax.ShapeDtypeStruct((d, tokens), BF16)],
        scratch_shapes=[pltpu.VMEM((tokens, d), BF16), pltpu.VMEM((tokens, d), F32)],
        compiler_params=params(),
    )(x, wg, wu, wd)


class PairSum:
    def __init__(self, place, tiles, landing, stage, send, recv):
        self.place, self.tiles, self.landing, self.stage, self.send, self.recv = place, tiles, landing, stage, send, recv

    @staticmethod
    def scratch(tiles, rows, cols):
        dma = pltpu.SemaphoreType.DMA
        return [pltpu.VMEM((tiles, rows, cols), BF16), pltpu.VMEM((2, rows, cols), BF16), dma((2,)), dma((tiles,))]

    def copy(self, i):
        slot = lax.rem(i, 2)
        return put(self.stage.at[slot], self.landing.at[i], self.send.at[slot], self.recv.at[i], self.place.partner())

    def reserve(self, i):
        pl.when(i >= 2)(lambda: self.copy(i - 2).wait_send())
        return self.stage.at[lax.rem(i, 2)]

    def drain(self):
        for i in (self.tiles - 2, self.tiles - 1):
            self.copy(i).wait_send()


def hidden_back(gate, up, dp):
    dp = dp.astype(BF16).astype(F32)
    s = lax.logistic(gate)
    act = gate * s
    return (act * up).astype(BF16), (dp * up * (s + act * (1.0 - s))).astype(BF16), (dp * act).astype(BF16)


def down_gradient(j, tiles, pair, p, dy, half, out):
    core = pair.place.core

    def columns(c):
        return pl.ds(pl.multiple_of(c * half, LANES), half)

    @pl.when(j < tiles)
    def _():
        slot = pair.reserve(j)
        slot[...] = dot(p[lax.rem(j, 2)], dy[:, columns(1 - core)], TN).astype(BF16)
        pair.copy(j).start()

    @pl.when(j >= 1)
    def _():
        pair.copy(j - 1).wait_recv()
        own = dot(p[lax.rem(j - 1, 2)], dy[:, columns(core)], TN)
        out[...] = (own + pair.landing[j - 1].astype(F32)).astype(BF16)

    pl.when(j == tiles)(pair.drain)


def layer_kernel(tiles, a, dy, wg, wu, wd, dgu, at, out, p, *rest):
    j = pl.program_id(0)
    place = Place()
    pair = PairSum(place, tiles, *rest)
    pl.when(j == 0)(lambda: signal_all([place.partner()]))

    @pl.when(j < tiles)
    def _():
        transpose_piece(j, tiles - 1, a, at)
        slot = lax.rem(j, 2)
        for m in range(a.shape[0] // ROWS):
            r = pl.ds(m * ROWS, ROWS)
            g = dot(a[r, :], wg[0], NN)
            u = dot(a[r, :], wu[0], NN)
            dp = dot(dy[r, :], wd[0], NT)
            p[slot, r, :], dgu[0, r, :], dgu[1, r, :] = hidden_back(g, u, dp)

    down_gradient(j, tiles, pair, p, dy, dy.shape[1] // 2, out)


def clip(tiles, back=0):
    return lambda j: jnp.clip(j - back, 0, tiles - 1)


def layer_call(collective_id, a, dy, wg, wu, wd):
    tokens, d = a.shape
    ff = wg.shape[2]
    tiles, half = ff // TILE, d // 2
    now, before = clip(tiles), clip(tiles, 1)
    w_in = spec((1, d, TILE), lambda j: (1, 0, now(j)))
    return pl.pallas_call(
        functools.partial(layer_kernel, tiles),
        name="layer_1",
        grid=(tiles + 1,),
        in_specs=[whole((tokens, d))] * 2 + [w_in, w_in, spec((1, TILE, d), lambda j: (1, now(j), 0))],
        out_specs=[spec((2, tokens, TILE), lambda j: (0, 0, now(j))), whole((d, tokens)), spec((TILE, half), lambda j: (before(j), 0))],
        out_shape=[
            jax.ShapeDtypeStruct((2, tokens, ff), BF16),
            jax.ShapeDtypeStruct((d, tokens), BF16),
            jax.ShapeDtypeStruct((ff, half), BF16),
        ],
        scratch_shapes=[pltpu.VMEM((2, tokens, TILE), BF16), *PairSum.scratch(tiles, TILE, half)],
        compiler_params=params(collective_id),
    )(a, dy, wg, wu, wd)


GATE_ROWS, DOWN_WINDOW = 24, 72


def gate_up_kernel(tiles, cols, at, ahead, behind, sum_down, out, half0, half1, *rest):
    j = pl.program_id(0)
    place = Place()
    core = place.core
    pair = PairSum(place, tiles, *rest[:4])
    first = First.of(place, DOWN_WINDOW, cols, rest[4:9])
    load_sem, save_sem = rest[9:11]
    loads = loads_down(sum_down, first, load_sem)

    @pl.when(j == 0)
    def _():
        signal_all(near(place))
        begin(loads)

    @pl.when(j < tiles)
    def _():
        slot = pair.reserve(j)
        other = ahead[1 - core]
        for m in range(at.shape[0] // ROWS):
            r = pl.ds(m * ROWS, ROWS)
            slot[r, :] = dot(at[r, :], other, NN).astype(BF16)
        pair.copy(j).start()

    @pl.when(j >= 1)
    def _():
        pair.copy(j - 1).wait_recv()
        own = behind[core]
        for m in range(at.shape[0] // ROWS):
            r = pl.ds(m * ROWS, ROWS)
            out[r, :] = (dot(at[r, :], own, NN) + pair.landing[j - 1, r, :].astype(F32)).astype(BF16)

    pl.when(j == 0)(lambda: end(loads))
    spread(j, tiles + 1, 16, first.tick)

    @pl.when(j == tiles)
    def _():
        saves = copies(first.results(), (half0, half1), save_sem)
        begin(saves)
        pair.drain()
        first.drain()
        end(saves)


def gate_up_call(name, collective_id, at, dgu, sum_down):
    d, tokens = at.shape
    ff = dgu.shape[2]
    tiles, cols, dma = ff // TILE, sum_down.shape[-1], pltpu.SemaphoreType.DMA
    now, before = clip(tiles), clip(tiles, 1)
    return pl.pallas_call(
        functools.partial(gate_up_kernel, tiles, cols),
        name=name,
        grid=(tiles + 1,),
        in_specs=[
            whole((d, tokens)),
            spec((2, tokens, TILE), lambda j: (0, 0, now(j))),
            spec((2, tokens, TILE), lambda j: (0, 0, before(j))),
            HBM,
        ],
        out_specs=[spec((d, TILE), lambda j: (0, before(j))), HBM, HBM],
        out_shape=[jax.ShapeDtypeStruct((d, ff), BF16)] + [jax.ShapeDtypeStruct(s, BF16) for s in half_sums(DOWN_WINDOW, cols)],
        scratch_shapes=[*PairSum.scratch(tiles, d, TILE), *First.scratch(DOWN_WINDOW, cols), dma((SIDE,)), dma((2,))],
        compiler_params=params(collective_id),
    )(at, dgu, dgu, sum_down)


def middle_kernel(tiles, gate_cols, down_cols, dgu, wg, wu, h, dy, sum_gu, down0, down1, dh, half0, half1, out_down, acc_g, acc_u, *rest):
    j = pl.program_id(0)
    place = Place()
    first = First.of(place, GATE_ROWS, gate_cols, rest[:5])
    before = rest[5:7]
    down = Rest.of(place, DOWN_WINDOW, down_cols, before, rest[7:15])
    load_sem, save_sem = rest[15:17]
    loads = copies((sum_gu, down0, down1), (first.held, *before), load_sem)

    @pl.when(j == 0)
    def _():
        signal_all(near(place))
        begin(loads)
        clear(acc_g)
        clear(acc_u)

    for m in range(h.shape[0] // ROWS):
        r = pl.ds(m * ROWS, ROWS)
        acc_g[r, :] += dot(dgu[0, r, :], wg[0], NT)
        acc_u[r, :] += dot(dgu[1, r, :], wu[0], NT)

    pl.when(j == 0)(lambda: end(loads))
    down.tick(j)
    pl.when(j == 7)(lambda: down.result(out_down))
    spread(j, tiles, 16, first.tick)

    @pl.when(j == tiles - 1)
    def _():
        saves = copies(first.results(), (half0, half1), save_sem)
        begin(saves)

        def rows(r):
            wide = h[r, :].astype(F32)
            scale = norm_scale(wide)
            da = (acc_g[r, :].astype(BF16).astype(F32) + acc_u[r, :].astype(BF16).astype(F32)).astype(BF16).astype(F32)
            back = scale * da - wide * (scale * scale * scale * jnp.mean(da * wide, -1, keepdims=True))
            dh[r, :] = (dy[r, :].astype(F32) + back.astype(BF16).astype(F32)).astype(BF16)

        in_rows(h.shape[0], 64, rows)
        first.drain()
        down.drain()
        end(saves)


def middle_call(collective_id, dgu, wg, wu, h, dy, sum_gu, down_halves):
    tokens, d = h.shape
    ff = dgu.shape[2]
    tiles, dma, down_cols = ff // TILE, pltpu.SemaphoreType.DMA, d // 2
    w_in = spec((1, d, TILE), lambda j: (1, 0, j))
    return pl.pallas_call(
        functools.partial(middle_kernel, tiles, ff, down_cols),
        name="middle",
        grid=(tiles,),
        in_specs=[spec((2, tokens, TILE), lambda j: (0, 0, j)), w_in, w_in, whole((tokens, d)), whole((tokens, d)), HBM, HBM, HBM],
        out_specs=[whole((tokens, d)), HBM, HBM, whole((DOWN_WINDOW, down_cols))],
        out_shape=[jax.ShapeDtypeStruct((tokens, d), BF16)]
        + [jax.ShapeDtypeStruct(s, BF16) for s in half_sums(GATE_ROWS, ff)]
        + [jax.ShapeDtypeStruct((DOWN_WINDOW, down_cols), BF16)],
        scratch_shapes=[pltpu.VMEM((tokens, d), F32)] * 2
        + First.scratch(GATE_ROWS, ff)
        + [pltpu.VMEM(s, BF16) for s in half_sums(DOWN_WINDOW, down_cols)]
        + Rest.scratch(DOWN_WINDOW, down_cols)
        + [dma((3,)), dma((2,))],
        compiler_params=params(collective_id),
    )(dgu, wg, wu, h, dy, sum_gu.reshape(SIDE, SIDE, SIDE, GATE_ROWS, ff), *down_halves)


def back_kernel(tiles, gate_cols, dh, gate, up, wd, gate0, gate1, dgu, out, out_gu, p, *rest):
    j = pl.program_id(0)
    place = Place()
    pair = PairSum(place, tiles, *rest[:4])
    before = rest[4:6]
    sums = Rest.of(place, GATE_ROWS, gate_cols, before, rest[6:14])
    loads = copies((gate0, gate1), before, rest[14])

    @pl.when(j == 0)
    def _():
        signal_all(near(place))
        begin(loads)

    @pl.when(j < tiles)
    def _():
        slot = lax.rem(j, 2)
        for m in range(dh.shape[0] // ROWS):
            r = pl.ds(m * ROWS, ROWS)
            dp = dot(dh[r, :], wd[0], NT)
            p[slot, r, :], dgu[0, r, :], dgu[1, r, :] = hidden_back(gate[r, :], up[r, :], dp)

    down_gradient(j, tiles, pair, p, dh, dh.shape[1] // 2, out)
    pl.when(j == 0)(lambda: end(loads))
    sums.tick(j)
    pl.when(j == 7)(lambda: sums.result(out_gu))
    pl.when(j == tiles)(sums.drain)


def back_call(collective_id, dh, gate, up, wd, gate_halves):
    tokens, d = dh.shape
    ff = gate.shape[1]
    tiles, half, dma = ff // TILE, d // 2, pltpu.SemaphoreType.DMA
    now, before = clip(tiles), clip(tiles, 1)
    tile = spec((tokens, TILE), lambda j: (0, now(j)))
    return pl.pallas_call(
        functools.partial(back_kernel, tiles, ff),
        name="back_0",
        grid=(tiles + 1,),
        in_specs=[whole((tokens, d)), tile, tile, spec((1, TILE, d), lambda j: (0, now(j), 0)), HBM, HBM],
        out_specs=[spec((2, tokens, TILE), lambda j: (0, 0, now(j))), spec((TILE, half), lambda j: (before(j), 0)), whole((GATE_ROWS, ff))],
        out_shape=[
            jax.ShapeDtypeStruct((2, tokens, ff), BF16),
            jax.ShapeDtypeStruct((ff, half), BF16),
            jax.ShapeDtypeStruct((GATE_ROWS, ff), BF16),
        ],
        scratch_shapes=[pltpu.VMEM((2, tokens, TILE), BF16), *PairSum.scratch(tiles, TILE, half)]
        + [pltpu.VMEM(s, BF16) for s in half_sums(GATE_ROWS, ff)]
        + Rest.scratch(GATE_ROWS, ff)
        + [dma((2,))],
        compiler_params=params(collective_id),
    )(dh, gate, up, wd, *gate_halves)


def last_kernel(gate_cols, down_cols, sum_gu, down0, down1, out_gu, out_down, *rest):
    place = Place()
    first = First.of(place, GATE_ROWS, gate_cols, rest[:5])
    gu = Rest.of(place, GATE_ROWS, gate_cols, first.results(), rest[5:13])
    before = rest[13:15]
    down = Rest.of(place, DOWN_WINDOW, down_cols, before, rest[15:23])
    load_sem = rest[23]
    gate_loads = [pltpu.make_async_copy(sum_gu.at[x], first.held.at[x], load_sem.at[x]) for x in range(SIDE)]
    down_loads = [pltpu.make_async_copy(s, t, load_sem.at[SIDE + i]) for i, (s, t) in enumerate(zip((down0, down1), before, strict=True))]
    begin(gate_loads + down_loads)
    signal_all(near(place))
    end(gate_loads)
    for k in range(SIDE):
        first.start(k)
    end(down_loads)
    down.start(1)

    def phase0(n, _):
        lax.fori_loop(0, SIDE, lambda k, _: (first.step(n, k), 0)[1], 0)
        down.step1(n)
        return 0

    lax.fori_loop(1, 4, phase0, 0)
    gu.start(1)
    down.start(2)

    def phase1(n, _):
        gu.step1(n)
        down.step2(n)
        return 0

    lax.fori_loop(1, 4, phase1, 0)
    gu.start(2)
    down.result(out_down)
    lax.fori_loop(1, 4, lambda n, _: (gu.step2(n), 0)[1], 0)
    gu.result(out_gu)
    first.drain()
    gu.drain()
    down.drain()


def last_call(collective_id, sum_gu, down_halves, down_cols):
    ff = sum_gu.shape[1]
    vmem = pl.BlockSpec(memory_space=pltpu.VMEM)
    return pl.pallas_call(
        functools.partial(last_kernel, ff, down_cols),
        name="last_sums",
        in_specs=[HBM] * 3,
        out_specs=[vmem] * 2,
        out_shape=[jax.ShapeDtypeStruct((GATE_ROWS, ff), BF16), jax.ShapeDtypeStruct((DOWN_WINDOW, down_cols), BF16)],
        scratch_shapes=[
            *First.scratch(GATE_ROWS, ff),
            *Rest.scratch(GATE_ROWS, ff),
            *[pltpu.VMEM(s, BF16) for s in half_sums(DOWN_WINDOW, down_cols)],
            *Rest.scratch(DOWN_WINDOW, down_cols),
            pltpu.SemaphoreType.DMA((SIDE + 2,)),
        ],
        compiler_params=pltpu.CompilerParams(collective_id=collective_id, has_side_effects=True, vmem_limit_bytes=VMEM_LIMIT),
    )(sum_gu.reshape(SIDE, SIDE, SIDE, GATE_ROWS, ff), *down_halves)


def flat(m):
    layers, rows, cols = m.shape
    split = m.transpose(1, 0, 2).reshape(rows, layers, cols // LANES, LANES)
    return with_layout_constraint(split, Layout((0, 2, 1, 3))).transpose(0, 2, 1, 3).reshape(-1, LANES)


def unflat(f, shape):
    layers, rows, cols = shape
    split = f.reshape(rows, cols // LANES, layers, LANES).transpose(0, 2, 1, 3)
    return with_layout_constraint(split, Layout((0, 2, 1, 3))).reshape(rows, layers, cols).transpose(1, 0, 2)


def solution(mesh):
    def body(x, dy, wg, wu, wd, mg, mu, md, vg, vu, vd):
        layers, d, ff = wg.shape
        x, dy = x[0], dy[0]
        windows = (SIDE, SIDE, 4 * 66, d // 2)
        gate0, up0, h1, a1, a0t = forward_call(x, wg, wu, wd)
        dgu1, a1t, down1 = layer_call(1, a1, dy, wg, wu, wd)
        gu1, *down1_halves = gate_up_call("gate_up_1", 2, a1t, dgu1, down1.reshape(windows))
        dh1, *rest = middle_call(3, dgu1, wg, wu, h1, dy, gu1, down1_halves)
        gu1_halves, sum_down1 = rest[:2], rest[2]
        dgu0, down0, sum_gu1 = back_call(4, dh1, gate0, up0, wd, gu1_halves)
        gu0, *down0_halves = gate_up_call("gate_up_0", 5, a0t, dgu0, down0.reshape(windows))
        sum_gu0, sum_down0 = last_call(6, gu0, down0_halves, d // 2)

        views = [(2, SIDE, SIDE, SIDE, GATE_ROWS, ff)] * 2 + [(2, SIDE, SIDE, 4 * 66, d)]
        w = [t.reshape(view) for t, view in zip((wg, wu, wd), views, strict=True)]
        m, v = [flat(t) for t in (mg, mu, md)], [flat(t) for t in (vg, vu, vd)]
        out = finish_call(3 * layers * d * ff, 7, [sum_gu0, sum_gu1], [sum_down0, sum_down1], m, v, w)
        new = [t.reshape(like.shape) for t, like in zip(out[:3], (wg, wu, wd), strict=True)]
        return (*new, *[unflat(t, like.shape) for t, like in zip(out[3:], (mg, mu, md, vg, vu, vd), strict=True)])

    shard = P(None, "dp", None)
    return jax.shard_map(
        body,
        mesh=mesh,
        in_specs=(P(("rep", "dp")), P(("rep", "dp")), P(), P(), P(), *[shard] * 6),
        out_specs=(P("rep"), P("rep"), P("rep"), *[P("rep", "dp", None)] * 6),
        check_vma=False,
    )
```

time: 4200 us -> 716 us (0.17)
  blocking collectives: 2420 us -> 0 us
  Pallas kernels: 0 us -> 646 us
  starting transfers between devices: 527 us -> 0 us
  local copies, waits for them, and re-layouts: 558 us -> 60.3 us
  matrix products: 349 us -> 0 us
  waiting for transfers between devices: 238 us -> 0 us
    unnamed x6 -> x0, blocking collectives: 2360 us -> none
    pallas_call x0 -> x8, Pallas kernels: none -> 646 us  [the longest x1 178 us: finish_call(): pl.pallas_call(functools.partial(finish_kernel, count), name='finish', ou...]
    unnamed x174 -> x0, starting transfers between devices: 527 us -> none
    unnamed x299 -> x35, local copies, waits for them, and re-layouts: 550 us -> 60.3 us
    dot_general x15 -> x0, matrix products: 349 us -> none  [the longest x5 120 us: layer(): up = jnp.dot(a, w['w_up'], preferred_element_type=jnp.float32)]
    reshape x3 -> x0, waiting for transfers between devices: 227 us -> none  [step(): t.reshape(-1, *t.shape[2:])]
    reduce_sum x1 -> x0, blocking collectives: 66 us -> none  [of_a_group(): jnp.sum(g * g)]
  transfers between devices with their start and end apart: 177 -> 0, of which waited for: 10 -> 0; matrix products, arithmetic and copies ran while one was open for 64% -> 0% of each run, Pallas kernels for 0% -> 0%
where the time goes in v2:
time: 716 us; the launch traced here: 707 us
  Pallas kernels  646 us (90%)
  local copies, waits for them, and re-layouts  60.3 us (8%)
    pallas_call x1, Pallas kernels, finish_call(): pl.pallas_call(functools.partial(finish_kernel, count), name='finish', ou...  178 us
    pallas_call x2, Pallas kernels, gate_up_call(): pl.pallas_call(functools.partial(gate_up_kernel, tiles, cols), name=name,...  109 us
    pallas_call x1, Pallas kernels, layer_call(): pl.pallas_call(functools.partial(layer_kernel, tiles), name='layer_1', gr...  86.8 us
    pallas_call x1, Pallas kernels, last_call(): pl.pallas_call(functools.partial(last_kernel, ff, down_cols), name='last_...  74.5 us
    pallas_call x1, Pallas kernels, forward_call(): pl.pallas_call(functools.partial(forward_kernel, tiles), name='forward_0'...  73.9 us
    pallas_call x1, Pallas kernels, middle_call(): pl.pallas_call(functools.partial(middle_kernel, tiles, ff, down_cols), na...  66 us
    unnamed x35, local copies, waits for them, and re-layouts  60.3 us
    pallas_call x1, Pallas kernels, back_call(): pl.pallas_call(functools.partial(back_kernel, tiles, ff), name='back_0',...  57.6 us

profile of v2, /device:TPU:1, one launch (start us, length us, event | category | flops | bytes accessed | tf_op | source)
XLA Modules:
  0.0 707.0 jit_solution(12468386328771526649)
XLA Ops:
  0.6 73.9 %forward_0.1 = (f32[1024,4224]{1,0:T(8,128)}, f32[1024,4224]{1,0:T(8,128)}, bf16[1024,1536]{1,0:T(8,128)(2,1)}, bf16[1024,1536]{1,0:T(8,128)(2,1)}, bf16[1536,1024]{1,0:T(8,128)(2,1)}) custom-call(bf16[1024,1536]{1,0:T(8,128)(2,1)} %bitcast.110, bf16[2,1536,4224]{2,1,0:T(8,128)(2,1)} %wg.5, bf16[2,1536,4224]{2,1,0:T(8,128)(2,1)} %wu.5, bf16[2,4224,1536]{2,1,0:T(8,128)(2,1)} %wd.5), custom_call_target="tpu_custom_call" | custom-call | tf_op jit(solution)/shard_map/forward_0/pallas_call | solution.py:655
  74.6 86.8 %layer_1.1 = (bf16[2,1024,4224]{2,1,0:T(8,128)(2,1)}, bf16[1536,1024]{1,0:T(8,128)(2,1)}, bf16[4224,768]{1,0:T(8,128)(2,1)}) custom-call(bf16[1024,1536]{1,0:T(8,128)(2,1)} %get-tuple-element.42.a, bf16[1024,1536]{1,0:T(8,128)(2,1)} %bitcast.106, bf16[2,1536,4224]{2,1,0:T(8,128)(2,1)} %wg.5, bf16[2,1536,4224]{2,1,0:T(8,128)(2,1)} %wu.5, ...), custom_call_target="tpu_custom_call" | custom-call | tf_op jit(solution)/shard_map/layer_1/pallas_call | solution.py:749
  161.4 56.7 %gate_up_1.1 = (bf16[1536,4224]{1,0:T(8,128)(2,1)}, bf16[3,4,4,24,384]{4,3,2,1,0:T(8,128)(2,1)}, bf16[3,4,4,24,384]{4,3,2,1,0:T(8,128)(2,1)}) custom-call(bf16[1536,1024]{1,0:T(8,128)(2,1)} %get-tuple-element.45.at, bf16[2,1024,4224]{2,1,0:T(8,128)(2,1)} %get-tuple-element.43.ahead.behind.dgu, bf16[2,1024,4224]{2,1,0:T(8,128)(2,1)} %get-tuple-element.43.ahead.behind.dgu, ...), custom_call_target="tpu_custom_call" | custom-call | tf_op jit(solution)/shard_map/gate_up_1/pallas_call | solution.py:816
  218.2 66.0 %middle.1 = (bf16[1024,1536]{1,0:T(8,128)(2,1)}, bf16[3,4,4,8,2176]{4,3,2,1,0:T(8,128)(2,1)}, bf16[3,4,4,8,2048]{4,3,2,1,0:T(8,128)(2,1)}, bf16[72,768]{1,0:T(8,128)(2,1)}) custom-call(bf16[2,1024,4224]{2,1,0:T(8,128)(2,1)} %get-tuple-element.43.ahead.behind.dgu, bf16[2,1536,4224]{2,1,0:T(8,128)(2,1)} %wg.5, bf16[2,1536,4224]{2,1,0:T(8,128)(2,1)} %wu.5, ...), custom_call_target="tpu_custom_call" | custom-call | tf_op jit(solution)/shard_map/middle/pallas_call | solution.py:882
  284.2 57.6 %back_0.1 = (bf16[2,1024,4224]{2,1,0:T(8,128)(2,1)}, bf16[4224,768]{1,0:T(8,128)(2,1)}, bf16[24,4224]{1,0:T(8,128)(2,1)}) custom-call(bf16[1024,1536]{1,0:T(8,128)(2,1)} %get-tuple-element.50.dh, f32[1024,4224]{1,0:T(8,128)} %get-tuple-element.51.gate, f32[1024,4224]{1,0:T(8,128)} %get-tuple-element.52.up, bf16[2,4224,1536]{2,1,0:T(8,128)(2,1)} %wd.5, ...), custom_call_target="tpu_custom_call" | custom-call | tf_op jit(solution)/shard_map/back_0/pallas_call | solution.py:934
  341.8 52.5 %gate_up_0.1 = (bf16[1536,4224]{1,0:T(8,128)(2,1)}, bf16[3,4,4,24,384]{4,3,2,1,0:T(8,128)(2,1)}, bf16[3,4,4,24,384]{4,3,2,1,0:T(8,128)(2,1)}) custom-call(bf16[1536,1024]{1,0:T(8,128)(2,1)} %get-tuple-element.41.at, bf16[2,1024,4224]{2,1,0:T(8,128)(2,1)} %get-tuple-element.55.ahead.behind, bf16[2,1024,4224]{2,1,0:T(8,128)(2,1)} %get-tuple-element.55.ahead.behind, ...), custom_call_target="tpu_custom_call" | custom-call | tf_op jit(solution)/shard_map/gate_up_0/pallas_call | solution.py:816
  394.3 74.5 %last_sums.1 = (bf16[24,4224]{1,0:T(8,128)(2,1)}, bf16[72,768]{1,0:T(8,128)(2,1)}) custom-call(bf16[4,4,4,24,4224]{4,3,2,1,0:T(8,128)(2,1)} %bitcast.105, bf16[3,4,4,24,384]{4,3,2,1,0:T(8,128)(2,1)} %get-tuple-element.58.down0, bf16[3,4,4,24,384]{4,3,2,1,0:T(8,128)(2,1)} %get-tuple-element.59.down1), custom_call_target="tpu_custom_call" | custom-call | tf_op jit(solution)/shard_map/last_sums/pallas_call | solution.py:997
  468.8 177.6 %finish.1 = (bf16[2,4,4,4,24,4224]{5,4,3,2,1,0:T(8,128)(2,1)}, bf16[2,4,4,4,24,4224]{5,4,3,2,1,0:T(8,128)(2,1)}, bf16[2,4,4,264,1536]{4,3,2,1,0:T(8,128)(2,1)}, ...) custom-call(bf16[24,4224]{1,0:T(8,128)(2,1)} %get-tuple-element.60.r, ...), custom_call_target="tpu_custom_call" | custom-call | flops 1000000000 | bytes 100000000 | tf_op jit(solution)/shard_map/finish/pallas_call | solution.py:549
  646.4 0.0 slice-start
  646.4 0.0 slice-start.1
  646.4 0.0 slice-start.2
  646.4 0.0 slice-start.3
  646.4 23.9 %copy.29 = bf16[2,1536,4224]{2,1,0:T(8,128)(2,1)} copy(bf16[2,1536,4224]{2,1,0:T(8,128)(2,1)} %bitcast.103) | data formatting | bytes 51904512
  670.3 22.6 %copy.30 = bf16[2,1536,4224]{2,1,0:T(8,128)(2,1)} copy(bf16[2,1536,4224]{2,1,0:T(8,128)(2,1)} %bitcast.102) | data formatting | bytes 51904512
  692.8 0.0 slice-done
  692.8 0.0 slice-done.2
  692.9 9.4 %copy.31 = bf16[2,4224,1536]{2,1,0:T(8,128)(2,1)} copy(bf16[2,4224,1536]{2,1,0:T(8,128)(2,1)S(1)} %bitcast.101) | data formatting | bytes 51904512
  702.3 0.8 copy.32
  703.1 0.8 copy.33
  703.8 0.8 copy.34
  704.6 0.0 copy-done.2
  704.6 0.8 copy.35
  705.3 0.8 copy.36
  706.1 0.8 copy.37
  (20 shorter events, 0.0 us)
Async XLA Ops:
  646.4 46.5 %slice-start = ((s8[25952256]{0:T(1024)(128)(4,1)}), s8[4194304]{0:T(1024)(128)(4,1)S(1)}, s32[]{:S(2)}) async-start(s8[25952256]{0:T(1024)(128)(4,1)} %bitcast.99), calls=%async_computation | async-start | bytes 8388608
  646.4 46.5 %slice-start.1 = ((s8[25952256]{0:T(1024)(128)(4,1)}), s8[4194304]{0:T(1024)(128)(4,1)S(1)}, s32[]{:S(2)}) async-start(s8[25952256]{0:T(1024)(128)(4,1)} %bitcast.99), calls=%async_computation.1 | async-start | bytes 8388608
  646.4 46.4 %slice-start.2 = ((s8[25952256]{0:T(1024)(128)(4,1)}), s8[4194304]{0:T(1024)(128)(4,1)S(1)}, s32[]{:S(2)}) async-start(s8[25952256]{0:T(1024)(128)(4,1)} %bitcast.99), calls=%async_computation.2 | async-start | bytes 8388608
  646.4 46.4 %slice-start.3 = ((s8[25952256]{0:T(1024)(128)(4,1)}), s8[4194304]{0:T(1024)(128)(4,1)S(1)}, s32[]{:S(2)}) async-start(s8[25952256]{0:T(1024)(128)(4,1)} %bitcast.99), calls=%async_computation.3 | async-start | bytes 8388608
  670.3 22.6 %slice-start.4 = ((s8[25952256]{0:T(1024)(128)(4,1)}), s8[4194304]{0:T(1024)(128)(4,1)S(1)}, s32[]{:S(2)}) async-start(s8[25952256]{0:T(1024)(128)(4,1)} %bitcast.99), calls=%async_computation.4 | async-start | bytes 8388608
  670.3 22.6 %slice-start.5 = ((s8[25952256]{0:T(1024)(128)(4,1)}), s8[4194304]{0:T(1024)(128)(4,1)S(1)}, s32[]{:S(2)}) async-start(s8[25952256]{0:T(1024)(128)(4,1)} %bitcast.99), calls=%async_computation.5 | async-start | bytes 8388608
  670.3 22.6 %slice-start.6 = ((s8[25952256]{0:T(1024)(128)(4,1)}), s8[786432]{0:T(1024)(128)(4,1)S(1)}, s32[]{:S(2)}) async-start(s8[25952256]{0:T(1024)(128)(4,1)} %bitcast.99), calls=%async_computation.6 | async-start | bytes 1572864
  692.9 9.4 %copy-start.5 = (f32[792,128]{1,0:T(8,128)S(1)}, f32[792,128]{1,0:T(8,128)}, u32[]{:S(2)}) copy-start(f32[792,128]{1,0:T(8,128)} %get-tuple-element.67) | copy-start | bytes 1216516
  692.9 10.2 %copy-start.4 = (f32[792,128]{1,0:T(8,128)S(1)}, f32[792,128]{1,0:T(8,128)}, u32[]{:S(2)}) copy-start(f32[792,128]{1,0:T(8,128)} %get-tuple-element.68) | copy-start | bytes 1216516
  692.9 10.9 %copy-start.3 = (f32[792,128]{1,0:T(8,128)S(1)}, f32[792,128]{1,0:T(8,128)}, u32[]{:S(2)}) copy-start(f32[792,128]{1,0:T(8,128)} %get-tuple-element.69) | copy-start | bytes 1216516
  692.9 11.6 %copy-start.2 = (f32[792,128]{1,0:T(8,128)S(1)}, f32[792,128]{1,0:T(8,128)}, u32[]{:S(2)}) copy-start(f32[792,128]{1,0:T(8,128)} %get-tuple-element.70) | copy-start | bytes 1216516
  692.9 12.4 %copy-start.1 = (f32[792,128]{1,0:T(8,128)S(1)}, f32[792,128]{1,0:T(8,128)}, u32[]{:S(2)}) copy-start(f32[792,128]{1,0:T(8,128)} %get-tuple-element.71) | copy-start | bytes 1216516
  692.9 13.1 %copy-start = (f32[792,128]{1,0:T(8,128)S(1)}, f32[792,128]{1,0:T(8,128)}, u32[]{:S(2)}) copy-start(f32[792,128]{1,0:T(8,128)} %get-tuple-element.72) | copy-start | bytes 1216516

commit v3 on v2

--- a/solution.py
+++ b/solution.py
@@ -763,16 +763,213 @@
 
 
 GATE_ROWS, DOWN_WINDOW = 24, 72
-
-
-def gate_up_kernel(tiles, cols, at, ahead, behind, sum_down, out, half0, half1, *rest):
+RING = 6
+
+
+def second(t, v, rest=ALL):
+    return (rest, v) if t == 1 else (v, rest)
+
+
+class Stream:
+    def __init__(self, place, tiles, phases, refs):
+        self.place, self.tiles, self.phases, self.rows = place, tiles, phases, GATE_ROWS // 3
+        self.held, self.slots, self.send, self.recv = refs[0], refs[1 : 1 + 2 * phases], refs[-2], refs[-1]
+        self.ways = ways_of(TILE)
+
+    @staticmethod
+    def scratch(tiles, phases):
+        third, dma = GATE_ROWS // 3, pltpu.SemaphoreType.DMA
+        leads = [(3, 3, tiles, SIDE, SIDE), (3, 3, tiles, SIDE), (3, 3, tiles)][:phases]
+        slots = [pltpu.VMEM((*lead, third, width), BF16) for lead in leads for _, width in ways_of(TILE)]
+        return [pltpu.VMEM((RING, SIDE, SIDE, SIDE, GATE_ROWS, TILE), BF16), *slots, dma((tiles, 3 * phases)), dma((tiles, 3 * phases))]
+
+    def part(self, t, way):
+        start, width = self.ways[way]
+        return pl.ds(t * self.rows, self.rows), pl.ds(start, width)
+
+    def own(self, c, t, way, hops, b=ALL, d=ALL):
+        at = index(ORDERS[t], (self.place.block(ORDERS[t][0], way, hops), ALL, ALL))
+        axes = [i for i in range(3) if i != ORDERS[t][0]]
+        at = list(at)
+        at[axes[0]], at[axes[1]] = b, d
+        return self.held.at[(lax.rem(c, RING), *at, *self.part(t, way))]
+
+    def copy(self, phase, t, way, n, c, first=False):
+        axis = ORDERS[t][phase]
+        slots = self.slots[2 * phase + way]
+        if not first:
+            src = slots.at[t, n - 1, c]
+        elif phase == 0:
+            src = self.own(c, t, way, 1)
+        else:
+            v = self.place.block(axis, way, 1)
+            at = second(t, v) if phase == 1 else (v,)
+            src = self.slots[2 * phase - 2 + way].at[(t, 2, c, *at)]
+        key = (c, 3 * phase + n)
+        return put(src, slots.at[t, n, c], self.send.at[key], self.recv.at[key], self.place.device(axis, self.place.onward(way)))
+
+    def pairs(self):
+        return [(t, way) for t in range(3) for way in range(2)]
+
+    def all_of(self, phase):
+        return self.held.at[(0,) * (phase + 2)]
+
+    def begin(self, phase, c):
+        for t, way in self.pairs():
+            self.copy(phase, t, way, 0, c, first=True).start()
+
+    def add(self, phase, t, way, n, c):
+        slots = self.slots[2 * phase + way]
+        v = self.place.block(ORDERS[t][phase], way, n + 1)
+
+        def one(at, other):
+            at = (t, n - 1, c, *at)
+            slots[at] = (slots[at].astype(F32) + other[...].astype(F32)).astype(BF16)
+
+        if phase == 0:
+            for b in range(SIDE):
+                for d in range(SIDE):
+                    one((b, d), self.own(c, t, way, n + 1, b, d))
+        elif phase == 1:
+            for d in range(SIDE):
+                one((d,), self.slots[way].at[(t, 2, c, *second(t, v, d))])
+        else:
+            one((), self.slots[2 + way].at[t, 2, c, v])
+
+    def stage(self, s, c, out):
+        phase, n = (s - 1) // 3, (s - 1) % 3 + 1
+        key = (c, 3 * phase + n - 1)
+        whole_stage = self.all_of(phase)
+        pltpu.make_async_copy(whole_stage, whole_stage, self.recv.at[key]).wait()
+        for t, way in self.pairs():
+            self.add(phase, t, way, n, c)
+            if n < 3:
+                self.copy(phase, t, way, n, c).start()
+        if n == 3 and phase + 1 < self.phases:
+            self.begin(phase + 1, c)
+        if n == 3 and phase == 2:
+            for t, way in self.pairs():
+                rows, _ = self.part(t, way)
+                start, width = self.ways[way]
+                out[rows, pl.ds(pl.multiple_of(c * TILE + start, LANES), width)] = self.slots[4 + way][t, 2, c]
+
+    def sent(self, phase, n, c):
+        whole_stage = self.all_of(phase)
+        pltpu.make_async_copy(whole_stage, whole_stage, self.send.at[c, 3 * phase + n]).wait()
+
+    def keep(self, c):
+        pl.when(c >= RING)(lambda: self.sent(0, 0, c - RING))
+        return self.held.at[lax.rem(c, RING)]
+
+    def step(self, newest, out=None):
+        valid = lambda c: (c >= 0) & (c < self.tiles)
+        pl.when(valid(newest))(lambda: self.begin(0, newest))
+        for s in range(3 * self.phases, 0, -1):
+            pl.when(valid(newest - s))(lambda s=s: self.stage(s, newest - s, out))
+
+    def drain(self):
+        def each(c, _):
+            pl.when(c >= self.tiles - RING)(lambda: self.sent(0, 0, c))
+            for i in range(1, 3 * self.phases):
+                self.sent(i // 3, i % 3, c)
+            return 0
+
+        lax.fori_loop(0, self.tiles, each, 0)
+
+    def results(self):
+        return [self.slots[way].at[:, 2] for way in range(2)]
+
+
+def stream_halves(tiles):
+    return [(3, tiles, SIDE, SIDE, GATE_ROWS // 3, width) for _, width in ways_of(TILE)]
+
+
+class StreamRest:
+    def __init__(self, place, tiles, before, refs):
+        self.place, self.tiles, self.before, self.slots, self.sems = place, tiles, before, refs[:4], refs[4:8]
+        self.rows, self.ways = GATE_ROWS // 3, ways_of(TILE)
+
+    @staticmethod
+    def scratch(tiles):
+        third, dma = GATE_ROWS // 3, pltpu.SemaphoreType.DMA
+        shapes = [pltpu.VMEM((3, 3, *lead, third, width), BF16) for lead in ((tiles, SIDE), (tiles,)) for _, width in ways_of(TILE)]
+        return shapes + [dma((3, 2, 3))] * 4
+
+    def pairs(self):
+        return [(t, way) for t in range(3) for way in range(2)]
+
+    def message(self, phase, t, way, n, arriving=False):
+        slots = self.slots[2 * phase - 2 + way]
+        axis = ORDERS[t][phase]
+        if arriving:
+            src = slots.at[t, n]
+        elif isinstance(n, int) and n == 0:
+            v = self.place.block(axis, way, 1)
+            src = self.before[way].at[(t, ALL, *second(t, v))] if phase == 1 else self.slots[way].at[t, 2, :, v]
+        else:
+            src = slots.at[t, n - 1]
+        send, recv = self.sems[2 * phase - 2 : 2 * phase]
+        key = (t, way, n)
+        return put(src, slots.at[t, n], send.at[key], recv.at[key], self.place.device(axis, self.place.onward(way)))
+
+    def start(self, phase):
+        for t, way in self.pairs():
+            self.message(phase, t, way, 0).start()
+
+    def step(self, phase, n):
+        for t, way in self.pairs():
+            self.message(phase, t, way, n - 1, arriving=True).wait_recv()
+            v = self.place.block(ORDERS[t][phase], way, n + 1)
+            slots = self.slots[2 * phase - 2 + way]
+
+            def add(c, _, t=t, way=way, v=v, slots=slots):
+                for d in range(SIDE if phase == 1 else 1):
+                    at = (t, n - 1, c, d) if phase == 1 else (t, n - 1, c)
+                    other = self.before[way].at[(t, c, *second(t, v, d))] if phase == 1 else self.slots[way].at[t, 2, c, v]
+                    slots[at] = (slots[at].astype(F32) + other[...].astype(F32)).astype(BF16)
+                return 0
+
+            lax.fori_loop(0, self.tiles, add, 0)
+            pl.when(n < 3)(lambda t=t, way=way: self.message(phase, t, way, n).start())
+
+    def tick(self, i):
+        pl.when(i == 0)(lambda: self.start(1))
+        pl.when((i >= 1) & (i <= 3))(lambda: self.step(1, i))
+        pl.when(i == 3)(lambda: self.start(2))
+        pl.when((i >= 4) & (i <= 6))(lambda: self.step(2, i - 3))
+
+    def result(self, out):
+        def one(c, _):
+            for t, way in self.pairs():
+                start, width = self.ways[way]
+                lanes = pl.ds(pl.multiple_of(c * TILE + start, LANES), width)
+                out[pl.ds(t * self.rows, self.rows), lanes] = self.slots[2 + way][t, 2, c]
+            return 0
+
+        lax.fori_loop(0, self.tiles, one, 0)
+
+    def drain(self):
+        for t, way in self.pairs():
+            for phase in (1, 2):
+                for n in range(3):
+                    self.message(phase, t, way, n).wait_send()
+
+
+BLOCK_ROWS = SIDE * SIDE * GATE_ROWS
+
+
+def gate_up_kernel(tiles, phases, cols, at, ahead, behind, sum_down, *rest):
     j = pl.program_id(0)
     place = Place()
     core = place.core
+    outs, rest = (rest[:4], rest[4:]) if phases == 1 else (rest[:2], rest[2:])
     pair = PairSum(place, tiles, *rest[:4])
     first = First.of(place, DOWN_WINDOW, cols, rest[4:9])
-    load_sem, save_sem = rest[9:11]
+    stream = Stream(place, tiles, phases, rest[9 : 9 + 3 + 2 * phases])
+    rest = rest[9 + 3 + 2 * phases :]
+    load_sem, save_sem = rest[:2]
     loads = loads_down(sum_down, first, load_sem)
+    last = tiles + 3 * phases
 
     @pl.when(j == 0)
     def _():
@@ -783,61 +980,90 @@
     def _():
         slot = pair.reserve(j)
         other = ahead[1 - core]
-        for m in range(at.shape[0] // ROWS):
-            r = pl.ds(m * ROWS, ROWS)
+        for m in range(SIDE):
+            r = pl.ds(m * BLOCK_ROWS, BLOCK_ROWS)
             slot[r, :] = dot(at[r, :], other, NN).astype(BF16)
         pair.copy(j).start()
 
-    @pl.when(j >= 1)
+    @pl.when((j >= 1) & (j <= tiles))
     def _():
         pair.copy(j - 1).wait_recv()
         own = behind[core]
-        for m in range(at.shape[0] // ROWS):
-            r = pl.ds(m * ROWS, ROWS)
-            out[r, :] = (dot(at[r, :], own, NN) + pair.landing[j - 1, r, :].astype(F32)).astype(BF16)
-
+        kept = stream.keep(j - 1)
+        for m in range(SIDE):
+            r = pl.ds(m * BLOCK_ROWS, BLOCK_ROWS)
+            total = (dot(at[r, :], own, NN) + pair.landing[j - 1, r, :].astype(F32)).astype(BF16)
+            kept[m] = total.reshape(SIDE, SIDE, GATE_ROWS, TILE)
+
+    if phases == 1:
+        stream.step(j - 1)
+    else:
+        stream.step(j - 1, outs[0])
     pl.when(j == 0)(lambda: end(loads))
-    spread(j, tiles + 1, 16, first.tick)
-
-    @pl.when(j == tiles)
-    def _():
-        saves = copies(first.results(), (half0, half1), save_sem)
-        begin(saves)
+    if phases == 1:
+        pl.when(j <= tiles)(lambda: spread(j, tiles + 1, 16, first.tick))
+    else:
+        down = Rest.of(place, DOWN_WINDOW, cols, first.results(), rest[2:10])
+        pl.when(j < 8)(lambda: spread(j, 8, 16, first.tick))
+        pl.when(j >= 8)(lambda: down.tick(j - 8))
+        pl.when(j == 15)(lambda: down.result(outs[1]))
+
+    @pl.when(j == last)
+    def _():
         pair.drain()
+        if phases == 1:
+            saves = copies([*first.results(), *stream.results()], outs, save_sem)
+            begin(saves)
         first.drain()
-        end(saves)
-
-
-def gate_up_call(name, collective_id, at, dgu, sum_down):
+        stream.drain()
+        if phases == 1:
+            end(saves)
+        else:
+            down.drain()
+
+
+def gate_up_call(name, collective_id, phases, at, dgu, sum_down):
     d, tokens = at.shape
     ff = dgu.shape[2]
     tiles, cols, dma = ff // TILE, sum_down.shape[-1], pltpu.SemaphoreType.DMA
     now, before = clip(tiles), clip(tiles, 1)
+    if phases == 1:
+        shapes = [*half_sums(DOWN_WINDOW, cols), *stream_halves(tiles)]
+        out_specs, more = [HBM] * 4, []
+    else:
+        shapes = [(GATE_ROWS, ff), (DOWN_WINDOW, cols)]
+        out_specs, more = [whole(s) for s in shapes], Rest.scratch(DOWN_WINDOW, cols)
     return pl.pallas_call(
-        functools.partial(gate_up_kernel, tiles, cols),
+        functools.partial(gate_up_kernel, tiles, phases, cols),
         name=name,
-        grid=(tiles + 1,),
+        grid=(tiles + 3 * phases + 1,),
         in_specs=[
             whole((d, tokens)),
             spec((2, tokens, TILE), lambda j: (0, 0, now(j))),
             spec((2, tokens, TILE), lambda j: (0, 0, before(j))),
             HBM,
         ],
-        out_specs=[spec((d, TILE), lambda j: (0, before(j))), HBM, HBM],
-        out_shape=[jax.ShapeDtypeStruct((d, ff), BF16)] + [jax.ShapeDtypeStruct(s, BF16) for s in half_sums(DOWN_WINDOW, cols)],
-        scratch_shapes=[*PairSum.scratch(tiles, d, TILE), *First.scratch(DOWN_WINDOW, cols), dma((SIDE,)), dma((2,))],
+        out_specs=out_specs,
+        out_shape=[jax.ShapeDtypeStruct(s, BF16) for s in shapes],
+        scratch_shapes=[
+            *PairSum.scratch(tiles, d, TILE),
+            *First.scratch(DOWN_WINDOW, cols),
+            *Stream.scratch(tiles, phases),
+            dma((SIDE,)),
+            dma((4,)),
+            *more,
+        ],
         compiler_params=params(collective_id),
     )(at, dgu, dgu, sum_down)
 
 
-def middle_kernel(tiles, gate_cols, down_cols, dgu, wg, wu, h, dy, sum_gu, down0, down1, dh, half0, half1, out_down, acc_g, acc_u, *rest):
+def middle_kernel(tiles, down_cols, dgu, wg, wu, h, dy, down0, down1, gate0, gate1, dh, out_down, out_gu, acc_g, acc_u, *rest):
     j = pl.program_id(0)
     place = Place()
-    first = First.of(place, GATE_ROWS, gate_cols, rest[:5])
-    before = rest[5:7]
-    down = Rest.of(place, DOWN_WINDOW, down_cols, before, rest[7:15])
-    load_sem, save_sem = rest[15:17]
-    loads = copies((sum_gu, down0, down1), (first.held, *before), load_sem)
+    before = rest[:4]
+    down = Rest.of(place, DOWN_WINDOW, down_cols, before[:2], rest[4:12])
+    gate = StreamRest(place, gate0.shape[1], before[2:], rest[12:20])
+    loads = copies((down0, down1, gate0, gate1), before, rest[20])
 
     @pl.when(j == 0)
     def _():
@@ -853,14 +1079,15 @@
 
     pl.when(j == 0)(lambda: end(loads))
     down.tick(j)
-    pl.when(j == 7)(lambda: down.result(out_down))
-    spread(j, tiles, 16, first.tick)
+    gate.tick(j)
+
+    @pl.when(j == 7)
+    def _():
+        down.result(out_down)
+        gate.result(out_gu)
 
     @pl.when(j == tiles - 1)
     def _():
-        saves = copies(first.results(), (half0, half1), save_sem)
-        begin(saves)
-
         def rows(r):
             wide = h[r, :].astype(F32)
             scale = norm_scale(wide)
@@ -869,46 +1096,37 @@
             dh[r, :] = (dy[r, :].astype(F32) + back.astype(BF16).astype(F32)).astype(BF16)
 
         in_rows(h.shape[0], 64, rows)
-        first.drain()
         down.drain()
-        end(saves)
-
-
-def middle_call(collective_id, dgu, wg, wu, h, dy, sum_gu, down_halves):
+        gate.drain()
+
+
+def middle_call(collective_id, dgu, wg, wu, h, dy, halves):
     tokens, d = h.shape
     ff = dgu.shape[2]
     tiles, dma, down_cols = ff // TILE, pltpu.SemaphoreType.DMA, d // 2
     w_in = spec((1, d, TILE), lambda j: (1, 0, j))
+    sums = [(DOWN_WINDOW, down_cols), (GATE_ROWS, ff)]
     return pl.pallas_call(
-        functools.partial(middle_kernel, tiles, ff, down_cols),
+        functools.partial(middle_kernel, tiles, down_cols),
         name="middle",
         grid=(tiles,),
-        in_specs=[spec((2, tokens, TILE), lambda j: (0, 0, j)), w_in, w_in, whole((tokens, d)), whole((tokens, d)), HBM, HBM, HBM],
-        out_specs=[whole((tokens, d)), HBM, HBM, whole((DOWN_WINDOW, down_cols))],
-        out_shape=[jax.ShapeDtypeStruct((tokens, d), BF16)]
-        + [jax.ShapeDtypeStruct(s, BF16) for s in half_sums(GATE_ROWS, ff)]
-        + [jax.ShapeDtypeStruct((DOWN_WINDOW, down_cols), BF16)],
+        in_specs=[spec((2, tokens, TILE), lambda j: (0, 0, j)), w_in, w_in, whole((tokens, d)), whole((tokens, d))] + [HBM] * 4,
+        out_specs=[whole((tokens, d)), *[whole(s) for s in sums]],
+        out_shape=[jax.ShapeDtypeStruct(s, BF16) for s in ((tokens, d), *sums)],
         scratch_shapes=[pltpu.VMEM((tokens, d), F32)] * 2
-        + First.scratch(GATE_ROWS, ff)
-        + [pltpu.VMEM(s, BF16) for s in half_sums(DOWN_WINDOW, down_cols)]
+        + [pltpu.VMEM(t.shape, BF16) for t in halves]
         + Rest.scratch(DOWN_WINDOW, down_cols)
-        + [dma((3,)), dma((2,))],
+        + StreamRest.scratch(tiles)
+        + [dma((4,))],
         compiler_params=params(collective_id),
-    )(dgu, wg, wu, h, dy, sum_gu.reshape(SIDE, SIDE, SIDE, GATE_ROWS, ff), *down_halves)
-
-
-def back_kernel(tiles, gate_cols, dh, gate, up, wd, gate0, gate1, dgu, out, out_gu, p, *rest):
+    )(dgu, wg, wu, h, dy, *halves)
+
+
+def back_kernel(tiles, dh, gate, up, wd, dgu, out, p, *rest):
     j = pl.program_id(0)
     place = Place()
-    pair = PairSum(place, tiles, *rest[:4])
-    before = rest[4:6]
-    sums = Rest.of(place, GATE_ROWS, gate_cols, before, rest[6:14])
-    loads = copies((gate0, gate1), before, rest[14])
-
-    @pl.when(j == 0)
-    def _():
-        signal_all(near(place))
-        begin(loads)
+    pair = PairSum(place, tiles, *rest)
+    pl.when(j == 0)(lambda: signal_all([place.partner()]))
 
     @pl.when(j < tiles)
     def _():
@@ -919,96 +1137,24 @@
             p[slot, r, :], dgu[0, r, :], dgu[1, r, :] = hidden_back(gate[r, :], up[r, :], dp)
 
     down_gradient(j, tiles, pair, p, dh, dh.shape[1] // 2, out)
-    pl.when(j == 0)(lambda: end(loads))
-    sums.tick(j)
-    pl.when(j == 7)(lambda: sums.result(out_gu))
-    pl.when(j == tiles)(sums.drain)
-
-
-def back_call(collective_id, dh, gate, up, wd, gate_halves):
+
+
+def back_call(collective_id, dh, gate, up, wd):
     tokens, d = dh.shape
     ff = gate.shape[1]
-    tiles, half, dma = ff // TILE, d // 2, pltpu.SemaphoreType.DMA
+    tiles, half = ff // TILE, d // 2
     now, before = clip(tiles), clip(tiles, 1)
     tile = spec((tokens, TILE), lambda j: (0, now(j)))
     return pl.pallas_call(
-        functools.partial(back_kernel, tiles, ff),
+        functools.partial(back_kernel, tiles),
         name="back_0",
         grid=(tiles + 1,),
-        in_specs=[whole((tokens, d)), tile, tile, spec((1, TILE, d), lambda j: (0, now(j), 0)), HBM, HBM],
-        out_specs=[spec((2, tokens, TILE), lambda j: (0, 0, now(j))), spec((TILE, half), lambda j: (before(j), 0)), whole((GATE_ROWS, ff))],
-        out_shape=[
-            jax.ShapeDtypeStruct((2, tokens, ff), BF16),
-            jax.ShapeDtypeStruct((ff, half), BF16),
-            jax.ShapeDtypeStruct((GATE_ROWS, ff), BF16),
-        ],
-        scratch_shapes=[pltpu.VMEM((2, tokens, TILE), BF16), *PairSum.scratch(tiles, TILE, half)]
-        + [pltpu.VMEM(s, BF16) for s in half_sums(GATE_ROWS, ff)]
-        + Rest.scratch(GATE_ROWS, ff)
-        + [dma((2,))],
+        in_specs=[whole((tokens, d)), tile, tile, spec((1, TILE, d), lambda j: (0, now(j), 0))],
+        out_specs=[spec((2, tokens, TILE), lambda j: (0, 0, now(j))), spec((TILE, half), lambda j: (before(j), 0))],
+        out_shape=[jax.ShapeDtypeStruct((2, tokens, ff), BF16), jax.ShapeDtypeStruct((ff, half), BF16)],
+        scratch_shapes=[pltpu.VMEM((2, tokens, TILE), BF16), *PairSum.scratch(tiles, TILE, half)],
         compiler_params=params(collective_id),
-    )(dh, gate, up, wd, *gate_halves)
-
-
-def last_kernel(gate_cols, down_cols, sum_gu, down0, down1, out_gu, out_down, *rest):
-    place = Place()
-    first = First.of(place, GATE_ROWS, gate_cols, rest[:5])
-    gu = Rest.of(place, GATE_ROWS, gate_cols, first.results(), rest[5:13])
-    before = rest[13:15]
-    down = Rest.of(place, DOWN_WINDOW, down_cols, before, rest[15:23])
-    load_sem = rest[23]
-    gate_loads = [pltpu.make_async_copy(sum_gu.at[x], first.held.at[x], load_sem.at[x]) for x in range(SIDE)]
-    down_loads = [pltpu.make_async_copy(s, t, load_sem.at[SIDE + i]) for i, (s, t) in enumerate(zip((down0, down1), before, strict=True))]
-    begin(gate_loads + down_loads)
-    signal_all(near(place))
-    end(gate_loads)
-    for k in range(SIDE):
-        first.start(k)
-    end(down_loads)
-    down.start(1)
-
-    def phase0(n, _):
-        lax.fori_loop(0, SIDE, lambda k, _: (first.step(n, k), 0)[1], 0)
-        down.step1(n)
-        return 0
-
-    lax.fori_loop(1, 4, phase0, 0)
-    gu.start(1)
-    down.start(2)
-
-    def phase1(n, _):
-        gu.step1(n)
-        down.step2(n)
-        return 0
-
-    lax.fori_loop(1, 4, phase1, 0)
-    gu.start(2)
-    down.result(out_down)
-    lax.fori_loop(1, 4, lambda n, _: (gu.step2(n), 0)[1], 0)
-    gu.result(out_gu)
-    first.drain()
-    gu.drain()
-    down.drain()
-
-
-def last_call(collective_id, sum_gu, down_halves, down_cols):
-    ff = sum_gu.shape[1]
-    vmem = pl.BlockSpec(memory_space=pltpu.VMEM)
-    return pl.pallas_call(
-        functools.partial(last_kernel, ff, down_cols),
-        name="last_sums",
-        in_specs=[HBM] * 3,
-        out_specs=[vmem] * 2,
-        out_shape=[jax.ShapeDtypeStruct((GATE_ROWS, ff), BF16), jax.ShapeDtypeStruct((DOWN_WINDOW, down_cols), BF16)],
-        scratch_shapes=[
-            *First.scratch(GATE_ROWS, ff),
-            *Rest.scratch(GATE_ROWS, ff),
-            *[pltpu.VMEM(s, BF16) for s in half_sums(DOWN_WINDOW, down_cols)],
-            *Rest.scratch(DOWN_WINDOW, down_cols),
-            pltpu.SemaphoreType.DMA((SIDE + 2,)),
-        ],
-        compiler_params=pltpu.CompilerParams(collective_id=collective_id, has_side_effects=True, vmem_limit_bytes=VMEM_LIMIT),
-    )(sum_gu.reshape(SIDE, SIDE, SIDE, GATE_ROWS, ff), *down_halves)
+    )(dh, gate, up, wd)
 
 
 def flat(m):
@@ -1030,12 +1176,10 @@
         windows = (SIDE, SIDE, 4 * 66, d // 2)
         gate0, up0, h1, a1, a0t = forward_call(x, wg, wu, wd)
         dgu1, a1t, down1 = layer_call(1, a1, dy, wg, wu, wd)
-        gu1, *down1_halves = gate_up_call("gate_up_1", 2, a1t, dgu1, down1.reshape(windows))
-        dh1, *rest = middle_call(3, dgu1, wg, wu, h1, dy, gu1, down1_halves)
-        gu1_halves, sum_down1 = rest[:2], rest[2]
-        dgu0, down0, sum_gu1 = back_call(4, dh1, gate0, up0, wd, gu1_halves)
-        gu0, *down0_halves = gate_up_call("gate_up_0", 5, a0t, dgu0, down0.reshape(windows))
-        sum_gu0, sum_down0 = last_call(6, gu0, down0_halves, d // 2)
+        halves = gate_up_call("gate_up_1", 2, 1, a1t, dgu1, down1.reshape(windows))
+        dh1, sum_down1, sum_gu1 = middle_call(3, dgu1, wg, wu, h1, dy, halves)
+        dgu0, down0 = back_call(4, dh1, gate0, up0, wd)
+        sum_gu0, sum_down0 = gate_up_call("gate_up_0", 5, 3, a0t, dgu0, down0.reshape(windows))
 
         views = [(2, SIDE, SIDE, SIDE, GATE_ROWS, ff)] * 2 + [(2, SIDE, SIDE, 4 * 66, d)]
         w = [t.reshape(view) for t, view in zip((wg, wu, wd), views, strict=True)]

time: 716 us -> 706 us (0.986); the launches traced: 707 us -> 706 us
    pallas_call x5 -> x4, Pallas kernels: 307 us -> 303 us  [the longest x2 188 us: gate_up_call(): pl.pallas_call(functools.partial(gate_up_kernel, tiles, phases, cols), na...]
where the time goes in v3:
time: 706 us
  Pallas kernels  645 us (91%)
  local copies, waits for them, and re-layouts  60.3 us (9%)
    pallas_call x2, Pallas kernels, gate_up_call(): pl.pallas_call(functools.partial(gate_up_kernel, tiles, phases, cols), na...  188 us
    pallas_call x1, Pallas kernels, finish_call(): pl.pallas_call(functools.partial(finish_kernel, count), name='finish', ou...  180 us
    pallas_call x1, Pallas kernels, layer_call(): pl.pallas_call(functools.partial(layer_kernel, tiles), name='layer_1', gr...  87 us
    pallas_call x1, Pallas kernels, forward_call(): pl.pallas_call(functools.partial(forward_kernel, tiles), name='forward_0'...  74 us
    pallas_call x1, Pallas kernels, middle_call(): pl.pallas_call(functools.partial(middle_kernel, tiles, down_cols), name='...  66.2 us
    unnamed x35, local copies, waits for them, and re-layouts  60.3 us
    pallas_call x1, Pallas kernels, back_call(): pl.pallas_call(functools.partial(back_kernel, tiles), name='back_0', grid...  49.5 us

profile of v3, /device:TPU:1, one launch (start us, length us, event | category | flops | bytes accessed | tf_op | source)
XLA Modules:
  0.0 706.1 jit_solution(8543948037503540621)
XLA Ops:
  0.6 74.0 %forward_0.1 = (f32[1024,4224]{1,0:T(8,128)}, f32[1024,4224]{1,0:T(8,128)}, bf16[1024,1536]{1,0:T(8,128)(2,1)}, bf16[1024,1536]{1,0:T(8,128)(2,1)}, bf16[1536,1024]{1,0:T(8,128)(2,1)}) custom-call(bf16[1024,1536]{1,0:T(8,128)(2,1)} %bitcast.106, bf16[2,1536,4224]{2,1,0:T(8,128)(2,1)} %wg.5, bf16[2,1536,4224]{2,1,0:T(8,128)(2,1)} %wu.5, bf16[2,4224,1536]{2,1,0:T(8,128)(2,1)} %wd.5), custom_call_target="tpu_custom_call" | custom-call | tf_op jit(solution)/shard_map/forward_0/pallas_call | solution.py:655
  74.6 87.0 %layer_1.1 = (bf16[2,1024,4224]{2,1,0:T(8,128)(2,1)}, bf16[1536,1024]{1,0:T(8,128)(2,1)}, bf16[4224,768]{1,0:T(8,128)(2,1)}) custom-call(bf16[1024,1536]{1,0:T(8,128)(2,1)} %get-tuple-element.38.a, bf16[1024,1536]{1,0:T(8,128)(2,1)} %bitcast.102, bf16[2,1536,4224]{2,1,0:T(8,128)(2,1)} %wg.5, bf16[2,1536,4224]{2,1,0:T(8,128)(2,1)} %wu.5, ...), custom_call_target="tpu_custom_call" | custom-call | tf_op jit(solution)/shard_map/layer_1/pallas_call | solution.py:749
  161.6 83.6 %gate_up_1.1 = (bf16[3,4,4,24,384]{4,3,2,1,0:T(8,128)(2,1)}, bf16[3,4,4,24,384]{4,3,2,1,0:T(8,128)(2,1)}, bf16[3,11,4,4,8,256]{5,4,3,2,1,0:T(8,128)(2,1)}, bf16[3,11,4,4,8,128]{5,4,3,2,1,0:T(8,128)(2,1)}) custom-call(bf16[1536,1024]{1,0:T(8,128)(2,1)} %get-tuple-element.41.at, bf16[2,1024,4224]{2,1,0:T(8,128)(2,1)} %get-tuple-element.39.ahead.behind.dgu, ...), custom_call_target="tpu_custom_call" | custom-call | tf_op jit(solution)/shard_map/gate_up_1/pallas_call | solution.py:1036
  245.3 66.2 %middle.1 = (bf16[1024,1536]{1,0:T(8,128)(2,1)}, bf16[72,768]{1,0:T(8,128)(2,1)}, bf16[24,4224]{1,0:T(8,128)(2,1)}) custom-call(bf16[2,1024,4224]{2,1,0:T(8,128)(2,1)} %get-tuple-element.39.ahead.behind.dgu, bf16[2,1536,4224]{2,1,0:T(8,128)(2,1)} %wg.5, bf16[2,1536,4224]{2,1,0:T(8,128)(2,1)} %wu.5, bf16[1024,1536]{1,0:T(8,128)(2,1)} %get-tuple-element.40.h, ...), custom_call_target="tpu_custom_call" | custom-call | tf_op jit(solution)/shard_map/middle/pallas_call | solution.py:1109
  311.5 49.5 %back_0.1 = (bf16[2,1024,4224]{2,1,0:T(8,128)(2,1)}, bf16[4224,768]{1,0:T(8,128)(2,1)}) custom-call(bf16[1024,1536]{1,0:T(8,128)(2,1)} %get-tuple-element.47.dh, f32[1024,4224]{1,0:T(8,128)} %get-tuple-element.48.gate, f32[1024,4224]{1,0:T(8,128)} %get-tuple-element.49.up, bf16[2,4224,1536]{2,1,0:T(8,128)(2,1)} %wd.5), custom_call_target="tpu_custom_call" | custom-call | tf_op jit(solution)/shard_map/back_0/pallas_call | solution.py:1148
  361.0 104.1 %gate_up_0.1 = (bf16[24,4224]{1,0:T(8,128)(2,1)}, bf16[72,768]{1,0:T(8,128)(2,1)}) custom-call(bf16[1536,1024]{1,0:T(8,128)(2,1)} %get-tuple-element.37.at, bf16[2,1024,4224]{2,1,0:T(8,128)(2,1)} %get-tuple-element.50.ahead.behind, bf16[2,1024,4224]{2,1,0:T(8,128)(2,1)} %get-tuple-element.50.ahead.behind, bf16[4,4,264,768]{3,2,1,0:T(8,128)(2,1)} %bitcast.105), custom_call_target="tpu_custom_call" | custom-call | tf_op jit(solution)/shard_map/gate_up_0/pallas_call | solution.py:1036
  465.1 180.5 %finish.1 = (bf16[2,4,4,4,24,4224]{5,4,3,2,1,0:T(8,128)(2,1)}, bf16[2,4,4,4,24,4224]{5,4,3,2,1,0:T(8,128)(2,1)}, bf16[2,4,4,264,1536]{4,3,2,1,0:T(8,128)(2,1)}, ...) custom-call(bf16[24,4224]{1,0:T(8,128)(2,1)} %get-tuple-element.52.r, ...), custom_call_target="tpu_custom_call" | custom-call | flops 1000000000 | bytes 100000000 | tf_op jit(solution)/shard_map/finish/pallas_call | solution.py:549
  645.6 0.0 slice-start
  645.6 0.0 slice-start.1
  645.6 0.0 slice-start.2
  645.7 0.0 slice-start.3
  645.7 23.9 %copy.29 = bf16[2,1536,4224]{2,1,0:T(8,128)(2,1)} copy(bf16[2,1536,4224]{2,1,0:T(8,128)(2,1)} %bitcast.101) | data formatting | bytes 51904512
  669.5 22.6 %copy.30 = bf16[2,1536,4224]{2,1,0:T(8,128)(2,1)} copy(bf16[2,1536,4224]{2,1,0:T(8,128)(2,1)} %bitcast.100) | data formatting | bytes 51904512
  692.1 0.0 slice-done
  692.1 0.0 slice-done.1
  692.1 0.0 slice-done.2
  692.1 0.0 slice-done.3
  692.2 9.4 %copy.31 = bf16[2,4224,1536]{2,1,0:T(8,128)(2,1)} copy(bf16[2,4224,1536]{2,1,0:T(8,128)(2,1)S(1)} %bitcast.99) | data formatting | bytes 51904512
  701.6 0.8 copy.32
  702.3 0.8 copy.33
  703.1 0.8 copy.34
  703.8 0.8 copy.35
  704.6 0.8 copy.36
  705.3 0.8 copy.37
  (19 shorter events, 0.0 us)
Async XLA Ops:
  645.6 46.5 %slice-start = ((s8[25952256]{0:T(1024)(128)(4,1)}), s8[4194304]{0:T(1024)(128)(4,1)S(1)}, s32[]{:S(2)}) async-start(s8[25952256]{0:T(1024)(128)(4,1)} %bitcast.97), calls=%async_computation | async-start | bytes 8388608
  645.6 46.5 %slice-start.1 = ((s8[25952256]{0:T(1024)(128)(4,1)}), s8[4194304]{0:T(1024)(128)(4,1)S(1)}, s32[]{:S(2)}) async-start(s8[25952256]{0:T(1024)(128)(4,1)} %bitcast.97), calls=%async_computation.1 | async-start | bytes 8388608
  645.6 46.4 %slice-start.2 = ((s8[25952256]{0:T(1024)(128)(4,1)}), s8[4194304]{0:T(1024)(128)(4,1)S(1)}, s32[]{:S(2)}) async-start(s8[25952256]{0:T(1024)(128)(4,1)} %bitcast.97), calls=%async_computation.2 | async-start | bytes 8388608
  645.7 46.4 %slice-start.3 = ((s8[25952256]{0:T(1024)(128)(4,1)}), s8[4194304]{0:T(1024)(128)(4,1)S(1)}, s32[]{:S(2)}) async-start(s8[25952256]{0:T(1024)(128)(4,1)} %bitcast.97), calls=%async_computation.3 | async-start | bytes 8388608
  669.5 22.6 %slice-start.4 = ((s8[25952256]{0:T(1024)(128)(4,1)}), s8[4194304]{0:T(1024)(128)(4,1)S(1)}, s32[]{:S(2)}) async-start(s8[25952256]{0:T(1024)(128)(4,1)} %bitcast.97), calls=%async_computation.4 | async-start | bytes 8388608
  669.5 22.6 %slice-start.5 = ((s8[25952256]{0:T(1024)(128)(4,1)}), s8[4194304]{0:T(1024)(128)(4,1)S(1)}, s32[]{:S(2)}) async-start(s8[25952256]{0:T(1024)(128)(4,1)} %bitcast.97), calls=%async_computation.5 | async-start | bytes 8388608
  669.5 22.6 %slice-start.6 = ((s8[25952256]{0:T(1024)(128)(4,1)}), s8[786432]{0:T(1024)(128)(4,1)S(1)}, s32[]{:S(2)}) async-start(s8[25952256]{0:T(1024)(128)(4,1)} %bitcast.97), calls=%async_computation.6 | async-start | bytes 1572864
  692.1 9.4 %copy-start.5 = (f32[792,128]{1,0:T(8,128)S(1)}, f32[792,128]{1,0:T(8,128)}, u32[]{:S(2)}) copy-start(f32[792,128]{1,0:T(8,128)} %get-tuple-element.59) | copy-start | bytes 1216516
  692.2 10.2 %copy-start.4 = (f32[792,128]{1,0:T(8,128)S(1)}, f32[792,128]{1,0:T(8,128)}, u32[]{:S(2)}) copy-start(f32[792,128]{1,0:T(8,128)} %get-tuple-element.60) | copy-start | bytes 1216516
  692.2 10.9 %copy-start.3 = (f32[792,128]{1,0:T(8,128)S(1)}, f32[792,128]{1,0:T(8,128)}, u32[]{:S(2)}) copy-start(f32[792,128]{1,0:T(8,128)} %get-tuple-element.61) | copy-start | bytes 1216516
  692.2 11.6 %copy-start.2 = (f32[792,128]{1,0:T(8,128)S(1)}, f32[792,128]{1,0:T(8,128)}, u32[]{:S(2)}) copy-start(f32[792,128]{1,0:T(8,128)} %get-tuple-element.62) | copy-start | bytes 1216516
  692.2 12.4 %copy-start.1 = (f32[792,128]{1,0:T(8,128)S(1)}, f32[792,128]{1,0:T(8,128)}, u32[]{:S(2)}) copy-start(f32[792,128]{1,0:T(8,128)} %get-tuple-element.63) | copy-start | bytes 1216516
  692.2 13.1 %copy-start = (f32[792,128]{1,0:T(8,128)S(1)}, f32[792,128]{1,0:T(8,128)}, u32[]{:S(2)}) copy-start(f32[792,128]{1,0:T(8,128)} %get-tuple-element.64) | copy-start | bytes 1216516

commit v4 on v3

--- a/solution.py
+++ b/solution.py
@@ -245,46 +245,52 @@
     @staticmethod
     def scratch(gate_cols, down_cols):
         bufs = [pltpu.VMEM((2, SIDE, SIDE, SIDE, 24, gate_cols), BF16), pltpu.VMEM((2, SIDE, SIDE, SIDE, 72, down_cols), BF16)]
-        return bufs + [pltpu.SemaphoreType.DMA((2, 3, 2, 3, 3))] * 4 + [pltpu.SemaphoreType.DMA((2,))] * 3
+        return bufs + [pltpu.SemaphoreType.DMA((2, 3, 2, 6, 3))] * 4 + [pltpu.SemaphoreType.DMA((2,))] * 3
 
     def part(self, kind, t, way):
         rows, cols = self.bufs[kind].shape[-2:]
         start, width = ways_of(cols)[way]
         return pl.ds(t * (rows // 3), rows // 3), pl.ds(start, width)
 
-    def message(self, kind, l, t, way, phase, n, hops):
+    def behind(self, t, way, axis, hops):
+        return self.place.block(ORDERS[t][axis], way, hops)
+
+    def message(self, kind, l, t, way, line, n, hops):
         order, place = ORDERS[t], self.place
-        v = place.block(order[phase], way, hops)
-        values = [ALL] * phase + [v] + [place.at[axis] for axis in order[phase + 1 :]]
+        if isinstance(line, int) and line == 0:
+            axis, values = order[0], [self.behind(t, way, 0, hops), place.at[order[1]], place.at[order[2]]]
+        elif isinstance(line, int) and line == 1:
+            axis, values = order[1], [ALL, self.behind(t, way, 1, hops), place.at[order[2]]]
+        else:
+            axis, values = order[2], [ALL, self.behind(t, way, 1, line - 2), self.behind(t, way, 2, hops)]
         ref = self.bufs[kind].at[(l, *index(order, values), *self.part(kind, t, way))]
-        key = (l, t, way, phase, n)
-        axis = order[phase]
+        key = (l, t, way, line, n)
         return put(ref, ref, self.sems[2 * kind].at[key], self.sems[2 * kind + 1].at[key], place.device(axis, place.onward(way)))
 
-    def copies(self, kind, l, t, way, v):
+    def copies(self, kind, l, t, way, b, c):
         order = ORDERS[t]
         rows, cols = self.part(kind, t, way)
+        at = index(order, (ALL, b, c))
         if kind == 0:
-            at = (l, *index(order, (ALL, ALL, v)), rows, cols)
-            return [(lambda out, at=at: (self.bufs[0].at[at], out.at[at]))]
+            return [lambda out: (self.bufs[0].at[(l, *at, rows, cols)], out.at[(l, *at, rows, cols)])]
         half = self.bufs[1].shape[-1]
         start, width = ways_of(half)[way]
         columns = pl.ds(pl.multiple_of(self.place.core * half + start, LANES), width)
+        x, y, z = at
 
         def pair(out, z, count):
-            x, y, _ = index(order, (ALL, ALL, v))
             src = self.bufs[1].at[l, x, y, z, pl.ds(24 * t, count), cols]
-            return src, out.at[l, x, y, pl.ds(64 * z + 24 * t, count), columns]
-
-        if order[2] == 2:
-            return [lambda out: pair(out, v, 24)]
-        return [lambda out, z=z: pair(out, z, 16 if t == 2 and z < SIDE - 1 else 24) for z in range(SIDE)]
-
-    def copy_out(self, kind, l, t, way, v):
+            return src, out.at[l, x, y, pl.ds(pl.multiple_of(64 * z + 24 * t, 8), count), columns]
+
+        if t < 2:
+            return [lambda out: pair(out, z, 24)]
+        return [lambda out, z=z: pair(out, z, 16 if z < SIDE - 1 else 24) for z in range(SIDE)]
+
+    def copy_out(self, kind, l, t, way, b, c):
         local, send, recv = self.copy_sems
 
         def both(out):
-            for pair in self.copies(kind, l, t, way, v):
+            for pair in self.copies(kind, l, t, way, b, c):
                 src, dst = pair(out)
                 pltpu.make_async_copy(src, dst, local.at[kind]).start()
                 put(src, dst, send.at[kind], recv.at[kind], self.place.partner()).start()
@@ -302,25 +308,48 @@
         for kind, t, way in self.parts():
             self.message(kind, l, t, way, 0, 0, 0).start()
 
-    def phase(self, phase):
+    def start_third(self, kind, l, t, way, m):
+        self.message(kind, l, t, way, 2 + m, 0, 0).start()
+        self.copy_out(kind, l, t, way, self.behind(t, way, 1, m), self.place.at[ORDERS[t][2]])
+
+    def first_axis(self):
         def step(i, _):
             n, l = 1 + lax.div(i, 2), lax.rem(i, 2)
             for kind, t, way in self.parts():
-                self.message(kind, l, t, way, phase, n - 1, n).wait_recv()
-                pl.when(n < 3)(lambda kind=kind, t=t, way=way: self.message(kind, l, t, way, phase, n, n).start())
-                if phase < 2:
-
-                    @pl.when(n == 3)
-                    def _(kind=kind, t=t, way=way):
-                        self.message(kind, l, t, way, phase + 1, 0, 0).start()
-                        if phase == 1:
-                            self.copy_out(kind, l, t, way, self.place.at[ORDERS[t][2]])
-
-                else:
-                    self.copy_out(kind, l, t, way, self.place.block(ORDERS[t][2], way, n))
+                self.message(kind, l, t, way, 0, n - 1, n).wait_recv()
+                pl.when(n < 3)(lambda kind=kind, t=t, way=way: self.message(kind, l, t, way, 0, n, n).start())
+
+                @pl.when(n == 3)
+                def _(kind=kind, t=t, way=way):
+                    self.message(kind, l, t, way, 1, 0, 0).start()
+                    self.start_third(kind, l, t, way, 0)
+
             return 0
 
         lax.fori_loop(0, 6, step, 0)
+
+    def other_axes(self):
+        def step(i, _):
+            r, l = 1 + lax.div(i, 2), lax.rem(i, 2)
+            for kind, t, way in self.parts():
+
+                @pl.when(r <= 3)
+                def _(kind=kind, t=t, way=way):
+                    self.message(kind, l, t, way, 1, r - 1, r).wait_recv()
+                    pl.when(r < 3)(lambda: self.message(kind, l, t, way, 1, r, r).start())
+                    self.start_third(kind, l, t, way, r)
+
+                def third(m, _, kind=kind, t=t, way=way):
+                    n = r - m
+                    self.message(kind, l, t, way, 2 + m, n - 1, n).wait_recv()
+                    pl.when(n < 3)(lambda: self.message(kind, l, t, way, 2 + m, n, n).start())
+                    self.copy_out(kind, l, t, way, self.behind(t, way, 1, m), self.behind(t, way, 2, n))
+                    return 0
+
+                lax.fori_loop(jnp.maximum(r - 3, 0), jnp.minimum(r, SIDE), third, 0)
+            return 0
+
+        lax.fori_loop(0, 12, step, 0)
 
     def drain(self):
         local, send, recv = self.copy_sems
@@ -334,9 +363,10 @@
 
         def sent(i, _):
             l, n = lax.div(i, 3), lax.rem(i, 3)
-            for phase in range(3):
-                for kind, t, way in self.parts():
-                    self.message(kind, l, t, way, phase, n, n).wait_send()
+            for kind, t, way in self.parts():
+                for line in range(2):
+                    self.message(kind, l, t, way, line, n, n).wait_send()
+                lax.fori_loop(2, 6, lambda line, _: (self.message(kind, l, t, way, line, n, n).wait_send(), 0)[1], 0)
             return 0
 
         lax.fori_loop(0, 6, sent, 0)
@@ -483,7 +513,7 @@
                 gather.bufs[0][l, x, y, z, rows, lanes] = weight(old_gu[l, rows, lanes], step)
             return 0
 
-        lax.fori_loop(0, gate_tiles, gate_up, 0)
+        lax.fori_loop(0, gate_tiles, gate_up, 0, unroll=3)
 
         def down(i, _, l=l):
             rows = pl.ds(pl.multiple_of(8 * i, 8), 8)
@@ -493,12 +523,21 @@
                 g = sums_d[l][rows, lanes].astype(F32) * factor
                 step = moments(moments_d, start + 2 * down_tiles * core, down_stride, g)
                 gather.bufs[1][l, x, y, z, rows, lanes] = weight(old_d[l, rows, lanes], step)
-                g = other_d[l, rows, lanes].astype(F32) * factor
+            return 0
+
+        lax.fori_loop(0, 9, down, 0)
+        gather.own(l)
+    for l in range(2):
+
+        def down_other(i, _, l=l):
+            rows = pl.ds(pl.multiple_of(8 * i, 8), 8)
+            for j in range(down_tiles):
+                start = (PREV + 8 * i) * down_stride + 2 * j + l
+                g = other_d[l, rows, pl.ds(j * LANES, LANES)].astype(F32) * factor
                 moments(moments_d, start + 2 * down_tiles * (1 - core), down_stride, g)
             return 0
 
-        lax.fori_loop(0, 9, down, 0)
-        gather.own(l)
+        lax.fori_loop(0, 9, down_other, 0)
 
     late = []
     for i, out in enumerate((m_out, v_out)):
@@ -510,8 +549,8 @@
                 put(gate_rows(i, 1 - core), out[c], late_send.at[i], late_recv.at[i], partner).start()
 
         pltpu.make_async_copy(down_rows(i, own_rows, DOWN_ROWS), out[2], late_local.at[2 + i]).start()
-    for phase in range(3):
-        gather.phase(phase)
+    gather.first_axis()
+    gather.other_axes()
     for i, out in enumerate((m_out, v_out)):
         pltpu.make_async_copy(gate_rows(i, core), out[0], late_local.at[i]).wait()
         pltpu.make_async_copy(down_rows(i, own_rows, DOWN_ROWS), out[2], late_local.at[2 + i]).wait()
@@ -781,7 +820,7 @@
         third, dma = GATE_ROWS // 3, pltpu.SemaphoreType.DMA
         leads = [(3, 3, tiles, SIDE, SIDE), (3, 3, tiles, SIDE), (3, 3, tiles)][:phases]
         slots = [pltpu.VMEM((*lead, third, width), BF16) for lead in leads for _, width in ways_of(TILE)]
-        return [pltpu.VMEM((RING, SIDE, SIDE, SIDE, GATE_ROWS, TILE), BF16), *slots, dma((tiles, 3 * phases)), dma((tiles, 3 * phases))]
+        return [pltpu.VMEM((RING, SIDE, SIDE, SIDE, GATE_ROWS, TILE), BF16), *slots, dma((tiles, 7)), dma((tiles, 7))]
 
     def part(self, t, way):
         start, width = self.ways[way]
@@ -802,21 +841,29 @@
         elif phase == 0:
             src = self.own(c, t, way, 1)
         else:
-            v = self.place.block(axis, way, 1)
-            at = second(t, v) if phase == 1 else (v,)
-            src = self.slots[2 * phase - 2 + way].at[(t, 2, c, *at)]
+            src = self.slots[way].at[(t, 2, c, *second(t, self.place.block(axis, way, 1)))]
         key = (c, 3 * phase + n)
         return put(src, slots.at[t, n, c], self.send.at[key], self.recv.at[key], self.place.device(axis, self.place.onward(way)))
 
+    def direct(self, t, way, off, c):
+        axis = ORDERS[t][2]
+        v = lax.rem(self.place.at[axis] + off, SIDE)
+        src, dst = self.slots[2 + way].at[t, 2, c, v], self.slots[4 + way].at[t, off - 1, c]
+        return put(src, dst, self.send.at[c, 6], self.recv.at[c, 6], self.place.device(axis, off))
+
     def pairs(self):
         return [(t, way) for t in range(3) for way in range(2)]
 
     def all_of(self, phase):
-        return self.held.at[(0,) * (phase + 2)]
+        return self.held.at[(0,) * (phase + 2)] if phase < 2 else self.held.at[0, 0, 0, pl.ds(0, 3)]
 
     def begin(self, phase, c):
         for t, way in self.pairs():
-            self.copy(phase, t, way, 0, c, first=True).start()
+            if phase < 2:
+                self.copy(phase, t, way, 0, c, first=True).start()
+            else:
+                for off in range(1, SIDE):
+                    self.direct(t, way, off, c).start()
 
     def add(self, phase, t, way, n, c):
         slots = self.slots[2 * phase + way]
@@ -830,47 +877,60 @@
             for b in range(SIDE):
                 for d in range(SIDE):
                     one((b, d), self.own(c, t, way, n + 1, b, d))
-        elif phase == 1:
+        else:
             for d in range(SIDE):
                 one((d,), self.slots[way].at[(t, 2, c, *second(t, v, d))])
-        else:
-            one((), self.slots[2 + way].at[t, 2, c, v])
 
     def stage(self, s, c, out):
         phase, n = (s - 1) // 3, (s - 1) % 3 + 1
-        key = (c, 3 * phase + n - 1)
         whole_stage = self.all_of(phase)
-        pltpu.make_async_copy(whole_stage, whole_stage, self.recv.at[key]).wait()
+        pltpu.make_async_copy(whole_stage, whole_stage, self.recv.at[c, s - 1]).wait()
+        if phase == 2:
+            for t, way in self.pairs():
+                total = self.slots[2 + way][t, 2, c, self.place.at[ORDERS[t][2]]].astype(F32)
+                for i in range(3):
+                    total += self.slots[4 + way][t, i, c].astype(F32)
+                rows, _ = self.part(t, way)
+                start, width = self.ways[way]
+                out[rows, pl.ds(pl.multiple_of(c * TILE + start, LANES), width)] = total.astype(BF16)
+            return
         for t, way in self.pairs():
             self.add(phase, t, way, n, c)
             if n < 3:
                 self.copy(phase, t, way, n, c).start()
         if n == 3 and phase + 1 < self.phases:
             self.begin(phase + 1, c)
-        if n == 3 and phase == 2:
-            for t, way in self.pairs():
-                rows, _ = self.part(t, way)
-                start, width = self.ways[way]
-                out[rows, pl.ds(pl.multiple_of(c * TILE + start, LANES), width)] = self.slots[4 + way][t, 2, c]
 
     def sent(self, phase, n, c):
         whole_stage = self.all_of(phase)
         pltpu.make_async_copy(whole_stage, whole_stage, self.send.at[c, 3 * phase + n]).wait()
 
+    def count(self):
+        return 3 if self.phases == 1 else 7
+
     def keep(self, c):
         pl.when(c >= RING)(lambda: self.sent(0, 0, c - RING))
         return self.held.at[lax.rem(c, RING)]
 
-    def step(self, newest, out=None):
-        valid = lambda c: (c >= 0) & (c < self.tiles)
-        pl.when(valid(newest))(lambda: self.begin(0, newest))
-        for s in range(3 * self.phases, 0, -1):
-            pl.when(valid(newest - s))(lambda s=s: self.stage(s, newest - s, out))
+    def run(self, s, c, out):
+        act = (lambda: self.begin(0, c)) if s == 0 else (lambda: self.stage(s, c, out))
+        pl.when((c >= 0) & (c < self.tiles))(act)
+
+    def early(self, j, out=None):
+        for s in range(self.count(), 1, -1):
+            self.run(s, j - 2 - s, out)
+
+    def late(self, j, out=None):
+        self.run(0, j - 1, out)
+        self.run(1, j - 2, out)
+
+    def last_step(self):
+        return self.tiles - 1 + 2 + self.count()
 
     def drain(self):
         def each(c, _):
             pl.when(c >= self.tiles - RING)(lambda: self.sent(0, 0, c))
-            for i in range(1, 3 * self.phases):
+            for i in range(1, self.count()):
                 self.sent(i // 3, i % 3, c)
             return 0
 
@@ -932,7 +992,8 @@
             lax.fori_loop(0, self.tiles, add, 0)
             pl.when(n < 3)(lambda t=t, way=way: self.message(phase, t, way, n).start())
 
-    def tick(self, i):
+    def tick(self, j):
+        i = jnp.where(j <= 8, jnp.where(lax.rem(j, 2) == 0, lax.div(j, 2), -1), j - 4)
         pl.when(i == 0)(lambda: self.start(1))
         pl.when((i >= 1) & (i <= 3))(lambda: self.step(1, i))
         pl.when(i == 3)(lambda: self.start(2))
@@ -958,23 +1019,28 @@
 BLOCK_ROWS = SIDE * SIDE * GATE_ROWS
 
 
-def gate_up_kernel(tiles, phases, cols, at, ahead, behind, sum_down, *rest):
+def gate_up_kernel(tiles, phases, cols, at, ahead, behind, *rest):
     j = pl.program_id(0)
     place = Place()
     core = place.core
-    outs, rest = (rest[:4], rest[4:]) if phases == 1 else (rest[:2], rest[2:])
+    if phases == 1:
+        outs, out, rest = rest[:2], None, rest[2:]
+    else:
+        sum_down, out, out_down, rest = rest[0], rest[1], rest[2], rest[3:]
     pair = PairSum(place, tiles, *rest[:4])
-    first = First.of(place, DOWN_WINDOW, cols, rest[4:9])
-    stream = Stream(place, tiles, phases, rest[9 : 9 + 3 + 2 * phases])
-    rest = rest[9 + 3 + 2 * phases :]
-    load_sem, save_sem = rest[:2]
-    loads = loads_down(sum_down, first, load_sem)
-    last = tiles + 3 * phases
+    stream = Stream(place, tiles, phases, rest[4 : 4 + 3 + 2 * phases])
+    rest = rest[4 + 3 + 2 * phases :]
+    if phases == 3:
+        first = First.of(place, DOWN_WINDOW, cols, rest[1:6])
+        down = Rest.of(place, DOWN_WINDOW, cols, first.results(), rest[6:14])
+        loads = loads_down(sum_down, first, rest[0])
 
     @pl.when(j == 0)
     def _():
-        signal_all(near(place))
-        begin(loads)
+        opposite = [place.device(axis, 2) for axis in range(3)] if phases == 3 else []
+        signal_all(near(place) + opposite)
+        if phases == 3:
+            begin(loads)
 
     @pl.when(j < tiles)
     def _():
@@ -984,6 +1050,13 @@
             r = pl.ds(m * BLOCK_ROWS, BLOCK_ROWS)
             slot[r, :] = dot(at[r, :], other, NN).astype(BF16)
         pair.copy(j).start()
+
+    stream.early(j, out)
+    if phases == 3:
+        pl.when(j == 0)(lambda: end(loads))
+        pl.when(j < 8)(lambda: spread(j, 8, 16, first.tick))
+        pl.when(j >= 8)(lambda: down.tick(j - 8))
+        pl.when(j == 15)(lambda: down.result(out_down))
 
     @pl.when((j >= 1) & (j <= tiles))
     def _():
@@ -995,75 +1068,58 @@
             total = (dot(at[r, :], own, NN) + pair.landing[j - 1, r, :].astype(F32)).astype(BF16)
             kept[m] = total.reshape(SIDE, SIDE, GATE_ROWS, TILE)
 
-    if phases == 1:
-        stream.step(j - 1)
-    else:
-        stream.step(j - 1, outs[0])
-    pl.when(j == 0)(lambda: end(loads))
-    if phases == 1:
-        pl.when(j <= tiles)(lambda: spread(j, tiles + 1, 16, first.tick))
-    else:
-        down = Rest.of(place, DOWN_WINDOW, cols, first.results(), rest[2:10])
-        pl.when(j < 8)(lambda: spread(j, 8, 16, first.tick))
-        pl.when(j >= 8)(lambda: down.tick(j - 8))
-        pl.when(j == 15)(lambda: down.result(outs[1]))
-
-    @pl.when(j == last)
+    stream.late(j, out)
+
+    @pl.when(j == stream.last_step())
     def _():
         pair.drain()
         if phases == 1:
-            saves = copies([*first.results(), *stream.results()], outs, save_sem)
+            saves = copies(stream.results(), outs, rest[0])
             begin(saves)
-        first.drain()
-        stream.drain()
-        if phases == 1:
+            stream.drain()
             end(saves)
         else:
+            stream.drain()
+            first.drain()
             down.drain()
 
 
-def gate_up_call(name, collective_id, phases, at, dgu, sum_down):
+def gate_up_call(name, collective_id, phases, at, dgu, *sum_down):
     d, tokens = at.shape
     ff = dgu.shape[2]
-    tiles, cols, dma = ff // TILE, sum_down.shape[-1], pltpu.SemaphoreType.DMA
+    tiles, cols, dma = ff // TILE, d // 2, pltpu.SemaphoreType.DMA
     now, before = clip(tiles), clip(tiles, 1)
     if phases == 1:
-        shapes = [*half_sums(DOWN_WINDOW, cols), *stream_halves(tiles)]
-        out_specs, more = [HBM] * 4, []
+        shapes = stream_halves(tiles)
+        out_specs, more = [HBM] * 2, [dma((2,))]
     else:
         shapes = [(GATE_ROWS, ff), (DOWN_WINDOW, cols)]
-        out_specs, more = [whole(s) for s in shapes], Rest.scratch(DOWN_WINDOW, cols)
+        out_specs = [whole(s) for s in shapes]
+        more = [dma((SIDE,)), *First.scratch(DOWN_WINDOW, cols), *Rest.scratch(DOWN_WINDOW, cols)]
     return pl.pallas_call(
         functools.partial(gate_up_kernel, tiles, phases, cols),
         name=name,
-        grid=(tiles + 3 * phases + 1,),
+        grid=(tiles + (5 if phases == 1 else 9),),
         in_specs=[
             whole((d, tokens)),
             spec((2, tokens, TILE), lambda j: (0, 0, now(j))),
             spec((2, tokens, TILE), lambda j: (0, 0, before(j))),
-            HBM,
+            *[HBM] * len(sum_down),
         ],
         out_specs=out_specs,
         out_shape=[jax.ShapeDtypeStruct(s, BF16) for s in shapes],
-        scratch_shapes=[
-            *PairSum.scratch(tiles, d, TILE),
-            *First.scratch(DOWN_WINDOW, cols),
-            *Stream.scratch(tiles, phases),
-            dma((SIDE,)),
-            dma((4,)),
-            *more,
-        ],
+        scratch_shapes=[*PairSum.scratch(tiles, d, TILE), *Stream.scratch(tiles, phases), *more],
         compiler_params=params(collective_id),
-    )(at, dgu, dgu, sum_down)
-
-
-def middle_kernel(tiles, down_cols, dgu, wg, wu, h, dy, down0, down1, gate0, gate1, dh, out_down, out_gu, acc_g, acc_u, *rest):
+    )(at, dgu, dgu, *sum_down)
+
+
+def middle_kernel(tiles, down_cols, dgu, wg, wu, h, dy, sum_down, gate0, gate1, dh, out_gu, half0, half1, acc_g, acc_u, *rest):
     j = pl.program_id(0)
     place = Place()
-    before = rest[:4]
-    down = Rest.of(place, DOWN_WINDOW, down_cols, before[:2], rest[4:12])
-    gate = StreamRest(place, gate0.shape[1], before[2:], rest[12:20])
-    loads = copies((down0, down1, gate0, gate1), before, rest[20])
+    first = First.of(place, DOWN_WINDOW, down_cols, rest[:5])
+    gate = StreamRest(place, gate0.shape[1], rest[5:7], rest[7:15])
+    load_sem, gate_sem, save_sem = rest[15:18]
+    loads = loads_down(sum_down, first, load_sem) + copies((gate0, gate1), rest[5:7], gate_sem)
 
     @pl.when(j == 0)
     def _():
@@ -1078,16 +1134,15 @@
         acc_u[r, :] += dot(dgu[1, r, :], wu[0], NT)
 
     pl.when(j == 0)(lambda: end(loads))
-    down.tick(j)
     gate.tick(j)
-
-    @pl.when(j == 7)
-    def _():
-        down.result(out_down)
-        gate.result(out_gu)
+    spread(j, tiles, 16, first.tick)
 
     @pl.when(j == tiles - 1)
     def _():
+        saves = copies(first.results(), (half0, half1), save_sem)
+        begin(saves)
+        gate.result(out_gu)
+
         def rows(r):
             wide = h[r, :].astype(F32)
             scale = norm_scale(wide)
@@ -1096,37 +1151,45 @@
             dh[r, :] = (dy[r, :].astype(F32) + back.astype(BF16).astype(F32)).astype(BF16)
 
         in_rows(h.shape[0], 64, rows)
-        down.drain()
+        first.drain()
         gate.drain()
-
-
-def middle_call(collective_id, dgu, wg, wu, h, dy, halves):
+        end(saves)
+
+
+def middle_call(collective_id, dgu, wg, wu, h, dy, sum_down, gate_halves):
     tokens, d = h.shape
     ff = dgu.shape[2]
     tiles, dma, down_cols = ff // TILE, pltpu.SemaphoreType.DMA, d // 2
     w_in = spec((1, d, TILE), lambda j: (1, 0, j))
-    sums = [(DOWN_WINDOW, down_cols), (GATE_ROWS, ff)]
     return pl.pallas_call(
         functools.partial(middle_kernel, tiles, down_cols),
         name="middle",
         grid=(tiles,),
-        in_specs=[spec((2, tokens, TILE), lambda j: (0, 0, j)), w_in, w_in, whole((tokens, d)), whole((tokens, d))] + [HBM] * 4,
-        out_specs=[whole((tokens, d)), *[whole(s) for s in sums]],
-        out_shape=[jax.ShapeDtypeStruct(s, BF16) for s in ((tokens, d), *sums)],
+        in_specs=[spec((2, tokens, TILE), lambda j: (0, 0, j)), w_in, w_in, whole((tokens, d)), whole((tokens, d))] + [HBM] * 3,
+        out_specs=[whole((tokens, d)), whole((GATE_ROWS, ff)), HBM, HBM],
+        out_shape=[jax.ShapeDtypeStruct(s, BF16) for s in ((tokens, d), (GATE_ROWS, ff), *half_sums(DOWN_WINDOW, down_cols))],
         scratch_shapes=[pltpu.VMEM((tokens, d), F32)] * 2
-        + [pltpu.VMEM(t.shape, BF16) for t in halves]
-        + Rest.scratch(DOWN_WINDOW, down_cols)
+        + First.scratch(DOWN_WINDOW, down_cols)
+        + [pltpu.VMEM(t.shape, BF16) for t in gate_halves]
         + StreamRest.scratch(tiles)
-        + [dma((4,))],
+        + [dma((SIDE,)), dma((2,)), dma((2,))],
         compiler_params=params(collective_id),
-    )(dgu, wg, wu, h, dy, *halves)
-
-
-def back_kernel(tiles, dh, gate, up, wd, dgu, out, p, *rest):
+    )(dgu, wg, wu, h, dy, sum_down, *gate_halves)
+
+
+def back_kernel(tiles, dh, gate, up, wd, down0, down1, dgu, out, out_down, p, *rest):
     j = pl.program_id(0)
     place = Place()
-    pair = PairSum(place, tiles, *rest)
-    pl.when(j == 0)(lambda: signal_all([place.partner()]))
+    half = dh.shape[1] // 2
+    pair = PairSum(place, tiles, *rest[:4])
+    before = rest[4:6]
+    down = Rest.of(place, DOWN_WINDOW, half, before, rest[6:14])
+    loads = copies((down0, down1), before, rest[14])
+
+    @pl.when(j == 0)
+    def _():
+        signal_all(near(place))
+        begin(loads)
 
     @pl.when(j < tiles)
     def _():
@@ -1136,10 +1199,14 @@
             dp = dot(dh[r, :], wd[0], NT)
             p[slot, r, :], dgu[0, r, :], dgu[1, r, :] = hidden_back(gate[r, :], up[r, :], dp)
 
-    down_gradient(j, tiles, pair, p, dh, dh.shape[1] // 2, out)
-
-
-def back_call(collective_id, dh, gate, up, wd):
+    down_gradient(j, tiles, pair, p, dh, half, out)
+    pl.when(j == 0)(lambda: end(loads))
+    down.tick(j)
+    pl.when(j == 7)(lambda: down.result(out_down))
+    pl.when(j == tiles)(down.drain)
+
+
+def back_call(collective_id, dh, gate, up, wd, down_halves):
     tokens, d = dh.shape
     ff = gate.shape[1]
     tiles, half = ff // TILE, d // 2
@@ -1149,12 +1216,19 @@
         functools.partial(back_kernel, tiles),
         name="back_0",
         grid=(tiles + 1,),
-        in_specs=[whole((tokens, d)), tile, tile, spec((1, TILE, d), lambda j: (0, now(j), 0))],
-        out_specs=[spec((2, tokens, TILE), lambda j: (0, 0, now(j))), spec((TILE, half), lambda j: (before(j), 0))],
-        out_shape=[jax.ShapeDtypeStruct((2, tokens, ff), BF16), jax.ShapeDtypeStruct((ff, half), BF16)],
-        scratch_shapes=[pltpu.VMEM((2, tokens, TILE), BF16), *PairSum.scratch(tiles, TILE, half)],
+        in_specs=[whole((tokens, d)), tile, tile, spec((1, TILE, d), lambda j: (0, now(j), 0)), HBM, HBM],
+        out_specs=[
+            spec((2, tokens, TILE), lambda j: (0, 0, now(j))),
+            spec((TILE, half), lambda j: (before(j), 0)),
+            whole((DOWN_WINDOW, half)),
+        ],
+        out_shape=[jax.ShapeDtypeStruct(s, BF16) for s in ((2, tokens, ff), (ff, half), (DOWN_WINDOW, half))],
+        scratch_shapes=[pltpu.VMEM((2, tokens, TILE), BF16), *PairSum.scratch(tiles, TILE, half)]
+        + [pltpu.VMEM(t.shape, BF16) for t in down_halves]
+        + Rest.scratch(DOWN_WINDOW, half)
+        + [pltpu.SemaphoreType.DMA((2,))],
         compiler_params=params(collective_id),
-    )(dh, gate, up, wd)
+    )(dh, gate, up, wd, *down_halves)
 
 
 def flat(m):
@@ -1176,9 +1250,10 @@
         windows = (SIDE, SIDE, 4 * 66, d // 2)
         gate0, up0, h1, a1, a0t = forward_call(x, wg, wu, wd)
         dgu1, a1t, down1 = layer_call(1, a1, dy, wg, wu, wd)
-        halves = gate_up_call("gate_up_1", 2, 1, a1t, dgu1, down1.reshape(windows))
-        dh1, sum_down1, sum_gu1 = middle_call(3, dgu1, wg, wu, h1, dy, halves)
-        dgu0, down0 = back_call(4, dh1, gate0, up0, wd)
+        down1 = down1.reshape(windows)
+        gate_halves = gate_up_call("gate_up_1", 2, 1, a1t, dgu1)
+        dh1, sum_gu1, *down_halves = middle_call(3, dgu1, wg, wu, h1, dy, down1, gate_halves)
+        dgu0, down0, sum_down1 = back_call(4, dh1, gate0, up0, wd, down_halves)
         sum_gu0, sum_down0 = gate_up_call("gate_up_0", 5, 3, a0t, dgu0, down0.reshape(windows))
 
         views = [(2, SIDE, SIDE, SIDE, GATE_ROWS, ff)] * 2 + [(2, SIDE, SIDE, 4 * 66, d)]

time: 706 us -> 691 us (0.979)
  Pallas kernels: 645 us -> 629 us
    pallas_call x2, Pallas kernels: 188 us -> 168 us  [gate_up_call(): pl.pallas_call(functools.partial(gate_up_kernel, tiles, phases, cols), na...]
where the time goes in v4:
time: 691 us; the launch traced here: 690 us
  Pallas kernels  629 us (91%)
  local copies, waits for them, and re-layouts  60.3 us (9%)
    pallas_call x1, Pallas kernels, finish_call(): pl.pallas_call(functools.partial(finish_kernel, count), name='finish', ou...  182 us
    pallas_call x2, Pallas kernels, gate_up_call(): pl.pallas_call(functools.partial(gate_up_kernel, tiles, phases, cols), na...  168 us
    pallas_call x1, Pallas kernels, layer_call(): pl.pallas_call(functools.partial(layer_kernel, tiles), name='layer_1', gr...  87 us
    pallas_call x1, Pallas kernels, forward_call(): pl.pallas_call(functools.partial(forward_kernel, tiles), name='forward_0'...  74 us
    pallas_call x1, Pallas kernels, middle_call(): pl.pallas_call(functools.partial(middle_kernel, tiles, down_cols), name='...  64.5 us
    unnamed x35, local copies, waits for them, and re-layouts  60.3 us
    pallas_call x1, Pallas kernels, back_call(): pl.pallas_call(functools.partial(back_kernel, tiles), name='back_0', grid...  53.5 us

profile of v4, /device:TPU:1, one launch (start us, length us, event | category | flops | bytes accessed | tf_op | source)
XLA Modules:
  0.0 690.3 jit_solution(13362311947957573563)
XLA Ops:
  0.6 74.0 %forward_0.1 = (f32[1024,4224]{1,0:T(8,128)}, f32[1024,4224]{1,0:T(8,128)}, bf16[1024,1536]{1,0:T(8,128)(2,1)}, bf16[1024,1536]{1,0:T(8,128)(2,1)}, bf16[1536,1024]{1,0:T(8,128)(2,1)}) custom-call(bf16[1024,1536]{1,0:T(8,128)(2,1)} %bitcast.106, bf16[2,1536,4224]{2,1,0:T(8,128)(2,1)} %wg.5, bf16[2,1536,4224]{2,1,0:T(8,128)(2,1)} %wu.5, bf16[2,4224,1536]{2,1,0:T(8,128)(2,1)} %wd.5), custom_call_target="tpu_custom_call" | custom-call | tf_op jit(solution)/shard_map/forward_0/pallas_call | solution.py:694
  74.6 87.0 %layer_1.1 = (bf16[2,1024,4224]{2,1,0:T(8,128)(2,1)}, bf16[1536,1024]{1,0:T(8,128)(2,1)}, bf16[4224,768]{1,0:T(8,128)(2,1)}) custom-call(bf16[1024,1536]{1,0:T(8,128)(2,1)} %get-tuple-element.38.a, bf16[1024,1536]{1,0:T(8,128)(2,1)} %bitcast.102, bf16[2,1536,4224]{2,1,0:T(8,128)(2,1)} %wg.5, bf16[2,1536,4224]{2,1,0:T(8,128)(2,1)} %wu.5, ...), custom_call_target="tpu_custom_call" | custom-call | tf_op jit(solution)/shard_map/layer_1/pallas_call | solution.py:788
  161.6 71.3 %gate_up_1.1 = (bf16[3,11,4,4,8,256]{5,4,3,2,1,0:T(8,128)(2,1)}, bf16[3,11,4,4,8,128]{5,4,3,2,1,0:T(8,128)(2,1)}) custom-call(bf16[1536,1024]{1,0:T(8,128)(2,1)} %get-tuple-element.42.at, bf16[2,1024,4224]{2,1,0:T(8,128)(2,1)} %get-tuple-element.39.ahead.behind.dgu, bf16[2,1024,4224]{2,1,0:T(8,128)(2,1)} %get-tuple-element.39.ahead.behind.dgu), custom_call_target="tpu_custom_call" | custom-call | tf_op jit(solution)/shard_map/gate_up_1/pallas_call | solution.py:1099
  232.9 64.5 %middle.1 = (bf16[1024,1536]{1,0:T(8,128)(2,1)}, bf16[24,4224]{1,0:T(8,128)(2,1)}, bf16[3,4,4,24,384]{4,3,2,1,0:T(8,128)(2,1)}, bf16[3,4,4,24,384]{4,3,2,1,0:T(8,128)(2,1)}) custom-call(bf16[2,1024,4224]{2,1,0:T(8,128)(2,1)} %get-tuple-element.39.ahead.behind.dgu, bf16[2,1536,4224]{2,1,0:T(8,128)(2,1)} %wg.5, bf16[2,1536,4224]{2,1,0:T(8,128)(2,1)} %wu.5, ...), custom_call_target="tpu_custom_call" | custom-call | tf_op jit(solution)/shard_map/middle/pallas_call | solution.py:1164
  297.5 53.5 %back_0.1 = (bf16[2,1024,4224]{2,1,0:T(8,128)(2,1)}, bf16[4224,768]{1,0:T(8,128)(2,1)}, bf16[72,768]{1,0:T(8,128)(2,1)}) custom-call(bf16[1024,1536]{1,0:T(8,128)(2,1)} %get-tuple-element.45.dh, f32[1024,4224]{1,0:T(8,128)} %get-tuple-element.46.gate, f32[1024,4224]{1,0:T(8,128)} %get-tuple-element.47.up, bf16[2,4224,1536]{2,1,0:T(8,128)(2,1)} %wd.5, ...), custom_call_target="tpu_custom_call" | custom-call | tf_op jit(solution)/shard_map/back_0/pallas_call | solution.py:1215
  351.0 96.9 %gate_up_0.1 = (bf16[24,4224]{1,0:T(8,128)(2,1)}, bf16[72,768]{1,0:T(8,128)(2,1)}) custom-call(bf16[1536,1024]{1,0:T(8,128)(2,1)} %get-tuple-element.37.at, bf16[2,1024,4224]{2,1,0:T(8,128)(2,1)} %get-tuple-element.50.ahead.behind, bf16[2,1024,4224]{2,1,0:T(8,128)(2,1)} %get-tuple-element.50.ahead.behind, bf16[4,4,264,768]{3,2,1,0:T(8,128)(2,1)} %bitcast.105), custom_call_target="tpu_custom_call" | custom-call | tf_op jit(solution)/shard_map/gate_up_0/pallas_call | solution.py:1099
  447.9 181.9 %finish.1 = (bf16[2,4,4,4,24,4224]{5,4,3,2,1,0:T(8,128)(2,1)}, bf16[2,4,4,4,24,4224]{5,4,3,2,1,0:T(8,128)(2,1)}, bf16[2,4,4,264,1536]{4,3,2,1,0:T(8,128)(2,1)}, ...) custom-call(bf16[24,4224]{1,0:T(8,128)(2,1)} %get-tuple-element.52.r, ...), custom_call_target="tpu_custom_call" | custom-call | flops 1000000000 | bytes 100000000 | tf_op jit(solution)/shard_map/finish/pallas_call | solution.py:588
  629.8 0.0 slice-start
  629.8 0.0 slice-start.1
  629.8 0.0 slice-start.2
  629.9 0.0 slice-start.3
  629.9 23.9 %copy.29 = bf16[2,1536,4224]{2,1,0:T(8,128)(2,1)} copy(bf16[2,1536,4224]{2,1,0:T(8,128)(2,1)} %bitcast.101) | data formatting | bytes 51904512
  653.7 22.6 %copy.30 = bf16[2,1536,4224]{2,1,0:T(8,128)(2,1)} copy(bf16[2,1536,4224]{2,1,0:T(8,128)(2,1)} %bitcast.100) | data formatting | bytes 51904512
  676.3 0.0 slice-done
  676.3 0.0 slice-done.1
  676.4 9.4 %copy.31 = bf16[2,4224,1536]{2,1,0:T(8,128)(2,1)} copy(bf16[2,4224,1536]{2,1,0:T(8,128)(2,1)S(1)} %bitcast.99) | data formatting | bytes 51904512
  685.8 0.8 copy.32
  686.5 0.8 copy.33
  687.3 0.8 copy.34
  688.0 0.8 copy.35
  688.8 0.0 copy-done.1
  688.8 0.8 copy.36
  689.5 0.0 copy-done
  689.5 0.8 copy.37
  (19 shorter events, 0.0 us)
Async XLA Ops:
  629.8 46.5 %slice-start = ((s8[25952256]{0:T(1024)(128)(4,1)}), s8[4194304]{0:T(1024)(128)(4,1)S(1)}, s32[]{:S(2)}) async-start(s8[25952256]{0:T(1024)(128)(4,1)} %bitcast.97), calls=%async_computation | async-start | bytes 8388608
  629.8 46.5 %slice-start.1 = ((s8[25952256]{0:T(1024)(128)(4,1)}), s8[4194304]{0:T(1024)(128)(4,1)S(1)}, s32[]{:S(2)}) async-start(s8[25952256]{0:T(1024)(128)(4,1)} %bitcast.97), calls=%async_computation.1 | async-start | bytes 8388608
  629.8 46.4 %slice-start.2 = ((s8[25952256]{0:T(1024)(128)(4,1)}), s8[4194304]{0:T(1024)(128)(4,1)S(1)}, s32[]{:S(2)}) async-start(s8[25952256]{0:T(1024)(128)(4,1)} %bitcast.97), calls=%async_computation.2 | async-start | bytes 8388608
  629.9 46.4 %slice-start.3 = ((s8[25952256]{0:T(1024)(128)(4,1)}), s8[4194304]{0:T(1024)(128)(4,1)S(1)}, s32[]{:S(2)}) async-start(s8[25952256]{0:T(1024)(128)(4,1)} %bitcast.97), calls=%async_computation.3 | async-start | bytes 8388608
  653.7 22.6 %slice-start.4 = ((s8[25952256]{0:T(1024)(128)(4,1)}), s8[4194304]{0:T(1024)(128)(4,1)S(1)}, s32[]{:S(2)}) async-start(s8[25952256]{0:T(1024)(128)(4,1)} %bitcast.97), calls=%async_computation.4 | async-start | bytes 8388608
  653.7 22.6 %slice-start.5 = ((s8[25952256]{0:T(1024)(128)(4,1)}), s8[4194304]{0:T(1024)(128)(4,1)S(1)}, s32[]{:S(2)}) async-start(s8[25952256]{0:T(1024)(128)(4,1)} %bitcast.97), calls=%async_computation.5 | async-start | bytes 8388608
  653.7 22.6 %slice-start.6 = ((s8[25952256]{0:T(1024)(128)(4,1)}), s8[786432]{0:T(1024)(128)(4,1)S(1)}, s32[]{:S(2)}) async-start(s8[25952256]{0:T(1024)(128)(4,1)} %bitcast.97), calls=%async_computation.6 | async-start | bytes 1572864
  676.4 9.4 %copy-start.5 = (f32[792,128]{1,0:T(8,128)S(1)}, f32[792,128]{1,0:T(8,128)}, u32[]{:S(2)}) copy-start(f32[792,128]{1,0:T(8,128)} %get-tuple-element.59) | copy-start | bytes 1216516
  676.4 10.2 %copy-start.4 = (f32[792,128]{1,0:T(8,128)S(1)}, f32[792,128]{1,0:T(8,128)}, u32[]{:S(2)}) copy-start(f32[792,128]{1,0:T(8,128)} %get-tuple-element.60) | copy-start | bytes 1216516
  676.4 10.9 %copy-start.3 = (f32[792,128]{1,0:T(8,128)S(1)}, f32[792,128]{1,0:T(8,128)}, u32[]{:S(2)}) copy-start(f32[792,128]{1,0:T(8,128)} %get-tuple-element.61) | copy-start | bytes 1216516
  676.4 11.6 %copy-start.2 = (f32[792,128]{1,0:T(8,128)S(1)}, f32[792,128]{1,0:T(8,128)}, u32[]{:S(2)}) copy-start(f32[792,128]{1,0:T(8,128)} %get-tuple-element.62) | copy-start | bytes 1216516
  676.4 12.4 %copy-start.1 = (f32[792,128]{1,0:T(8,128)S(1)}, f32[792,128]{1,0:T(8,128)}, u32[]{:S(2)}) copy-start(f32[792,128]{1,0:T(8,128)} %get-tuple-element.63) | copy-start | bytes 1216516
  676.4 13.1 %copy-start = (f32[792,128]{1,0:T(8,128)S(1)}, f32[792,128]{1,0:T(8,128)}, u32[]{:S(2)}) copy-start(f32[792,128]{1,0:T(8,128)} %get-tuple-element.64) | copy-start | bytes 1216516

commit v5 on v4

--- a/solution.py
+++ b/solution.py
@@ -653,7 +653,11 @@
     pl.when(j == last)(lambda: piece(last + 1))
 
 
-def forward_kernel(tiles, x, wg, wu, wd, gate, up, h_out, a_out, at, a, acc):
+def side_by_side(a, b):
+    return jnp.concatenate([a, b], axis=1)
+
+
+def forward_kernel(tiles, x, wg, wu, wd, gate, up, h_out, a_out, at, a, acc, p):
     j = pl.program_id(0)
 
     @pl.when(j == 0)
@@ -662,28 +666,40 @@
             wide = x[r, :].astype(F32)
             a[r, :] = (wide * norm_scale(wide)).astype(BF16)
 
-        in_rows(x.shape[0], 128, rows)
+        in_rows(x.shape[0], 32, rows)
         clear(acc)
 
     transpose_piece(j, tiles - 1, a, at)
+    both = side_by_side(wg[0], wu[0])
+    slot = lax.rem(j, 2)
     for m in range(x.shape[0] // ROWS):
         r = pl.ds(m * ROWS, ROWS)
-        g = dot(a[r, :], wg[0], NN)
-        u = dot(a[r, :], wu[0], NN)
+        gu = dot(a[r, :], both, NN)
+        g, u = gu[:, :TILE], gu[:, TILE:]
         gate[r, :] = g
         up[r, :] = u
-        p = (g * lax.logistic(g) * u).astype(BF16)
-        acc[r, :] += dot(p, wd[0], NN)
+        p[slot, r, :] = (g * lax.logistic(g) * u).astype(BF16)
+
+    @pl.when(slot == 1)
+    def _():
+        for m in range(x.shape[0] // ROWS):
+            r = pl.ds(m * ROWS, ROWS)
+            acc[r, :] += dot(side_by_side(p[0, r, :], p[1, r, :]), wd[0], NN)
 
     @pl.when(j == tiles - 1)
     def _():
+        def last_down(r):
+            acc[r, :] += dot(p[0, r, :], wd[0, pl.ds(0, TILE), :], NN)
+
+        in_rows(x.shape[0], ROWS, last_down)
+
         def rows(r):
             h = (x[r, :].astype(F32) + acc[r, :].astype(BF16).astype(F32)).astype(BF16)
             h_out[r, :] = h
             wide = h.astype(F32)
             a_out[r, :] = (wide * norm_scale(wide)).astype(BF16)
 
-        in_rows(x.shape[0], 128, rows)
+        in_rows(x.shape[0], 32, rows)
 
 
 def forward_call(x, wg, wu, wd):
@@ -695,12 +711,12 @@
         functools.partial(forward_kernel, tiles),
         name="forward_0",
         grid=(tiles,),
-        in_specs=[whole((tokens, d)), w_in, w_in, spec((1, TILE, d), lambda j: (0, j, 0))],
+        in_specs=[whole((tokens, d)), w_in, w_in, spec((1, 2 * TILE, d), lambda j: (0, lax.div(j, 2), 0))],
         out_specs=[spec((tokens, TILE), lambda j: (0, j))] * 2 + [whole((tokens, d))] * 2 + [whole((d, tokens))],
         out_shape=[jax.ShapeDtypeStruct((tokens, ff), F32)] * 2
         + [jax.ShapeDtypeStruct((tokens, d), BF16)] * 2
         + [jax.ShapeDtypeStruct((d, tokens), BF16)],
-        scratch_shapes=[pltpu.VMEM((tokens, d), BF16), pltpu.VMEM((tokens, d), F32)],
+        scratch_shapes=[pltpu.VMEM((tokens, d), BF16), pltpu.VMEM((tokens, d), F32), pltpu.VMEM((2, tokens, TILE), BF16)],
         compiler_params=params(),
     )(x, wg, wu, wd)
 
@@ -728,7 +744,7 @@
 
 
 def hidden_back(gate, up, dp):
-    dp = dp.astype(BF16).astype(F32)
+    dp = dp.astype(F32)
     s = lax.logistic(gate)
     act = gate * s
     return (act * up).astype(BF16), (dp * up * (s + act * (1.0 - s))).astype(BF16), (dp * act).astype(BF16)
@@ -755,24 +771,41 @@
     pl.when(j == tiles)(pair.drain)
 
 
-def layer_kernel(tiles, a, dy, wg, wu, wd, dgu, at, out, p, *rest):
+def layer_kernel(tiles, a, dy, wg, wu, wd, dgu, at, out, p, dps, *rest):
     j = pl.program_id(0)
     place = Place()
     pair = PairSum(place, tiles, *rest)
     pl.when(j == 0)(lambda: signal_all([place.partner()]))
+    two_tiles_of_dp(j, tiles, dy, wd, dps)
 
     @pl.when(j < tiles)
     def _():
         transpose_piece(j, tiles - 1, a, at)
         slot = lax.rem(j, 2)
+        both = side_by_side(wg[0], wu[0])
         for m in range(a.shape[0] // ROWS):
             r = pl.ds(m * ROWS, ROWS)
-            g = dot(a[r, :], wg[0], NN)
-            u = dot(a[r, :], wu[0], NN)
-            dp = dot(dy[r, :], wd[0], NT)
-            p[slot, r, :], dgu[0, r, :], dgu[1, r, :] = hidden_back(g, u, dp)
+            gu = dot(a[r, :], both, NN)
+            p[slot, r, :], dgu[0, r, :], dgu[1, r, :] = hidden_back(gu[:, :TILE], gu[:, TILE:], dps[slot, r, :])
 
     down_gradient(j, tiles, pair, p, dy, dy.shape[1] // 2, out)
+
+
+def two_tiles_of_dp(j, tiles, dy, wd, dps):
+    @pl.when((lax.rem(j, 2) == 0) & (j < tiles - 1))
+    def _():
+        for m in range(dy.shape[0] // ROWS):
+            r = pl.ds(m * ROWS, ROWS)
+            dp = dot(dy[r, :], wd[0], NT).astype(BF16)
+            dps[0, r, :] = dp[:, :TILE]
+            dps[1, r, :] = dp[:, TILE:]
+
+    @pl.when(j == tiles - 1)
+    def _():
+        def one_tile(r):
+            dps[0, r, :] = dot(dy[r, :], wd[0, pl.ds(0, TILE), :], NT).astype(BF16)
+
+        in_rows(dy.shape[0], ROWS, one_tile)
 
 
 def clip(tiles, back=0):
@@ -789,14 +822,14 @@
         functools.partial(layer_kernel, tiles),
         name="layer_1",
         grid=(tiles + 1,),
-        in_specs=[whole((tokens, d))] * 2 + [w_in, w_in, spec((1, TILE, d), lambda j: (1, now(j), 0))],
+        in_specs=[whole((tokens, d))] * 2 + [w_in, w_in, spec((1, 2 * TILE, d), lambda j: (1, lax.div(now(j), 2), 0))],
         out_specs=[spec((2, tokens, TILE), lambda j: (0, 0, now(j))), whole((d, tokens)), spec((TILE, half), lambda j: (before(j), 0))],
         out_shape=[
             jax.ShapeDtypeStruct((2, tokens, ff), BF16),
             jax.ShapeDtypeStruct((d, tokens), BF16),
             jax.ShapeDtypeStruct((ff, half), BF16),
         ],
-        scratch_shapes=[pltpu.VMEM((2, tokens, TILE), BF16), *PairSum.scratch(tiles, TILE, half)],
+        scratch_shapes=[pltpu.VMEM((2, tokens, TILE), BF16)] * 2 + PairSum.scratch(tiles, TILE, half),
         compiler_params=params(collective_id),
     )(a, dy, wg, wu, wd)
 
@@ -910,7 +943,7 @@
 
     def keep(self, c):
         pl.when(c >= RING)(lambda: self.sent(0, 0, c - RING))
-        return self.held.at[lax.rem(c, RING)]
+        return self.held.at[lax.rem(c + RING, RING)]
 
     def run(self, s, c, out):
         act = (lambda: self.begin(0, c)) if s == 0 else (lambda: self.stage(s, c, out))
@@ -918,14 +951,14 @@
 
     def early(self, j, out=None):
         for s in range(self.count(), 1, -1):
-            self.run(s, j - 2 - s, out)
+            self.run(s, j - 3 - s, out)
 
     def late(self, j, out=None):
-        self.run(0, j - 1, out)
-        self.run(1, j - 2, out)
+        self.run(0, j - 2, out)
+        self.run(1, j - 3, out)
 
     def last_step(self):
-        return self.tiles - 1 + 2 + self.count()
+        return self.tiles - 1 + 3 + self.count()
 
     def drain(self):
         def each(c, _):
@@ -992,8 +1025,7 @@
             lax.fori_loop(0, self.tiles, add, 0)
             pl.when(n < 3)(lambda t=t, way=way: self.message(phase, t, way, n).start())
 
-    def tick(self, j):
-        i = jnp.where(j <= 8, jnp.where(lax.rem(j, 2) == 0, lax.div(j, 2), -1), j - 4)
+    def tick(self, i):
         pl.when(i == 0)(lambda: self.start(1))
         pl.when((i >= 1) & (i <= 3))(lambda: self.step(1, i))
         pl.when(i == 3)(lambda: self.start(2))
@@ -1042,37 +1074,32 @@
         if phases == 3:
             begin(loads)
 
-    @pl.when(j < tiles)
-    def _():
-        slot = pair.reserve(j)
-        other = ahead[1 - core]
+    stream.early(j, out)
+
+    pl.when((j >= 2) & (j <= tiles + 1))(lambda: pair.copy(j - 2).wait_recv())
+
+    @pl.when(j <= tiles + 1)
+    def _():
+        slot, kept = pair.reserve(j), stream.keep(j - 2)
+        both = side_by_side(ahead[1 - core], behind[core])
+        landed = lax.rem(j + tiles - 2, tiles)
         for m in range(SIDE):
             r = pl.ds(m * BLOCK_ROWS, BLOCK_ROWS)
-            slot[r, :] = dot(at[r, :], other, NN).astype(BF16)
-        pair.copy(j).start()
-
-    stream.early(j, out)
+            tile = dot(at[r, :], both, NN)
+            slot[r, :] = tile[:, :TILE].astype(BF16)
+            total = (tile[:, TILE:] + pair.landing[landed, r, :].astype(F32)).astype(BF16)
+            kept[m] = total.reshape(SIDE, SIDE, GATE_ROWS, TILE)
+
+    pl.when(j < tiles)(lambda: pair.copy(j).start())
+    stream.late(j, out)
     if phases == 3:
         pl.when(j == 0)(lambda: end(loads))
         pl.when(j < 8)(lambda: spread(j, 8, 16, first.tick))
         pl.when(j >= 8)(lambda: down.tick(j - 8))
         pl.when(j == 15)(lambda: down.result(out_down))
 
-    @pl.when((j >= 1) & (j <= tiles))
-    def _():
-        pair.copy(j - 1).wait_recv()
-        own = behind[core]
-        kept = stream.keep(j - 1)
-        for m in range(SIDE):
-            r = pl.ds(m * BLOCK_ROWS, BLOCK_ROWS)
-            total = (dot(at[r, :], own, NN) + pair.landing[j - 1, r, :].astype(F32)).astype(BF16)
-            kept[m] = total.reshape(SIDE, SIDE, GATE_ROWS, TILE)
-
-    stream.late(j, out)
-
     @pl.when(j == stream.last_step())
     def _():
-        pair.drain()
         if phases == 1:
             saves = copies(stream.results(), outs, rest[0])
             begin(saves)
@@ -1088,7 +1115,7 @@
     d, tokens = at.shape
     ff = dgu.shape[2]
     tiles, cols, dma = ff // TILE, d // 2, pltpu.SemaphoreType.DMA
-    now, before = clip(tiles), clip(tiles, 1)
+    now, before = clip(tiles), clip(tiles, 2)
     if phases == 1:
         shapes = stream_halves(tiles)
         out_specs, more = [HBM] * 2, [dma((2,))]
@@ -1099,7 +1126,7 @@
     return pl.pallas_call(
         functools.partial(gate_up_kernel, tiles, phases, cols),
         name=name,
-        grid=(tiles + (5 if phases == 1 else 9),),
+        grid=(tiles + (6 if phases == 1 else 10),),
         in_specs=[
             whole((d, tokens)),
             spec((2, tokens, TILE), lambda j: (0, 0, now(j))),
@@ -1113,7 +1140,7 @@
     )(at, dgu, dgu, *sum_down)
 
 
-def middle_kernel(tiles, down_cols, dgu, wg, wu, h, dy, sum_down, gate0, gate1, dh, out_gu, half0, half1, acc_g, acc_u, *rest):
+def middle_kernel(steps, down_cols, dgu, wg, wu, h, dy, sum_down, gate0, gate1, dh, out_gu, half0, half1, acc_g, acc_u, *rest):
     j = pl.program_id(0)
     place = Place()
     first = First.of(place, DOWN_WINDOW, down_cols, rest[:5])
@@ -1128,17 +1155,24 @@
         clear(acc_g)
         clear(acc_u)
 
-    for m in range(h.shape[0] // ROWS):
-        r = pl.ds(m * ROWS, ROWS)
-        acc_g[r, :] += dot(dgu[0, r, :], wg[0], NT)
-        acc_u[r, :] += dot(dgu[1, r, :], wu[0], NT)
+    def add_up(r, k):
+        acc_g[r, :] += dot(dgu[0, r, pl.ds(0, k)], wg[0, :, pl.ds(0, k)], NT)
+        acc_u[r, :] += dot(dgu[1, r, pl.ds(0, k)], wu[0, :, pl.ds(0, k)], NT)
+
+    @pl.when(j < steps - 1)
+    def _():
+        for m in range(h.shape[0] // ROWS):
+            add_up(pl.ds(m * ROWS, ROWS), 2 * TILE)
+
+    pl.when(j == steps - 1)(lambda: in_rows(h.shape[0], ROWS, lambda r: add_up(r, TILE)))
 
     pl.when(j == 0)(lambda: end(loads))
     gate.tick(j)
-    spread(j, tiles, 16, first.tick)
-
-    @pl.when(j == tiles - 1)
-    def _():
+    spread(j, steps, 16, first.tick)
+
+    @pl.when(j == steps - 1)
+    def _():
+        lax.fori_loop(steps, 7, lambda i, _: (gate.tick(i), 0)[1], 0)
         saves = copies(first.results(), (half0, half1), save_sem)
         begin(saves)
         gate.result(out_gu)
@@ -1150,7 +1184,7 @@
             back = scale * da - wide * (scale * scale * scale * jnp.mean(da * wide, -1, keepdims=True))
             dh[r, :] = (dy[r, :].astype(F32) + back.astype(BF16).astype(F32)).astype(BF16)
 
-        in_rows(h.shape[0], 64, rows)
+        in_rows(h.shape[0], 32, rows)
         first.drain()
         gate.drain()
         end(saves)
@@ -1160,12 +1194,13 @@
     tokens, d = h.shape
     ff = dgu.shape[2]
     tiles, dma, down_cols = ff // TILE, pltpu.SemaphoreType.DMA, d // 2
-    w_in = spec((1, d, TILE), lambda j: (1, 0, j))
+    steps = (tiles + 1) // 2
+    w_in = spec((1, d, 2 * TILE), lambda j: (1, 0, j))
     return pl.pallas_call(
-        functools.partial(middle_kernel, tiles, down_cols),
+        functools.partial(middle_kernel, steps, down_cols),
         name="middle",
-        grid=(tiles,),
-        in_specs=[spec((2, tokens, TILE), lambda j: (0, 0, j)), w_in, w_in, whole((tokens, d)), whole((tokens, d))] + [HBM] * 3,
+        grid=(steps,),
+        in_specs=[spec((2, tokens, 2 * TILE), lambda j: (0, 0, j)), w_in, w_in, whole((tokens, d)), whole((tokens, d))] + [HBM] * 3,
         out_specs=[whole((tokens, d)), whole((GATE_ROWS, ff)), HBM, HBM],
         out_shape=[jax.ShapeDtypeStruct(s, BF16) for s in ((tokens, d), (GATE_ROWS, ff), *half_sums(DOWN_WINDOW, down_cols))],
         scratch_shapes=[pltpu.VMEM((tokens, d), F32)] * 2
@@ -1177,7 +1212,7 @@
     )(dgu, wg, wu, h, dy, sum_down, *gate_halves)
 
 
-def back_kernel(tiles, dh, gate, up, wd, down0, down1, dgu, out, out_down, p, *rest):
+def back_kernel(tiles, dh, gate, up, wd, down0, down1, dgu, out, out_down, p, dps, *rest):
     j = pl.program_id(0)
     place = Place()
     half = dh.shape[1] // 2
@@ -1191,13 +1226,14 @@
         signal_all(near(place))
         begin(loads)
 
+    two_tiles_of_dp(j, tiles, dh, wd, dps)
+
     @pl.when(j < tiles)
     def _():
         slot = lax.rem(j, 2)
         for m in range(dh.shape[0] // ROWS):
             r = pl.ds(m * ROWS, ROWS)
-            dp = dot(dh[r, :], wd[0], NT)
-            p[slot, r, :], dgu[0, r, :], dgu[1, r, :] = hidden_back(gate[r, :], up[r, :], dp)
+            p[slot, r, :], dgu[0, r, :], dgu[1, r, :] = hidden_back(gate[r, :], up[r, :], dps[slot, r, :])
 
     down_gradient(j, tiles, pair, p, dh, half, out)
     pl.when(j == 0)(lambda: end(loads))
@@ -1216,14 +1252,15 @@
         functools.partial(back_kernel, tiles),
         name="back_0",
         grid=(tiles + 1,),
-        in_specs=[whole((tokens, d)), tile, tile, spec((1, TILE, d), lambda j: (0, now(j), 0)), HBM, HBM],
+        in_specs=[whole((tokens, d)), tile, tile, spec((1, 2 * TILE, d), lambda j: (0, lax.div(now(j), 2), 0)), HBM, HBM],
         out_specs=[
             spec((2, tokens, TILE), lambda j: (0, 0, now(j))),
             spec((TILE, half), lambda j: (before(j), 0)),
             whole((DOWN_WINDOW, half)),
         ],
         out_shape=[jax.ShapeDtypeStruct(s, BF16) for s in ((2, tokens, ff), (ff, half), (DOWN_WINDOW, half))],
-        scratch_shapes=[pltpu.VMEM((2, tokens, TILE), BF16), *PairSum.scratch(tiles, TILE, half)]
+        scratch_shapes=[pltpu.VMEM((2, tokens, TILE), BF16)] * 2
+        + PairSum.scratch(tiles, TILE, half)
         + [pltpu.VMEM(t.shape, BF16) for t in down_halves]
         + Rest.scratch(DOWN_WINDOW, half)
         + [pltpu.SemaphoreType.DMA((2,))],

time: 691 us -> 677 us (0.980)
  Pallas kernels: 629 us -> 615 us
    pallas_call x1, Pallas kernels: 74 us -> 63 us  [forward_call(): pl.pallas_call(functools.partial(forward_kernel, tiles), name='forward_0'...]
    pallas_call x1, Pallas kernels: 87 us -> 76.3 us  [layer_call(): pl.pallas_call(functools.partial(layer_kernel, tiles), name='layer_1', gr...]
    pallas_call x1, Pallas kernels: 53.5 us -> 61.1 us  [back_call(): pl.pallas_call(functools.partial(back_kernel, tiles), name='back_0', grid...]
where the time goes in v5:
time: 677 us; the launch traced here: 676 us
  Pallas kernels  615 us (91%)
  local copies, waits for them, and re-layouts  60.3 us (9%)
    pallas_call x1, Pallas kernels, finish_call(): pl.pallas_call(functools.partial(finish_kernel, count), name='finish', ou...  181 us
    pallas_call x2, Pallas kernels, gate_up_call(): pl.pallas_call(functools.partial(gate_up_kernel, tiles, phases, cols), na...  169 us
    pallas_call x1, Pallas kernels, layer_call(): pl.pallas_call(functools.partial(layer_kernel, tiles), name='layer_1', gr...  76.3 us
    pallas_call x1, Pallas kernels, middle_call(): pl.pallas_call(functools.partial(middle_kernel, steps, down_cols), name='...  64.1 us
    pallas_call x1, Pallas kernels, forward_call(): pl.pallas_call(functools.partial(forward_kernel, tiles), name='forward_0'...  63 us
    pallas_call x1, Pallas kernels, back_call(): pl.pallas_call(functools.partial(back_kernel, tiles), name='back_0', grid...  61.1 us
    unnamed x35, local copies, waits for them, and re-layouts  60.3 us

profile of v5, /device:TPU:1, one launch (start us, length us, event | category | flops | bytes accessed | tf_op | source)
XLA Modules:
  0.0 676.4 jit_solution(1730569338450693665)
XLA Ops:
  0.6 63.0 %forward_0.1 = (f32[1024,4224]{1,0:T(8,128)}, f32[1024,4224]{1,0:T(8,128)}, bf16[1024,1536]{1,0:T(8,128)(2,1)}, bf16[1024,1536]{1,0:T(8,128)(2,1)}, bf16[1536,1024]{1,0:T(8,128)(2,1)}) custom-call(bf16[1024,1536]{1,0:T(8,128)(2,1)} %bitcast.106, bf16[2,1536,4224]{2,1,0:T(8,128)(2,1)} %wg.5, bf16[2,1536,4224]{2,1,0:T(8,128)(2,1)} %wu.5, bf16[2,4224,1536]{2,1,0:T(8,128)(2,1)} %wd.5), custom_call_target="tpu_custom_call" | custom-call | tf_op jit(solution)/shard_map/forward_0/pallas_call | solution.py:710
  63.7 76.3 %layer_1.1 = (bf16[2,1024,4224]{2,1,0:T(8,128)(2,1)}, bf16[1536,1024]{1,0:T(8,128)(2,1)}, bf16[4224,768]{1,0:T(8,128)(2,1)}) custom-call(bf16[1024,1536]{1,0:T(8,128)(2,1)} %get-tuple-element.38.a, bf16[1024,1536]{1,0:T(8,128)(2,1)} %bitcast.102, bf16[2,1536,4224]{2,1,0:T(8,128)(2,1)} %wg.5, bf16[2,1536,4224]{2,1,0:T(8,128)(2,1)} %wu.5, ...), custom_call_target="tpu_custom_call" | custom-call | tf_op jit(solution)/shard_map/layer_1/pallas_call | solution.py:821
  140.0 71.0 %gate_up_1.1 = (bf16[3,11,4,4,8,256]{5,4,3,2,1,0:T(8,128)(2,1)}, bf16[3,11,4,4,8,128]{5,4,3,2,1,0:T(8,128)(2,1)}) custom-call(bf16[1536,1024]{1,0:T(8,128)(2,1)} %get-tuple-element.42.at, bf16[2,1024,4224]{2,1,0:T(8,128)(2,1)} %get-tuple-element.39.ahead.behind.dgu, bf16[2,1024,4224]{2,1,0:T(8,128)(2,1)} %get-tuple-element.39.ahead.behind.dgu), custom_call_target="tpu_custom_call" | custom-call | tf_op jit(solution)/shard_map/gate_up_1/pallas_call | solution.py:1126
  211.0 64.1 %middle.1 = (bf16[1024,1536]{1,0:T(8,128)(2,1)}, bf16[24,4224]{1,0:T(8,128)(2,1)}, bf16[3,4,4,24,384]{4,3,2,1,0:T(8,128)(2,1)}, bf16[3,4,4,24,384]{4,3,2,1,0:T(8,128)(2,1)}) custom-call(bf16[2,1024,4224]{2,1,0:T(8,128)(2,1)} %get-tuple-element.39.ahead.behind.dgu, bf16[2,1536,4224]{2,1,0:T(8,128)(2,1)} %wg.5, bf16[2,1536,4224]{2,1,0:T(8,128)(2,1)} %wu.5, ...), custom_call_target="tpu_custom_call" | custom-call | tf_op jit(solution)/shard_map/middle/pallas_call | solution.py:1199
  275.2 61.1 %back_0.1 = (bf16[2,1024,4224]{2,1,0:T(8,128)(2,1)}, bf16[4224,768]{1,0:T(8,128)(2,1)}, bf16[72,768]{1,0:T(8,128)(2,1)}) custom-call(bf16[1024,1536]{1,0:T(8,128)(2,1)} %get-tuple-element.45.dh, f32[1024,4224]{1,0:T(8,128)} %get-tuple-element.46.gate, f32[1024,4224]{1,0:T(8,128)} %get-tuple-element.47.up, bf16[2,4224,1536]{2,1,0:T(8,128)(2,1)} %wd.5, ...), custom_call_target="tpu_custom_call" | custom-call | tf_op jit(solution)/shard_map/back_0/pallas_call | solution.py:1251
  336.3 98.1 %gate_up_0.1 = (bf16[24,4224]{1,0:T(8,128)(2,1)}, bf16[72,768]{1,0:T(8,128)(2,1)}) custom-call(bf16[1536,1024]{1,0:T(8,128)(2,1)} %get-tuple-element.37.at, bf16[2,1024,4224]{2,1,0:T(8,128)(2,1)} %get-tuple-element.50.ahead.behind, bf16[2,1024,4224]{2,1,0:T(8,128)(2,1)} %get-tuple-element.50.ahead.behind, bf16[4,4,264,768]{3,2,1,0:T(8,128)(2,1)} %bitcast.105), custom_call_target="tpu_custom_call" | custom-call | tf_op jit(solution)/shard_map/gate_up_0/pallas_call | solution.py:1126
  434.4 181.5 %finish.1 = (bf16[2,4,4,4,24,4224]{5,4,3,2,1,0:T(8,128)(2,1)}, bf16[2,4,4,4,24,4224]{5,4,3,2,1,0:T(8,128)(2,1)}, bf16[2,4,4,264,1536]{4,3,2,1,0:T(8,128)(2,1)}, ...) custom-call(bf16[24,4224]{1,0:T(8,128)(2,1)} %get-tuple-element.52.r, ...), custom_call_target="tpu_custom_call" | custom-call | flops 1000000000 | bytes 100000000 | tf_op jit(solution)/shard_map/finish/pallas_call | solution.py:588
  615.9 0.0 slice-start
  615.9 0.0 slice-start.1
  615.9 0.0 slice-start.2
  615.9 0.0 slice-start.3
  616.0 23.9 %copy.29 = bf16[2,1536,4224]{2,1,0:T(8,128)(2,1)} copy(bf16[2,1536,4224]{2,1,0:T(8,128)(2,1)} %bitcast.101) | data formatting | bytes 51904512
  639.8 22.6 %copy.30 = bf16[2,1536,4224]{2,1,0:T(8,128)(2,1)} copy(bf16[2,1536,4224]{2,1,0:T(8,128)(2,1)} %bitcast.100) | data formatting | bytes 51904512
  662.4 0.0 slice-done
  662.4 0.0 slice-done.1
  662.4 0.0 slice-done.2
  662.5 9.4 %copy.31 = bf16[2,4224,1536]{2,1,0:T(8,128)(2,1)} copy(bf16[2,4224,1536]{2,1,0:T(8,128)(2,1)S(1)} %bitcast.99) | data formatting | bytes 51904512
  671.9 0.8 copy.32
  672.6 0.8 copy.33
  673.4 0.8 copy.34
  674.1 0.8 copy.35
  674.9 0.8 copy.36
  675.6 0.0 copy-done
  675.6 0.8 copy.37
  (19 shorter events, 0.0 us)
Async XLA Ops:
  615.9 46.5 %slice-start = ((s8[25952256]{0:T(1024)(128)(4,1)}), s8[4194304]{0:T(1024)(128)(4,1)S(1)}, s32[]{:S(2)}) async-start(s8[25952256]{0:T(1024)(128)(4,1)} %bitcast.97), calls=%async_computation | async-start | bytes 8388608
  615.9 46.5 %slice-start.1 = ((s8[25952256]{0:T(1024)(128)(4,1)}), s8[4194304]{0:T(1024)(128)(4,1)S(1)}, s32[]{:S(2)}) async-start(s8[25952256]{0:T(1024)(128)(4,1)} %bitcast.97), calls=%async_computation.1 | async-start | bytes 8388608
  615.9 46.4 %slice-start.2 = ((s8[25952256]{0:T(1024)(128)(4,1)}), s8[4194304]{0:T(1024)(128)(4,1)S(1)}, s32[]{:S(2)}) async-start(s8[25952256]{0:T(1024)(128)(4,1)} %bitcast.97), calls=%async_computation.2 | async-start | bytes 8388608
  615.9 46.4 %slice-start.3 = ((s8[25952256]{0:T(1024)(128)(4,1)}), s8[4194304]{0:T(1024)(128)(4,1)S(1)}, s32[]{:S(2)}) async-start(s8[25952256]{0:T(1024)(128)(4,1)} %bitcast.97), calls=%async_computation.3 | async-start | bytes 8388608
  639.8 22.6 %slice-start.4 = ((s8[25952256]{0:T(1024)(128)(4,1)}), s8[4194304]{0:T(1024)(128)(4,1)S(1)}, s32[]{:S(2)}) async-start(s8[25952256]{0:T(1024)(128)(4,1)} %bitcast.97), calls=%async_computation.4 | async-start | bytes 8388608
  639.8 22.6 %slice-start.5 = ((s8[25952256]{0:T(1024)(128)(4,1)}), s8[4194304]{0:T(1024)(128)(4,1)S(1)}, s32[]{:S(2)}) async-start(s8[25952256]{0:T(1024)(128)(4,1)} %bitcast.97), calls=%async_computation.5 | async-start | bytes 8388608
  639.8 22.6 %slice-start.6 = ((s8[25952256]{0:T(1024)(128)(4,1)}), s8[786432]{0:T(1024)(128)(4,1)S(1)}, s32[]{:S(2)}) async-start(s8[25952256]{0:T(1024)(128)(4,1)} %bitcast.97), calls=%async_computation.6 | async-start | bytes 1572864
  662.4 9.4 %copy-start.5 = (f32[792,128]{1,0:T(8,128)S(1)}, f32[792,128]{1,0:T(8,128)}, u32[]{:S(2)}) copy-start(f32[792,128]{1,0:T(8,128)} %get-tuple-element.59) | copy-start | bytes 1216516
  662.4 10.2 %copy-start.4 = (f32[792,128]{1,0:T(8,128)S(1)}, f32[792,128]{1,0:T(8,128)}, u32[]{:S(2)}) copy-start(f32[792,128]{1,0:T(8,128)} %get-tuple-element.60) | copy-start | bytes 1216516
  662.5 10.9 %copy-start.3 = (f32[792,128]{1,0:T(8,128)S(1)}, f32[792,128]{1,0:T(8,128)}, u32[]{:S(2)}) copy-start(f32[792,128]{1,0:T(8,128)} %get-tuple-element.61) | copy-start | bytes 1216516
  662.5 11.6 %copy-start.2 = (f32[792,128]{1,0:T(8,128)S(1)}, f32[792,128]{1,0:T(8,128)}, u32[]{:S(2)}) copy-start(f32[792,128]{1,0:T(8,128)} %get-tuple-element.62) | copy-start | bytes 1216516
  662.5 12.4 %copy-start.1 = (f32[792,128]{1,0:T(8,128)S(1)}, f32[792,128]{1,0:T(8,128)}, u32[]{:S(2)}) copy-start(f32[792,128]{1,0:T(8,128)} %get-tuple-element.63) | copy-start | bytes 1216516
  662.5 13.1 %copy-start = (f32[792,128]{1,0:T(8,128)S(1)}, f32[792,128]{1,0:T(8,128)}, u32[]{:S(2)}) copy-start(f32[792,128]{1,0:T(8,128)} %get-tuple-element.64) | copy-start | bytes 1216516

commit v6 on v5

--- a/solution.py
+++ b/solution.py
@@ -372,16 +372,14 @@
         lax.fori_loop(0, 6, sent, 0)
 
 
-def finish_kernel(count, *refs):
+def update_kernel(count, *refs):
     sums_gu, sums_d, m_in, v_in, w_in = refs[0:2], refs[2:4], refs[4:7], refs[7:10], refs[10:13]
-    w_out, m_out, v_out = refs[13:16], refs[16:19], refs[19:22]
-    moments_gu, moments_d, old_gu, old_d, other_d, tiles = refs[22:28]
-    load_sem, early_send, early_recv, norm_send, norm_recv, late_local, late_send, late_recv = refs[28:36]
-    gather_refs = refs[36:]
+    new_gu, new_d, m_out, v_out = refs[13], refs[14], refs[15:18], refs[18:21]
+    moments_gu, moments_d, old_gu, old_d, other_d, tiles = refs[21:27]
+    load_sem, early_send, early_recv, norm_send, norm_recv, late_local, late_send, late_recv = refs[27:35]
     place = Place()
     x, y, z = place.at
     core = place.core
-    gather = Gather(place, gather_refs[:2], gather_refs[2:6], w_out, gather_refs[6:9])
     partner = place.partner()
     gate_tiles, down_tiles = sums_gu[0].shape[1] // LANES, sums_d[0].shape[1] // LANES
     gate_stride, down_stride = 2 * gate_tiles, 4 * down_tiles
@@ -510,7 +508,7 @@
                 rows = pl.ds(8 * t, 8)
                 g = sums_gu[l][rows, lanes].astype(F32) * factor
                 step = moments(moments_gu, 8 * t * gate_stride + 2 * j + l, gate_stride, g)
-                gather.bufs[0][l, x, y, z, rows, lanes] = weight(old_gu[l, rows, lanes], step)
+                new_gu[l, rows, lanes] = weight(old_gu[l, rows, lanes], step)
             return 0
 
         lax.fori_loop(0, gate_tiles, gate_up, 0, unroll=3)
@@ -522,11 +520,10 @@
                 start = (PREV + 8 * i) * down_stride + 2 * j + l
                 g = sums_d[l][rows, lanes].astype(F32) * factor
                 step = moments(moments_d, start + 2 * down_tiles * core, down_stride, g)
-                gather.bufs[1][l, x, y, z, rows, lanes] = weight(old_d[l, rows, lanes], step)
+                new_d[l, rows, lanes] = weight(old_d[l, rows, lanes], step)
             return 0
 
         lax.fori_loop(0, 9, down, 0)
-        gather.own(l)
     for l in range(2):
 
         def down_other(i, _, l=l):
@@ -549,8 +546,6 @@
                 put(gate_rows(i, 1 - core), out[c], late_send.at[i], late_recv.at[i], partner).start()
 
         pltpu.make_async_copy(down_rows(i, own_rows, DOWN_ROWS), out[2], late_local.at[2 + i]).start()
-    gather.first_axis()
-    gather.other_axes()
     for i, out in enumerate((m_out, v_out)):
         pltpu.make_async_copy(gate_rows(i, core), out[0], late_local.at[i]).wait()
         pltpu.make_async_copy(down_rows(i, own_rows, DOWN_ROWS), out[2], late_local.at[2 + i]).wait()
@@ -567,10 +562,23 @@
                 rows = down_rows(i, 0, PREV)
                 put(rows, rows, early_send.at[4 + 2 * i + c], early_recv.at[4 + i], following[c]).wait_send()
 
+
+def gather_kernel(new_gu, new_d, *refs):
+    w_out, load_sem, rest = refs[:3], refs[3], refs[4:]
+    place = Place()
+    gather = Gather(place, rest[:2], rest[2:6], w_out, rest[6:9])
+    loads = [pltpu.make_async_copy(new, buf.at[(ALL, *place.at)], load_sem.at[i]) for i, (new, buf) in enumerate(zip((new_gu, new_d), rest[:2]))]
+    begin(loads)
+    signal_all(near(place))
+    end(loads)
+    for l in range(2):
+        gather.own(l)
+    gather.first_axis()
+    gather.other_axes()
     gather.drain()
 
 
-def finish_call(count, collective_id, sums_gu, sums_d, m, v, w):
+def update_call(count, collective_id, sums_gu, sums_d, m, v, w):
     gate_cols, down_half = sums_gu[0].shape[1], sums_d[0].shape[1]
     operands = [*sums_gu, *sums_d, *m, *v, *w]
     hbm, vmem = pl.BlockSpec(memory_space=pltpu.HBM), pl.BlockSpec(memory_space=pltpu.VMEM)
@@ -585,16 +593,29 @@
         pltpu.VMEM((4, SIDE, 8, LANES), F32),
         dma((6,)), dma((10,)), dma((8,)), dma((12,)), dma((12,)), dma((4,)), dma((2,)), dma((2,)),
     ]
+    new = [jax.ShapeDtypeStruct((2, 24, gate_cols), BF16), jax.ShapeDtypeStruct((2, 72, down_half), BF16)]
     return pl.pallas_call(
-        functools.partial(finish_kernel, count),
-        name="finish",
-        out_shape=[jax.ShapeDtypeStruct(t.shape, t.dtype) for t in (*w, *m, *v)],
+        functools.partial(update_kernel, count),
+        name="update",
+        out_shape=[*new, *[jax.ShapeDtypeStruct(t.shape, t.dtype) for t in (*m, *v)]],
         in_specs=[vmem] * 4 + [hbm] * 9,
-        out_specs=[hbm] * 9,
-        scratch_shapes=scratch + Gather.scratch(gate_cols, down_half),
+        out_specs=[vmem] * 2 + [hbm] * 6,
+        scratch_shapes=scratch,
         compiler_params=pltpu.CompilerParams(collective_id=collective_id, has_side_effects=True, vmem_limit_bytes=VMEM_LIMIT),
-        cost_estimate=pl.CostEstimate(flops=10**9, bytes_accessed=10**8, transcendentals=0),
     )(*operands)
+
+
+def gather_call(collective_id, new_gu, new_d, w):
+    hbm = pl.BlockSpec(memory_space=pltpu.HBM)
+    return pl.pallas_call(
+        gather_kernel,
+        name="gather",
+        out_shape=[jax.ShapeDtypeStruct(t.shape, t.dtype) for t in w],
+        in_specs=[hbm] * 2,
+        out_specs=[hbm] * 3,
+        scratch_shapes=[pltpu.SemaphoreType.DMA((2,)), *Gather.scratch(new_gu.shape[2], new_d.shape[2])],
+        compiler_params=pltpu.CompilerParams(collective_id=collective_id, has_side_effects=True, vmem_limit_bytes=VMEM_LIMIT),
+    )(new_gu, new_d)
 
 
 TILE = 384
@@ -676,8 +697,8 @@
         r = pl.ds(m * ROWS, ROWS)
         gu = dot(a[r, :], both, NN)
         g, u = gu[:, :TILE], gu[:, TILE:]
-        gate[r, :] = g
-        up[r, :] = u
+        gate[0, r, :] = g
+        up[0, r, :] = u
         p[slot, r, :] = (g * lax.logistic(g) * u).astype(BF16)
 
     @pl.when(slot == 1)
@@ -712,8 +733,8 @@
         name="forward_0",
         grid=(tiles,),
         in_specs=[whole((tokens, d)), w_in, w_in, spec((1, 2 * TILE, d), lambda j: (0, lax.div(j, 2), 0))],
-        out_specs=[spec((tokens, TILE), lambda j: (0, j))] * 2 + [whole((tokens, d))] * 2 + [whole((d, tokens))],
-        out_shape=[jax.ShapeDtypeStruct((tokens, ff), F32)] * 2
+        out_specs=[spec((1, tokens, TILE), lambda j: (j, 0, 0))] * 2 + [whole((tokens, d))] * 2 + [whole((d, tokens))],
+        out_shape=[jax.ShapeDtypeStruct((tiles, tokens, TILE), F32)] * 2
         + [jax.ShapeDtypeStruct((tokens, d), BF16)] * 2
         + [jax.ShapeDtypeStruct((d, tokens), BF16)],
         scratch_shapes=[pltpu.VMEM((tokens, d), BF16), pltpu.VMEM((tokens, d), F32), pltpu.VMEM((2, tokens, TILE), BF16)],
@@ -786,7 +807,7 @@
         for m in range(a.shape[0] // ROWS):
             r = pl.ds(m * ROWS, ROWS)
             gu = dot(a[r, :], both, NN)
-            p[slot, r, :], dgu[0, r, :], dgu[1, r, :] = hidden_back(gu[:, :TILE], gu[:, TILE:], dps[slot, r, :])
+            p[slot, r, :], dgu[0, 0, r, :], dgu[0, 1, r, :] = hidden_back(gu[:, :TILE], gu[:, TILE:], dps[slot, r, :])
 
     down_gradient(j, tiles, pair, p, dy, dy.shape[1] // 2, out)
 
@@ -823,9 +844,9 @@
         name="layer_1",
         grid=(tiles + 1,),
         in_specs=[whole((tokens, d))] * 2 + [w_in, w_in, spec((1, 2 * TILE, d), lambda j: (1, lax.div(now(j), 2), 0))],
-        out_specs=[spec((2, tokens, TILE), lambda j: (0, 0, now(j))), whole((d, tokens)), spec((TILE, half), lambda j: (before(j), 0))],
+        out_specs=[spec((1, 2, tokens, TILE), lambda j: (now(j), 0, 0, 0)), whole((d, tokens)), spec((TILE, half), lambda j: (before(j), 0))],
         out_shape=[
-            jax.ShapeDtypeStruct((2, tokens, ff), BF16),
+            jax.ShapeDtypeStruct((tiles, 2, tokens, TILE), BF16),
             jax.ShapeDtypeStruct((d, tokens), BF16),
             jax.ShapeDtypeStruct((ff, half), BF16),
         ],
@@ -1081,7 +1102,7 @@
     @pl.when(j <= tiles + 1)
     def _():
         slot, kept = pair.reserve(j), stream.keep(j - 2)
-        both = side_by_side(ahead[1 - core], behind[core])
+        both = side_by_side(ahead[0, 1 - core], behind[0, core])
         landed = lax.rem(j + tiles - 2, tiles)
         for m in range(SIDE):
             r = pl.ds(m * BLOCK_ROWS, BLOCK_ROWS)
@@ -1113,8 +1134,8 @@
 
 def gate_up_call(name, collective_id, phases, at, dgu, *sum_down):
     d, tokens = at.shape
-    ff = dgu.shape[2]
-    tiles, cols, dma = ff // TILE, d // 2, pltpu.SemaphoreType.DMA
+    tiles, cols, dma = dgu.shape[0], d // 2, pltpu.SemaphoreType.DMA
+    ff = tiles * TILE
     now, before = clip(tiles), clip(tiles, 2)
     if phases == 1:
         shapes = stream_halves(tiles)
@@ -1129,8 +1150,8 @@
         grid=(tiles + (6 if phases == 1 else 10),),
         in_specs=[
             whole((d, tokens)),
-            spec((2, tokens, TILE), lambda j: (0, 0, now(j))),
-            spec((2, tokens, TILE), lambda j: (0, 0, before(j))),
+            spec((1, 2, tokens, TILE), lambda j: (now(j), 0, 0, 0)),
+            spec((1, 2, tokens, TILE), lambda j: (before(j), 0, 0, 0)),
             *[HBM] * len(sum_down),
         ],
         out_specs=out_specs,
@@ -1140,13 +1161,82 @@
     )(at, dgu, dgu, *sum_down)
 
 
-def middle_kernel(steps, down_cols, dgu, wg, wu, h, dy, sum_down, gate0, gate1, dh, out_gu, half0, half1, acc_g, acc_u, *rest):
+def gate_up_first_kernel(tiles, cols, at, ahead, behind, sum_down, out, half0, half1, *rest):
     j = pl.program_id(0)
     place = Place()
-    first = First.of(place, DOWN_WINDOW, down_cols, rest[:5])
-    gate = StreamRest(place, gate0.shape[1], rest[5:7], rest[7:15])
-    load_sem, gate_sem, save_sem = rest[15:18]
-    loads = loads_down(sum_down, first, load_sem) + copies((gate0, gate1), rest[5:7], gate_sem)
+    core = place.core
+    pair = PairSum(place, tiles, *rest[:4])
+    first = First.of(place, DOWN_WINDOW, cols, rest[4:9])
+    load_sem, save_sem = rest[9:11]
+    loads = loads_down(sum_down, first, load_sem)
+
+    @pl.when(j == 0)
+    def _():
+        signal_all(near(place))
+        begin(loads)
+
+    pl.when(j >= 2)(lambda: pair.copy(j - 2).wait_recv())
+    slot = pair.reserve(j)
+    both = side_by_side(ahead[0, 1 - core], behind[0, core])
+    landed = lax.rem(j + tiles - 2, tiles)
+    for m in range(at.shape[0] // ROWS):
+        r = pl.ds(m * ROWS, ROWS)
+        tile = dot(at[r, :], both, NN)
+        slot[r, :] = tile[:, :TILE].astype(BF16)
+        out[r, :] = (tile[:, TILE:] + pair.landing[landed, r, :].astype(F32)).astype(BF16)
+    pl.when(j < tiles)(lambda: pair.copy(j).start())
+
+    pl.when(j == 0)(lambda: end(loads))
+    spread(j, tiles + 2, 16, first.tick)
+
+    @pl.when(j == tiles + 1)
+    def _():
+        saves = copies(first.results(), (half0, half1), save_sem)
+        begin(saves)
+        first.drain()
+        end(saves)
+
+
+def gate_up_first_call(name, collective_id, at, dgu, sum_down):
+    d, tokens = at.shape
+    tiles, cols, dma = dgu.shape[0], sum_down.shape[-1], pltpu.SemaphoreType.DMA
+    now, before = clip(tiles), clip(tiles, 2)
+    return pl.pallas_call(
+        functools.partial(gate_up_first_kernel, tiles, cols),
+        name=name,
+        grid=(tiles + 2,),
+        in_specs=[
+            whole((d, tokens)),
+            spec((1, 2, tokens, TILE), lambda j: (now(j), 0, 0, 0)),
+            spec((1, 2, tokens, TILE), lambda j: (before(j), 0, 0, 0)),
+            HBM,
+        ],
+        out_specs=[spec((d, TILE), lambda j: (0, before(j))), HBM, HBM],
+        out_shape=[jax.ShapeDtypeStruct((d, tiles * TILE), BF16)]
+        + [jax.ShapeDtypeStruct(s, BF16) for s in half_sums(DOWN_WINDOW, cols)],
+        scratch_shapes=[*PairSum.scratch(tiles, d, TILE), *First.scratch(DOWN_WINDOW, cols), dma((SIDE,)), dma((2,))],
+        compiler_params=params(collective_id),
+    )(at, dgu, dgu, sum_down)
+
+
+def column_halves(cols):
+    return ways_of(cols)
+
+
+def load_columns(source, first, part, sem):
+    start, width = part
+    return [pltpu.make_async_copy(source.at[:, :, :, :, pl.ds(start, width)], first.held, sem)]
+
+
+def middle_kernel(steps, ff, down_cols, dgu, wg, wu, h, dy, sum_gu, down0, down1, dh, out_down, half0, half1, acc_g, acc_u, *rest):
+    j = pl.program_id(0)
+    place = Place()
+    part = column_halves(ff)[0]
+    first = First.of(place, GATE_ROWS, part[1], rest[:5])
+    before = rest[5:7]
+    down = Rest.of(place, DOWN_WINDOW, down_cols, before, rest[7:15])
+    load_sem, save_sem = rest[15:17]
+    loads = copies((down0, down1), before, load_sem) + load_columns(sum_gu, first, part, load_sem.at[2])
 
     @pl.when(j == 0)
     def _():
@@ -1155,27 +1245,26 @@
         clear(acc_g)
         clear(acc_u)
 
-    def add_up(r, k):
-        acc_g[r, :] += dot(dgu[0, r, pl.ds(0, k)], wg[0, :, pl.ds(0, k)], NT)
-        acc_u[r, :] += dot(dgu[1, r, pl.ds(0, k)], wu[0, :, pl.ds(0, k)], NT)
-
-    @pl.when(j < steps - 1)
-    def _():
-        for m in range(h.shape[0] // ROWS):
-            add_up(pl.ds(m * ROWS, ROWS), 2 * TILE)
-
-    pl.when(j == steps - 1)(lambda: in_rows(h.shape[0], ROWS, lambda r: add_up(r, TILE)))
+    def add_up(r, two):
+        for which, (acc, w) in enumerate(((acc_g, wg), (acc_u, wu))):
+            if two:
+                acc[r, :] += dot(side_by_side(dgu[0, which, r, :], dgu[1, which, r, :]), w[0], NT)
+            else:
+                acc[r, :] += dot(dgu[0, which, r, :], w[0, :, pl.ds(0, TILE)], NT)
+
+    pl.when(j < steps - 1)(lambda: in_rows(h.shape[0], 2 * ROWS, lambda r: add_up(r, True)))
+    pl.when(j == steps - 1)(lambda: in_rows(h.shape[0], ROWS, lambda r: add_up(r, False)))
 
     pl.when(j == 0)(lambda: end(loads))
-    gate.tick(j)
+    down.tick(j)
     spread(j, steps, 16, first.tick)
 
     @pl.when(j == steps - 1)
     def _():
-        lax.fori_loop(steps, 7, lambda i, _: (gate.tick(i), 0)[1], 0)
+        lax.fori_loop(steps, 7, lambda i, _: (down.tick(i), 0)[1], 0)
         saves = copies(first.results(), (half0, half1), save_sem)
         begin(saves)
-        gate.result(out_gu)
+        down.result(out_down)
 
         def rows(r):
             wide = h[r, :].astype(F32)
@@ -1186,40 +1275,45 @@
 
         in_rows(h.shape[0], 32, rows)
         first.drain()
-        gate.drain()
+        down.drain()
         end(saves)
 
 
-def middle_call(collective_id, dgu, wg, wu, h, dy, sum_down, gate_halves):
+def middle_call(collective_id, dgu, wg, wu, h, dy, sum_gu, down_halves):
     tokens, d = h.shape
-    ff = dgu.shape[2]
-    tiles, dma, down_cols = ff // TILE, pltpu.SemaphoreType.DMA, d // 2
+    tiles, dma, down_cols = dgu.shape[0], pltpu.SemaphoreType.DMA, d // 2
+    ff = tiles * TILE
     steps = (tiles + 1) // 2
+    width = column_halves(ff)[0][1]
     w_in = spec((1, d, 2 * TILE), lambda j: (1, 0, j))
     return pl.pallas_call(
-        functools.partial(middle_kernel, steps, down_cols),
+        functools.partial(middle_kernel, steps, ff, down_cols),
         name="middle",
         grid=(steps,),
-        in_specs=[spec((2, tokens, 2 * TILE), lambda j: (0, 0, j)), w_in, w_in, whole((tokens, d)), whole((tokens, d))] + [HBM] * 3,
-        out_specs=[whole((tokens, d)), whole((GATE_ROWS, ff)), HBM, HBM],
-        out_shape=[jax.ShapeDtypeStruct(s, BF16) for s in ((tokens, d), (GATE_ROWS, ff), *half_sums(DOWN_WINDOW, down_cols))],
+        in_specs=[spec((2, 2, tokens, TILE), lambda j: (j, 0, 0, 0)), w_in, w_in, whole((tokens, d)), whole((tokens, d))] + [HBM] * 3,
+        out_specs=[whole((tokens, d)), whole((DOWN_WINDOW, down_cols)), HBM, HBM],
+        out_shape=[jax.ShapeDtypeStruct(s, BF16) for s in ((tokens, d), (DOWN_WINDOW, down_cols), *half_sums(GATE_ROWS, width))],
         scratch_shapes=[pltpu.VMEM((tokens, d), F32)] * 2
-        + First.scratch(DOWN_WINDOW, down_cols)
-        + [pltpu.VMEM(t.shape, BF16) for t in gate_halves]
-        + StreamRest.scratch(tiles)
-        + [dma((SIDE,)), dma((2,)), dma((2,))],
+        + First.scratch(GATE_ROWS, width)
+        + [pltpu.VMEM(t.shape, BF16) for t in down_halves]
+        + Rest.scratch(DOWN_WINDOW, down_cols)
+        + [dma((3,)), dma((2,))],
         compiler_params=params(collective_id),
-    )(dgu, wg, wu, h, dy, sum_down, *gate_halves)
-
-
-def back_kernel(tiles, dh, gate, up, wd, down0, down1, dgu, out, out_down, p, dps, *rest):
+    )(dgu, wg, wu, h, dy, sum_gu, *down_halves)
+
+
+def back_kernel(tiles, ff, dh, gate, up, wd, gate0, gate1, sum_gu, dgu, out, out_gu, p, dps, *rest):
     j = pl.program_id(0)
     place = Place()
-    half = dh.shape[1] // 2
+    core, half = place.core, dh.shape[1] // 2
+    parts = column_halves(ff)
     pair = PairSum(place, tiles, *rest[:4])
     before = rest[4:6]
-    down = Rest.of(place, DOWN_WINDOW, half, before, rest[6:14])
-    loads = copies((down0, down1), before, rest[14])
+    rest_a = Rest.of(place, GATE_ROWS, parts[0][1], before, rest[6:14])
+    first = First.of(place, GATE_ROWS, parts[1][1], rest[14:19])
+    rest_b = Rest.of(place, GATE_ROWS, parts[1][1], first.results(), rest[19:27])
+    load_sem = rest[27]
+    loads = copies((gate0, gate1), before, load_sem) + load_columns(sum_gu, first, parts[1], load_sem.at[2])
 
     @pl.when(j == 0)
     def _():
@@ -1227,45 +1321,62 @@
         begin(loads)
 
     two_tiles_of_dp(j, tiles, dh, wd, dps)
+    pl.when(j >= 2)(lambda: pair.copy(j - 2).wait_recv())
+    tile = jnp.minimum(j, tiles - 1)
+    ours = p[lax.rem(j + 1, 3)]
+    for m in range(dh.shape[0] // ROWS):
+        r = pl.ds(m * ROWS, ROWS)
+        p[lax.rem(tile, 3), r, :], dgu[0, 0, r, :], dgu[0, 1, r, :] = hidden_back(gate[0, r, :], up[0, r, :], dps[lax.rem(tile, 2), r, :])
+    own = dot(ours, dh[:, pl.ds(pl.multiple_of(core * half, LANES), half)], TN)
+    out[...] = (own + pair.landing[lax.rem(j + tiles - 2, tiles)].astype(F32)).astype(BF16)
 
     @pl.when(j < tiles)
     def _():
-        slot = lax.rem(j, 2)
-        for m in range(dh.shape[0] // ROWS):
-            r = pl.ds(m * ROWS, ROWS)
-            p[slot, r, :], dgu[0, r, :], dgu[1, r, :] = hidden_back(gate[r, :], up[r, :], dps[slot, r, :])
-
-    down_gradient(j, tiles, pair, p, dh, half, out)
+        slot = pair.reserve(j)
+        slot[...] = dot(p[lax.rem(j, 3)], dh[:, pl.ds(pl.multiple_of((1 - core) * half, LANES), half)], TN).astype(BF16)
+        pair.copy(j).start()
+
     pl.when(j == 0)(lambda: end(loads))
-    down.tick(j)
-    pl.when(j == 7)(lambda: down.result(out_down))
-    pl.when(j == tiles)(down.drain)
-
-
-def back_call(collective_id, dh, gate, up, wd, down_halves):
+    rest_a.tick(j)
+    pl.when(j < 6)(lambda: spread(j, 6, 16, first.tick))
+    pl.when(j >= 5)(lambda: rest_b.tick(j - 5))
+
+    @pl.when(j == tiles + 1)
+    def _():
+        for sums, (start, width) in ((rest_a, parts[0]), (rest_b, parts[1])):
+            sums.result(out_gu.at[:, pl.ds(start, width)])
+        pair.drain()
+        for sums in (rest_a, first, rest_b):
+            sums.drain()
+
+
+def back_call(collective_id, dh, gate, up, wd, sum_gu, gate_halves):
     tokens, d = dh.shape
-    ff = gate.shape[1]
-    tiles, half = ff // TILE, d // 2
-    now, before = clip(tiles), clip(tiles, 1)
-    tile = spec((tokens, TILE), lambda j: (0, now(j)))
+    tiles, half, dma = gate.shape[0], d // 2, pltpu.SemaphoreType.DMA
+    ff = tiles * TILE
+    now, before = clip(tiles), clip(tiles, 2)
+    tile = spec((1, tokens, TILE), lambda j: (now(j), 0, 0))
+    parts = column_halves(ff)
     return pl.pallas_call(
-        functools.partial(back_kernel, tiles),
+        functools.partial(back_kernel, tiles, ff),
         name="back_0",
-        grid=(tiles + 1,),
-        in_specs=[whole((tokens, d)), tile, tile, spec((1, 2 * TILE, d), lambda j: (0, lax.div(now(j), 2), 0)), HBM, HBM],
+        grid=(tiles + 2,),
+        in_specs=[whole((tokens, d)), tile, tile, spec((1, 2 * TILE, d), lambda j: (0, lax.div(now(j), 2), 0)), HBM, HBM, HBM],
         out_specs=[
-            spec((2, tokens, TILE), lambda j: (0, 0, now(j))),
+            spec((1, 2, tokens, TILE), lambda j: (now(j), 0, 0, 0)),
             spec((TILE, half), lambda j: (before(j), 0)),
-            whole((DOWN_WINDOW, half)),
+            whole((GATE_ROWS, ff)),
         ],
-        out_shape=[jax.ShapeDtypeStruct(s, BF16) for s in ((2, tokens, ff), (ff, half), (DOWN_WINDOW, half))],
-        scratch_shapes=[pltpu.VMEM((2, tokens, TILE), BF16)] * 2
+        out_shape=[jax.ShapeDtypeStruct(s, BF16) for s in ((tiles, 2, tokens, TILE), (ff, half), (GATE_ROWS, ff))],
+        scratch_shapes=[pltpu.VMEM((3, tokens, TILE), BF16), pltpu.VMEM((2, tokens, TILE), BF16)]
         + PairSum.scratch(tiles, TILE, half)
-        + [pltpu.VMEM(t.shape, BF16) for t in down_halves]
-        + Rest.scratch(DOWN_WINDOW, half)
-        + [pltpu.SemaphoreType.DMA((2,))],
+        + [pltpu.VMEM(t.shape, BF16) for t in gate_halves]
+        + Rest.scratch(GATE_ROWS, parts[0][1])
+        + First.scratch(GATE_ROWS, parts[1][1])
+        + Rest.scratch(GATE_ROWS, parts[1][1])
+        + [dma((3,))],
         compiler_params=params(collective_id),
-    )(dh, gate, up, wd, *down_halves)
+    )(dh, gate, up, wd, *gate_halves, sum_gu)
 
 
 def flat(m):
@@ -1287,16 +1398,18 @@
         windows = (SIDE, SIDE, 4 * 66, d // 2)
         gate0, up0, h1, a1, a0t = forward_call(x, wg, wu, wd)
         dgu1, a1t, down1 = layer_call(1, a1, dy, wg, wu, wd)
-        down1 = down1.reshape(windows)
-        gate_halves = gate_up_call("gate_up_1", 2, 1, a1t, dgu1)
-        dh1, sum_gu1, *down_halves = middle_call(3, dgu1, wg, wu, h1, dy, down1, gate_halves)
-        dgu0, down0, sum_down1 = back_call(4, dh1, gate0, up0, wd, down_halves)
+        blocks = (SIDE, SIDE, SIDE, GATE_ROWS, ff)
+        gu1, *down_halves = gate_up_first_call("gate_up_1", 2, a1t, dgu1, down1.reshape(windows))
+        gu1 = gu1.reshape(blocks)
+        dh1, sum_down1, *gate_halves = middle_call(3, dgu1, wg, wu, h1, dy, gu1, down_halves)
+        dgu0, down0, sum_gu1 = back_call(4, dh1, gate0, up0, wd, gu1, gate_halves)
         sum_gu0, sum_down0 = gate_up_call("gate_up_0", 5, 3, a0t, dgu0, down0.reshape(windows))
 
         views = [(2, SIDE, SIDE, SIDE, GATE_ROWS, ff)] * 2 + [(2, SIDE, SIDE, 4 * 66, d)]
         w = [t.reshape(view) for t, view in zip((wg, wu, wd), views, strict=True)]
         m, v = [flat(t) for t in (mg, mu, md)], [flat(t) for t in (vg, vu, vd)]
-        out = finish_call(3 * layers * d * ff, 7, [sum_gu0, sum_gu1], [sum_down0, sum_down1], m, v, w)
+        new_gu, new_d, *moments = update_call(3 * layers * d * ff, 6, [sum_gu0, sum_gu1], [sum_down0, sum_down1], m, v, w)
+        out = [*gather_call(7, new_gu, new_d, w), *moments]
         new = [t.reshape(like.shape) for t, like in zip(out[:3], (wg, wu, wd), strict=True)]
         return (*new, *[unflat(t, like.shape) for t, like in zip(out[3:], (mg, mu, md, vg, vu, vd), strict=True)])
 

time: 677 us -> 670 us (0.990)
    pallas_call x2 -> x1, Pallas kernels: 169 us -> 99.9 us  [gate_up_call(): pl.pallas_call(functools.partial(gate_up_kernel, tiles, phases, cols), na...]
    pallas_call x3 -> x5, Pallas kernels: 307 us -> 370 us  [the longest x1 160 us: gather_call(): pl.pallas_call(gather_kernel, name='gather', out_shape=[jax.ShapeDtypeStr...]
where the time goes in v6:
time: 670 us
  Pallas kernels  609 us (91%)
  local copies, waits for them, and re-layouts  60.3 us (9%)
    pallas_call x1, Pallas kernels, gather_call(): pl.pallas_call(gather_kernel, name='gather', out_shape=[jax.ShapeDtypeStr...  160 us
    pallas_call x1, Pallas kernels, gate_up_call(): pl.pallas_call(functools.partial(gate_up_kernel, tiles, phases, cols), na...  99.9 us
    pallas_call x1, Pallas kernels, layer_call(): pl.pallas_call(functools.partial(layer_kernel, tiles), name='layer_1', gr...  76.2 us
    pallas_call x1, Pallas kernels, back_call(): pl.pallas_call(functools.partial(back_kernel, tiles, ff), name='back_0',...  75.1 us
    pallas_call x1, Pallas kernels, forward_call(): pl.pallas_call(functools.partial(forward_kernel, tiles), name='forward_0'...  63 us
    unnamed x35, local copies, waits for them, and re-layouts  60.3 us
    pallas_call x1, Pallas kernels, middle_call(): pl.pallas_call(functools.partial(middle_kernel, steps, ff, down_cols), na...  57.5 us
    pallas_call x1, Pallas kernels, gate_up_first_call(): pl.pallas_call(functools.partial(gate_up_first_kernel, tiles, cols), name...  48.9 us

profile of v6, /device:TPU:1, one launch (start us, length us, event | category | flops | bytes accessed | tf_op | source)
XLA Modules:
  0.0 669.9 jit_solution(3412568061054930881)
XLA Ops:
  0.6 63.0 %forward_0.1 = (f32[11,1024,384]{2,1,0:T(8,128)}, f32[11,1024,384]{2,1,0:T(8,128)}, bf16[1024,1536]{1,0:T(8,128)(2,1)}, bf16[1024,1536]{1,0:T(8,128)(2,1)}, bf16[1536,1024]{1,0:T(8,128)(2,1)}) custom-call(bf16[1024,1536]{1,0:T(8,128)(2,1)} %bitcast.109, bf16[2,1536,4224]{2,1,0:T(8,128)(2,1)} %wg.5, bf16[2,1536,4224]{2,1,0:T(8,128)(2,1)} %wu.5, ...), custom_call_target="tpu_custom_call" | custom-call | tf_op jit(solution)/shard_map/forward_0/pallas_call | solution.py:731
  63.6 76.2 %layer_1.1 = (bf16[11,2,1024,384]{3,2,1,0:T(8,128)(2,1)}, bf16[1536,1024]{1,0:T(8,128)(2,1)}, bf16[4224,768]{1,0:T(8,128)(2,1)}) custom-call(bf16[1024,1536]{1,0:T(8,128)(2,1)} %get-tuple-element.41.a, bf16[1024,1536]{1,0:T(8,128)(2,1)} %bitcast.105, bf16[2,1536,4224]{2,1,0:T(8,128)(2,1)} %wg.5, bf16[2,1536,4224]{2,1,0:T(8,128)(2,1)} %wu.5, ...), custom_call_target="tpu_custom_call" | custom-call | tf_op jit(solution)/shard_map/layer_1/pallas_call | solution.py:842
  139.8 48.9 %gate_up_1.1 = (bf16[1536,4224]{1,0:T(8,128)(2,1)}, bf16[3,4,4,24,384]{4,3,2,1,0:T(8,128)(2,1)}, bf16[3,4,4,24,384]{4,3,2,1,0:T(8,128)(2,1)}) custom-call(bf16[1536,1024]{1,0:T(8,128)(2,1)} %get-tuple-element.44.at, bf16[11,2,1024,384]{3,2,1,0:T(8,128)(2,1)} %get-tuple-element.42.ahead.behind.dgu, ...), custom_call_target="tpu_custom_call" | custom-call | tf_op jit(solution)/shard_map/gate_up_1/pallas_call | solution.py:1204
  188.7 57.5 %middle.1 = (bf16[1024,1536]{1,0:T(8,128)(2,1)}, bf16[72,768]{1,0:T(8,128)(2,1)}, bf16[3,4,4,8,1152]{4,3,2,1,0:T(8,128)(2,1)}, bf16[3,4,4,8,1024]{4,3,2,1,0:T(8,128)(2,1)}) custom-call(bf16[11,2,1024,384]{3,2,1,0:T(8,128)(2,1)} %get-tuple-element.42.ahead.behind.dgu, bf16[2,1536,4224]{2,1,0:T(8,128)(2,1)} %wg.5, bf16[2,1536,4224]{2,1,0:T(8,128)(2,1)} %wu.5, ...), custom_call_target="tpu_custom_call" | custom-call | tf_op jit(solution)/shard_map/middle/pallas_call | solution.py:1289
  246.2 75.1 %back_0.1 = (bf16[11,2,1024,384]{3,2,1,0:T(8,128)(2,1)}, bf16[4224,768]{1,0:T(8,128)(2,1)}, bf16[24,4224]{1,0:T(8,128)(2,1)}) custom-call(bf16[1024,1536]{1,0:T(8,128)(2,1)} %get-tuple-element.49.dh, f32[11,1024,384]{2,1,0:T(8,128)} %get-tuple-element.50.gate, f32[11,1024,384]{2,1,0:T(8,128)} %get-tuple-element.51.up, bf16[2,4224,1536]{2,1,0:T(8,128)(2,1)} %wd.5, ...), custom_call_target="tpu_custom_call" | custom-call | tf_op jit(solution)/shard_map/back_0/pallas_call | solution.py:1360
  321.3 99.9 %gate_up_0.1 = (bf16[24,4224]{1,0:T(8,128)(2,1)}, bf16[72,768]{1,0:T(8,128)(2,1)}) custom-call(bf16[1536,1024]{1,0:T(8,128)(2,1)} %get-tuple-element.40.at, bf16[11,2,1024,384]{3,2,1,0:T(8,128)(2,1)} %get-tuple-element.54.ahead.behind, bf16[11,2,1024,384]{3,2,1,0:T(8,128)(2,1)} %get-tuple-element.54.ahead.behind, bf16[4,4,264,768]{3,2,1,0:T(8,128)(2,1)} %bitcast.107), custom_call_target="tpu_custom_call" | custom-call | tf_op jit(solution)/shard_map/gate_up_0/pallas_call | solution.py:1147
  421.2 27.9 %update.1 = (bf16[2,24,4224]{2,1,0:T(8,128)(2,1)}, bf16[2,72,768]{2,1,0:T(8,128)(2,1)}, f32[792,128]{1,0:T(8,128)}, f32[792,128]{1,0:T(8,128)}, f32[792,128]{1,0...) custom-call(bf16[24,4224]{1,0:T(8,128)(2,1)} %get-tuple-element.56.refs_0_, ...), custom_call_target="tpu_custom_call" | custom-call | tf_op jit(solution)/shard_map/update/pallas_call | solution.py:597
  449.2 160.2 %gather.1 = (bf16[2,4,4,4,24,4224]{5,4,3,2,1,0:T(8,128)(2,1)}, bf16[2,4,4,4,24,4224]{5,4,3,2,1,0:T(8,128)(2,1)}, bf16[2,4,4,264,1536]{4,3,2,1,0:T(8,128)(2,1)}) custom-call(bf16[2,24,4224]{2,1,0:T(8,128)(2,1)} %get-tuple-element.60.new_gu, bf16[2,72,768]{2,1,0:T(8,128)(2,1)} %get-tuple-element.61.new_d), custom_call_target="tpu_custom_call" | custom-call | tf_op jit(solution)/shard_map/gather/pallas_call | solution.py:610
  609.4 0.0 slice-start
  609.4 0.0 slice-start.1
  609.5 0.0 slice-start.2
  609.5 0.0 slice-start.3
  609.5 23.9 %copy.29 = bf16[2,1536,4224]{2,1,0:T(8,128)(2,1)} copy(bf16[2,1536,4224]{2,1,0:T(8,128)(2,1)} %bitcast.104) | data formatting | bytes 51904512
  633.3 22.6 %copy.30 = bf16[2,1536,4224]{2,1,0:T(8,128)(2,1)} copy(bf16[2,1536,4224]{2,1,0:T(8,128)(2,1)} %bitcast.103) | data formatting | bytes 51904512
  655.9 0.0 slice-done
  655.9 0.0 slice-done.2
  656.0 9.4 %copy.31 = bf16[2,4224,1536]{2,1,0:T(8,128)(2,1)} copy(bf16[2,4224,1536]{2,1,0:T(8,128)(2,1)S(1)} %bitcast.102) | data formatting | bytes 51904512
  665.4 0.8 copy.32
  666.1 0.8 copy.33
  666.9 0.8 copy.34
  667.6 0.0 copy-done.2
  667.6 0.8 copy.35
  668.4 0.8 copy.36
  669.1 0.8 copy.37
  (20 shorter events, 0.0 us)
Async XLA Ops:
  609.4 46.5 %slice-start = ((s8[25952256]{0:T(1024)(128)(4,1)}), s8[4194304]{0:T(1024)(128)(4,1)S(1)}, s32[]{:S(2)}) async-start(s8[25952256]{0:T(1024)(128)(4,1)} %bitcast.100), calls=%async_computation | async-start | bytes 8388608
  609.4 46.5 %slice-start.1 = ((s8[25952256]{0:T(1024)(128)(4,1)}), s8[4194304]{0:T(1024)(128)(4,1)S(1)}, s32[]{:S(2)}) async-start(s8[25952256]{0:T(1024)(128)(4,1)} %bitcast.100), calls=%async_computation.1 | async-start | bytes 8388608
  609.5 46.4 %slice-start.2 = ((s8[25952256]{0:T(1024)(128)(4,1)}), s8[4194304]{0:T(1024)(128)(4,1)S(1)}, s32[]{:S(2)}) async-start(s8[25952256]{0:T(1024)(128)(4,1)} %bitcast.100), calls=%async_computation.2 | async-start | bytes 8388608
  609.5 46.4 %slice-start.3 = ((s8[25952256]{0:T(1024)(128)(4,1)}), s8[4194304]{0:T(1024)(128)(4,1)S(1)}, s32[]{:S(2)}) async-start(s8[25952256]{0:T(1024)(128)(4,1)} %bitcast.100), calls=%async_computation.3 | async-start | bytes 8388608
  633.3 22.6 %slice-start.4 = ((s8[25952256]{0:T(1024)(128)(4,1)}), s8[4194304]{0:T(1024)(128)(4,1)S(1)}, s32[]{:S(2)}) async-start(s8[25952256]{0:T(1024)(128)(4,1)} %bitcast.100), calls=%async_computation.4 | async-start | bytes 8388608
  633.3 22.6 %slice-start.5 = ((s8[25952256]{0:T(1024)(128)(4,1)}), s8[4194304]{0:T(1024)(128)(4,1)S(1)}, s32[]{:S(2)}) async-start(s8[25952256]{0:T(1024)(128)(4,1)} %bitcast.100), calls=%async_computation.5 | async-start | bytes 8388608
  633.3 22.6 %slice-start.6 = ((s8[25952256]{0:T(1024)(128)(4,1)}), s8[786432]{0:T(1024)(128)(4,1)S(1)}, s32[]{:S(2)}) async-start(s8[25952256]{0:T(1024)(128)(4,1)} %bitcast.100), calls=%async_computation.6 | async-start | bytes 1572864
  656.0 9.4 %copy-start.5 = (f32[792,128]{1,0:T(8,128)S(1)}, f32[792,128]{1,0:T(8,128)}, u32[]{:S(2)}) copy-start(f32[792,128]{1,0:T(8,128)} %get-tuple-element.65) | copy-start | bytes 1216516
  656.0 10.2 %copy-start.4 = (f32[792,128]{1,0:T(8,128)S(1)}, f32[792,128]{1,0:T(8,128)}, u32[]{:S(2)}) copy-start(f32[792,128]{1,0:T(8,128)} %get-tuple-element.66) | copy-start | bytes 1216516
  656.0 10.9 %copy-start.3 = (f32[792,128]{1,0:T(8,128)S(1)}, f32[792,128]{1,0:T(8,128)}, u32[]{:S(2)}) copy-start(f32[792,128]{1,0:T(8,128)} %get-tuple-element.67) | copy-start | bytes 1216516
  656.0 11.6 %copy-start.2 = (f32[792,128]{1,0:T(8,128)S(1)}, f32[792,128]{1,0:T(8,128)}, u32[]{:S(2)}) copy-start(f32[792,128]{1,0:T(8,128)} %get-tuple-element.68) | copy-start | bytes 1216516
  656.0 12.4 %copy-start.1 = (f32[792,128]{1,0:T(8,128)S(1)}, f32[792,128]{1,0:T(8,128)}, u32[]{:S(2)}) copy-start(f32[792,128]{1,0:T(8,128)} %get-tuple-element.69) | copy-start | bytes 1216516
  656.0 13.1 %copy-start = (f32[792,128]{1,0:T(8,128)S(1)}, f32[792,128]{1,0:T(8,128)}, u32[]{:S(2)}) copy-start(f32[792,128]{1,0:T(8,128)} %get-tuple-element.70) | copy-start | bytes 1216516

commit v7 on v6

--- a/solution.py
+++ b/solution.py
@@ -22,6 +22,14 @@
         self.core = lax.rem(me, 2)
         chip = lax.div(me, 2)
         self.at = (lax.div(chip, SIDE * SIDE), lax.rem(lax.div(chip, SIDE), SIDE), lax.rem(chip, SIDE))
+        self.ways = [1 + 2 * lax.rem(way + self.core, 2) for way in range(2)]
+        self.onwards = {(axis, way): self.device(axis, self.ways[way]) for axis in range(3) for way in range(2)}
+        self.blocks = {
+            (axis, way, hops): lax.rem(self.at[axis] + hops * (SIDE - self.ways[way]), SIDE)
+            for axis in range(3)
+            for way in range(2)
+            for hops in range(1, 5)
+        }
 
     def device(self, axis=None, off=0, core=None):
         at = list(self.at)
@@ -34,10 +42,12 @@
         return self.device(core=1 - self.core)
 
     def onward(self, way):
-        return 1 + 2 * lax.rem(way + self.core, 2)
+        return self.ways[way]
 
     def block(self, axis, way, hops):
-        return lax.rem(self.at[axis] + hops * (SIDE - self.onward(way)), SIDE)
+        if isinstance(hops, int) and hops:
+            return self.blocks[axis, way, hops]
+        return lax.rem(self.at[axis] + hops * (SIDE - self.ways[way]), SIDE)
 
 
 def signal_all(devices):
@@ -88,7 +98,7 @@
 
     def send(self, axis, way, src, landing, key, sems):
         src = landing if src is None else src
-        return put(src, landing, sems[0].at[key], sems[1].at[key], self.place.device(axis, self.place.onward(way)))
+        return put(src, landing, sems[0].at[key], sems[1].at[key], self.place.onwards[axis, way])
 
 
 class First(Rings):
@@ -243,9 +253,9 @@
         self.place, self.bufs, self.sems, self.outs, self.copy_sems = place, bufs, sems, outs, copy_sems
 
     @staticmethod
-    def scratch(gate_cols, down_cols):
-        bufs = [pltpu.VMEM((2, SIDE, SIDE, SIDE, 24, gate_cols), BF16), pltpu.VMEM((2, SIDE, SIDE, SIDE, 72, down_cols), BF16)]
-        return bufs + [pltpu.SemaphoreType.DMA((2, 3, 2, 6, 3))] * 4 + [pltpu.SemaphoreType.DMA((2,))] * 3
+    def scratch(down_cols):
+        buf = pltpu.VMEM((2, SIDE, SIDE, SIDE, 72, down_cols), BF16)
+        return [buf] + [pltpu.SemaphoreType.DMA((2, 3, 2, 6, 3))] * 4 + [pltpu.SemaphoreType.DMA((2,))] * 3
 
     def part(self, kind, t, way):
         rows, cols = self.bufs[kind].shape[-2:]
@@ -265,7 +275,7 @@
             axis, values = order[2], [ALL, self.behind(t, way, 1, line - 2), self.behind(t, way, 2, hops)]
         ref = self.bufs[kind].at[(l, *index(order, values), *self.part(kind, t, way))]
         key = (l, t, way, line, n)
-        return put(ref, ref, self.sems[2 * kind].at[key], self.sems[2 * kind + 1].at[key], place.device(axis, place.onward(way)))
+        return put(ref, ref, self.sems[2 * kind].at[key], self.sems[2 * kind + 1].at[key], place.onwards[axis, way])
 
     def copies(self, kind, l, t, way, b, c):
         order = ORDERS[t]
@@ -288,18 +298,11 @@
 
     def copy_out(self, kind, l, t, way, b, c):
         local, send, recv = self.copy_sems
-
-        def both(out):
-            for pair in self.copies(kind, l, t, way, b, c):
-                src, dst = pair(out)
+        for pair in self.copies(kind, l, t, way, b, c):
+            src, dst = pair(self.outs[kind])
+            if kind:
                 pltpu.make_async_copy(src, dst, local.at[kind]).start()
-                put(src, dst, send.at[kind], recv.at[kind], self.place.partner()).start()
-
-        if kind:
-            both(self.outs[2])
-        else:
-            for core in range(2):
-                pl.when(self.place.core == core)(lambda core=core: both(self.outs[core]))
+            put(src, dst, send.at[kind], recv.at[kind], self.place.partner()).start()
 
     def parts(self):
         return [(kind, t, way) for kind in range(2) for t in range(3) for way in range(2)]
@@ -354,9 +357,10 @@
     def drain(self):
         local, send, recv = self.copy_sems
         half = self.bufs[1].shape[-1]
-        columns = self.outs[2].at[:, :, :, :, pl.ds(0, half)]
+        columns = self.outs[1].at[:, :, :, :, pl.ds(0, half)]
         for kind, whole in ((0, self.outs[0]), (1, columns)):
-            pltpu.make_async_copy(whole, whole, local.at[kind]).wait()
+            if kind:
+                pltpu.make_async_copy(whole, whole, local.at[kind]).wait()
             copy = put(whole, whole, send.at[kind], recv.at[kind], self.place.partner())
             copy.wait_send()
             copy.wait_recv()
@@ -372,14 +376,16 @@
         lax.fori_loop(0, 6, sent, 0)
 
 
-def update_kernel(count, *refs):
+def finish_kernel(count, *refs):
     sums_gu, sums_d, m_in, v_in, w_in = refs[0:2], refs[2:4], refs[4:7], refs[7:10], refs[10:13]
-    new_gu, new_d, m_out, v_out = refs[13], refs[14], refs[15:18], refs[18:21]
-    moments_gu, moments_d, old_gu, old_d, other_d, tiles = refs[21:27]
-    load_sem, early_send, early_recv, norm_send, norm_recv, late_local, late_send, late_recv = refs[27:35]
+    own_gu, w_out, m_out, v_out = refs[13], refs[14:16], refs[16:19], refs[19:22]
+    moments_gu, moments_d, old_gu, old_d, other_d, tiles = refs[22:28]
+    load_sem, early_send, early_recv, norm_send, norm_recv, late_local, late_send, late_recv = refs[28:36]
+    gather_refs = refs[36:]
     place = Place()
     x, y, z = place.at
     core = place.core
+    gather = Gather(place, (own_gu, gather_refs[0]), gather_refs[1:5], w_out, gather_refs[5:8])
     partner = place.partner()
     gate_tiles, down_tiles = sums_gu[0].shape[1] // LANES, sums_d[0].shape[1] // LANES
     gate_stride, down_stride = 2 * gate_tiles, 4 * down_tiles
@@ -508,7 +514,7 @@
                 rows = pl.ds(8 * t, 8)
                 g = sums_gu[l][rows, lanes].astype(F32) * factor
                 step = moments(moments_gu, 8 * t * gate_stride + 2 * j + l, gate_stride, g)
-                new_gu[l, rows, lanes] = weight(old_gu[l, rows, lanes], step)
+                gather.bufs[0][l, x, y, z, rows, lanes] = weight(old_gu[l, rows, lanes], step)
             return 0
 
         lax.fori_loop(0, gate_tiles, gate_up, 0, unroll=3)
@@ -520,10 +526,11 @@
                 start = (PREV + 8 * i) * down_stride + 2 * j + l
                 g = sums_d[l][rows, lanes].astype(F32) * factor
                 step = moments(moments_d, start + 2 * down_tiles * core, down_stride, g)
-                new_d[l, rows, lanes] = weight(old_d[l, rows, lanes], step)
+                gather.bufs[1][l, x, y, z, rows, lanes] = weight(old_d[l, rows, lanes], step)
             return 0
 
         lax.fori_loop(0, 9, down, 0)
+        gather.own(l)
     for l in range(2):
 
         def down_other(i, _, l=l):
@@ -546,6 +553,8 @@
                 put(gate_rows(i, 1 - core), out[c], late_send.at[i], late_recv.at[i], partner).start()
 
         pltpu.make_async_copy(down_rows(i, own_rows, DOWN_ROWS), out[2], late_local.at[2 + i]).start()
+    gather.first_axis()
+    gather.other_axes()
     for i, out in enumerate((m_out, v_out)):
         pltpu.make_async_copy(gate_rows(i, core), out[0], late_local.at[i]).wait()
         pltpu.make_async_copy(down_rows(i, own_rows, DOWN_ROWS), out[2], late_local.at[2 + i]).wait()
@@ -562,23 +571,10 @@
                 rows = down_rows(i, 0, PREV)
                 put(rows, rows, early_send.at[4 + 2 * i + c], early_recv.at[4 + i], following[c]).wait_send()
 
-
-def gather_kernel(new_gu, new_d, *refs):
-    w_out, load_sem, rest = refs[:3], refs[3], refs[4:]
-    place = Place()
-    gather = Gather(place, rest[:2], rest[2:6], w_out, rest[6:9])
-    loads = [pltpu.make_async_copy(new, buf.at[(ALL, *place.at)], load_sem.at[i]) for i, (new, buf) in enumerate(zip((new_gu, new_d), rest[:2]))]
-    begin(loads)
-    signal_all(near(place))
-    end(loads)
-    for l in range(2):
-        gather.own(l)
-    gather.first_axis()
-    gather.other_axes()
     gather.drain()
 
 
-def update_call(count, collective_id, sums_gu, sums_d, m, v, w):
+def finish_call(count, collective_id, sums_gu, sums_d, m, v, w):
     gate_cols, down_half = sums_gu[0].shape[1], sums_d[0].shape[1]
     operands = [*sums_gu, *sums_d, *m, *v, *w]
     hbm, vmem = pl.BlockSpec(memory_space=pltpu.HBM), pl.BlockSpec(memory_space=pltpu.VMEM)
@@ -593,29 +589,67 @@
         pltpu.VMEM((4, SIDE, 8, LANES), F32),
         dma((6,)), dma((10,)), dma((8,)), dma((12,)), dma((12,)), dma((4,)), dma((2,)), dma((2,)),
     ]
-    new = [jax.ShapeDtypeStruct((2, 24, gate_cols), BF16), jax.ShapeDtypeStruct((2, 72, down_half), BF16)]
     return pl.pallas_call(
-        functools.partial(update_kernel, count),
-        name="update",
-        out_shape=[*new, *[jax.ShapeDtypeStruct(t.shape, t.dtype) for t in (*m, *v)]],
+        functools.partial(finish_kernel, count),
+        name="finish",
+        out_shape=[pltpu.VMEM(w[0].shape, BF16), *[jax.ShapeDtypeStruct(t.shape, t.dtype) for t in (w[0], w[2], *m, *v)]],
         in_specs=[vmem] * 4 + [hbm] * 9,
-        out_specs=[vmem] * 2 + [hbm] * 6,
-        scratch_shapes=scratch,
-        compiler_params=pltpu.CompilerParams(collective_id=collective_id, has_side_effects=True, vmem_limit_bytes=VMEM_LIMIT),
+        out_specs=[vmem] + [hbm] * 8,
+        scratch_shapes=scratch + Gather.scratch(down_half),
+        compiler_params=pltpu.CompilerParams(collective_id=collective_id, has_side_effects=True, vmem_limit_bytes=26 * 1024 * 1024),
+        cost_estimate=pl.CostEstimate(flops=10**9, bytes_accessed=10**8, transcendentals=0),
     )(*operands)
 
 
-def gather_call(collective_id, new_gu, new_d, w):
+def write_kernel(bounces, own, other, down, gate_out, up_out, down_out, bounce, own_sem, in_sem, out_sem):
+    core = lax.rem(lax.axis_index("dp"), 2)
+    places = [(l, x, y) for l in range(2) for x in range(SIDE) for y in range(SIDE)]
+    pieces = [(other, None, at) for at in places] + [(down, down_out, at) for at in places]
+
+    def slot(i):
+        source = pieces[i][0]
+        return bounce[0 if source is other else 1].at[i % bounces]
+
+    def read(i):
+        source, _, at = pieces[i]
+        return pltpu.make_async_copy(source.at[at], slot(i), in_sem.at[i % bounces])
+
+    def write(i, out=None):
+        _, to, at = pieces[i]
+        return pltpu.make_async_copy(slot(i), (out if to is None else to).at[at], out_sem.at[i % bounces])
+
+    for i in range(bounces):
+        read(i).start()
+    for c, (mine, others) in enumerate(((gate_out, up_out), (up_out, gate_out))):
+
+        @pl.when(core == c)
+        def _(mine=mine, others=others):
+            pltpu.make_async_copy(own, mine, own_sem).start()
+            for i in range(len(pieces)):
+                read(i).wait()
+                write(i, others).start()
+                done = i - bounces // 2
+                if done >= 0 and done + bounces < len(pieces):
+                    write(done, others).wait()
+                    read(done + bounces).start()
+
+    for i in range(len(pieces) - bounces, len(pieces)):
+        write(i, gate_out).wait()
+    pltpu.make_async_copy(own, gate_out, own_sem).wait()
+
+
+def write_call(own, other, down):
     hbm = pl.BlockSpec(memory_space=pltpu.HBM)
+    bounces, dma = 8, pltpu.SemaphoreType.DMA
     return pl.pallas_call(
-        gather_kernel,
-        name="gather",
-        out_shape=[jax.ShapeDtypeStruct(t.shape, t.dtype) for t in w],
-        in_specs=[hbm] * 2,
+        lambda *refs: write_kernel(bounces, *refs[:6], refs[6:8], *refs[8:]),
+        name="write",
+        out_shape=[jax.ShapeDtypeStruct(t.shape, BF16) for t in (other, other, down)],
+        in_specs=[pl.BlockSpec(memory_space=pl.ANY), hbm, hbm],
         out_specs=[hbm] * 3,
-        scratch_shapes=[pltpu.SemaphoreType.DMA((2,)), *Gather.scratch(new_gu.shape[2], new_d.shape[2])],
-        compiler_params=pltpu.CompilerParams(collective_id=collective_id, has_side_effects=True, vmem_limit_bytes=VMEM_LIMIT),
-    )(new_gu, new_d)
+        scratch_shapes=[pltpu.VMEM((bounces, *t.shape[3:]), BF16) for t in (other, down)] + [dma, dma((bounces,)), dma((bounces,))],
+        compiler_params=pltpu.CompilerParams(vmem_limit_bytes=14 * 1024 * 1024),
+    )(own, other, down)
 
 
 TILE = 384
@@ -897,7 +931,7 @@
         else:
             src = self.slots[way].at[(t, 2, c, *second(t, self.place.block(axis, way, 1)))]
         key = (c, 3 * phase + n)
-        return put(src, slots.at[t, n, c], self.send.at[key], self.recv.at[key], self.place.device(axis, self.place.onward(way)))
+        return put(src, slots.at[t, n, c], self.send.at[key], self.recv.at[key], self.place.onwards[axis, way])
 
     def direct(self, t, way, off, c):
         axis = ORDERS[t][2]
@@ -1024,7 +1058,7 @@
             src = slots.at[t, n - 1]
         send, recv = self.sems[2 * phase - 2 : 2 * phase]
         key = (t, way, n)
-        return put(src, slots.at[t, n], send.at[key], recv.at[key], self.place.device(axis, self.place.onward(way)))
+        return put(src, slots.at[t, n], send.at[key], recv.at[key], self.place.onwards[axis, way])
 
     def start(self, phase):
         for t, way in self.pairs():
@@ -1408,8 +1442,8 @@
         views = [(2, SIDE, SIDE, SIDE, GATE_ROWS, ff)] * 2 + [(2, SIDE, SIDE, 4 * 66, d)]
         w = [t.reshape(view) for t, view in zip((wg, wu, wd), views, strict=True)]
         m, v = [flat(t) for t in (mg, mu, md)], [flat(t) for t in (vg, vu, vd)]
-        new_gu, new_d, *moments = update_call(3 * layers * d * ff, 6, [sum_gu0, sum_gu1], [sum_down0, sum_down1], m, v, w)
-        out = [*gather_call(7, new_gu, new_d, w), *moments]
+        own, other, down, *moments = finish_call(3 * layers * d * ff, 6, [sum_gu0, sum_gu1], [sum_down0, sum_down1], m, v, w)
+        out = [*write_call(own, other, down), *moments]
         new = [t.reshape(like.shape) for t, like in zip(out[:3], (wg, wu, wd), strict=True)]
         return (*new, *[unflat(t, like.shape) for t, like in zip(out[3:], (mg, mu, md, vg, vu, vd), strict=True)])
 

time: 670 us -> 652 us (0.973)
  local copies, waits for them, and re-layouts: 60.3 us -> 6.33 us
  Pallas kernels: 609 us -> 645 us
    unnamed x35 -> x14, local copies, waits for them, and re-layouts: 60.3 us -> 6.33 us
    pallas_call x2, Pallas kernels: 188 us -> 224 us  [the longest x1 181 us: finish_call(): pl.pallas_call(functools.partial(finish_kernel, count), name='finish', ou...]
where the time goes in v7:
time: 652 us
  Pallas kernels  645 us (99%)
    pallas_call x1, Pallas kernels, finish_call(): pl.pallas_call(functools.partial(finish_kernel, count), name='finish', ou...  181 us
    pallas_call x1, Pallas kernels, gate_up_call(): pl.pallas_call(functools.partial(gate_up_kernel, tiles, phases, cols), na...  99.3 us
    pallas_call x1, Pallas kernels, layer_call(): pl.pallas_call(functools.partial(layer_kernel, tiles), name='layer_1', gr...  76.2 us
    pallas_call x1, Pallas kernels, back_call(): pl.pallas_call(functools.partial(back_kernel, tiles, ff), name='back_0',...  75.7 us
    pallas_call x1, Pallas kernels, forward_call(): pl.pallas_call(functools.partial(forward_kernel, tiles), name='forward_0'...  63 us
    pallas_call x1, Pallas kernels, middle_call(): pl.pallas_call(functools.partial(middle_kernel, steps, ff, down_cols), na...  57.8 us
    pallas_call x1, Pallas kernels, gate_up_first_call(): pl.pallas_call(functools.partial(gate_up_first_kernel, tiles, cols), name...  49.3 us
    pallas_call x1, Pallas kernels, write_call(): pl.pallas_call(lambda *refs: write_kernel(bounces, *refs[:6], refs[6:8],...  43.2 us

profile of v7, /device:TPU:1, one launch (start us, length us, event | category | flops | bytes accessed | tf_op | source)
XLA Modules:
  0.0 652.1 jit_solution(10183249428737359935)
XLA Ops:
  0.6 63.0 %forward_0.1 = (f32[11,1024,384]{2,1,0:T(8,128)}, f32[11,1024,384]{2,1,0:T(8,128)}, bf16[1024,1536]{1,0:T(8,128)(2,1)}, bf16[1024,1536]{1,0:T(8,128)(2,1)}, bf16[1536,1024]{1,0:T(8,128)(2,1)}) custom-call(bf16[1024,1536]{1,0:T(8,128)(2,1)} %bitcast.110, bf16[2,1536,4224]{2,1,0:T(8,128)(2,1)} %wg.5, bf16[2,1536,4224]{2,1,0:T(8,128)(2,1)} %wu.5, ...), custom_call_target="tpu_custom_call" | custom-call | tf_op jit(solution)/shard_map/forward_0/pallas_call | solution.py:765
  63.6 76.2 %layer_1.1 = (bf16[11,2,1024,384]{3,2,1,0:T(8,128)(2,1)}, bf16[1536,1024]{1,0:T(8,128)(2,1)}, bf16[4224,768]{1,0:T(8,128)(2,1)}) custom-call(bf16[1024,1536]{1,0:T(8,128)(2,1)} %get-tuple-element.42.a, bf16[1024,1536]{1,0:T(8,128)(2,1)} %bitcast.106, bf16[2,1536,4224]{2,1,0:T(8,128)(2,1)} %wg.5, bf16[2,1536,4224]{2,1,0:T(8,128)(2,1)} %wu.5, ...), custom_call_target="tpu_custom_call" | custom-call | tf_op jit(solution)/shard_map/layer_1/pallas_call | solution.py:876
  139.8 49.3 %gate_up_1.1 = (bf16[1536,4224]{1,0:T(8,128)(2,1)}, bf16[3,4,4,24,384]{4,3,2,1,0:T(8,128)(2,1)}, bf16[3,4,4,24,384]{4,3,2,1,0:T(8,128)(2,1)}) custom-call(bf16[1536,1024]{1,0:T(8,128)(2,1)} %get-tuple-element.45.at, bf16[11,2,1024,384]{3,2,1,0:T(8,128)(2,1)} %get-tuple-element.43.ahead.behind.dgu, ...), custom_call_target="tpu_custom_call" | custom-call | tf_op jit(solution)/shard_map/gate_up_1/pallas_call | solution.py:1238
  189.1 57.8 %middle.1 = (bf16[1024,1536]{1,0:T(8,128)(2,1)}, bf16[72,768]{1,0:T(8,128)(2,1)}, bf16[3,4,4,8,1152]{4,3,2,1,0:T(8,128)(2,1)}, bf16[3,4,4,8,1024]{4,3,2,1,0:T(8,128)(2,1)}) custom-call(bf16[11,2,1024,384]{3,2,1,0:T(8,128)(2,1)} %get-tuple-element.43.ahead.behind.dgu, bf16[2,1536,4224]{2,1,0:T(8,128)(2,1)} %wg.5, bf16[2,1536,4224]{2,1,0:T(8,128)(2,1)} %wu.5, ...), custom_call_target="tpu_custom_call" | custom-call | tf_op jit(solution)/shard_map/middle/pallas_call | solution.py:1323
  246.9 75.7 %back_0.1 = (bf16[11,2,1024,384]{3,2,1,0:T(8,128)(2,1)}, bf16[4224,768]{1,0:T(8,128)(2,1)}, bf16[24,4224]{1,0:T(8,128)(2,1)}) custom-call(bf16[1024,1536]{1,0:T(8,128)(2,1)} %get-tuple-element.50.dh, f32[11,1024,384]{2,1,0:T(8,128)} %get-tuple-element.51.gate, f32[11,1024,384]{2,1,0:T(8,128)} %get-tuple-element.52.up, bf16[2,4224,1536]{2,1,0:T(8,128)(2,1)} %wd.5, ...), custom_call_target="tpu_custom_call" | custom-call | tf_op jit(solution)/shard_map/back_0/pallas_call | solution.py:1394
  322.6 0.0 copy-start
  322.7 0.0 copy-start.2
  322.7 99.3 %gate_up_0.1 = (bf16[24,4224]{1,0:T(8,128)(2,1)}, bf16[72,768]{1,0:T(8,128)(2,1)}) custom-call(bf16[1536,1024]{1,0:T(8,128)(2,1)} %get-tuple-element.41.at, bf16[11,2,1024,384]{3,2,1,0:T(8,128)(2,1)} %get-tuple-element.55.ahead.behind, bf16[11,2,1024,384]{3,2,1,0:T(8,128)(2,1)} %get-tuple-element.55.ahead.behind, bf16[4,4,264,768]{3,2,1,0:T(8,128)(2,1)} %bitcast.108), custom_call_target="tpu_custom_call" | custom-call | tf_op jit(solution)/shard_map/gate_up_0/pallas_call | solution.py:1181
  422.0 0.0 copy-done
  422.0 0.0 copy-done.2
  422.0 0.0 copy-start.1
  422.0 0.9 copy-done.1
  422.9 0.0 copy-start.3
  422.9 0.9 copy-done.3
  423.8 180.5 %finish.1 = (bf16[2,4,4,4,24,4224]{5,4,3,2,1,0:T(8,128)(2,1)S(1)}, bf16[2,4,4,4,24,4224]{5,4,3,2,1,0:T(8,128)(2,1)}, bf16[2,4,4,264,1536]{4,3,2,1,0:T(8,128)(2,1...) custom-call(bf16[24,4224]{1,0:T(8,128)(2,1)S(1)} %copy-done.1, ...), custom_call_target="tpu_custom_call" | custom-call | flops 1000000000 | bytes 100000000 | tf_op jit(solution)/shard_map/finish/pallas_call | solution.py:592
  604.4 43.2 %write.1 = (bf16[2,4,4,4,24,4224]{5,4,3,2,1,0:T(8,128)(2,1)}, bf16[2,4,4,4,24,4224]{5,4,3,2,1,0:T(8,128)(2,1)}, bf16[2,4,4,264,1536]{4,3,2,1,0:T(8,128)(2,1)}) custom-call(bf16[2,4,4,4,24,4224]{5,4,3,2,1,0:T(8,128)(2,1)S(1)} %get-tuple-element.61.refs_0_, bf16[2,4,4,4,24,4224]{5,4,3,2,1,0:T(8,128)(2,1)} %get-tuple-element.62.refs_1_, ...), custom_call_target="tpu_custom_call" | custom-call | tf_op jit(solution)/shard_map/write/pallas_call | solution.py:644
  647.6 0.8 copy.26
  648.3 0.7 copy.27
  649.1 0.7 copy.28
  649.8 0.7 copy.29
  650.6 0.7 copy.30
  651.3 0.7 copy.31
Async XLA Ops:
  322.6 99.3 %copy-start = (bf16[24,4224]{1,0:T(8,128)(2,1)S(1)}, bf16[24,4224]{1,0:T(8,128)(2,1)}, u32[]{:S(2)}) copy-start(bf16[24,4224]{1,0:T(8,128)(2,1)} %get-tuple-element.58.refs_1_) | copy-start | bytes 608260
  322.7 99.3 %copy-start.2 = (bf16[72,768]{1,0:T(8,128)(2,1)S(1)}, bf16[72,768]{1,0:T(8,128)(2,1)}, u32[]{:S(2)}) copy-start(bf16[72,768]{1,0:T(8,128)(2,1)} %get-tuple-element.60.refs_3_) | copy-start | bytes 331780
  422.0 0.9 copy-start.1
  422.9 0.9 copy-start.3

commit v8 on v7

--- a/solution.py
+++ b/solution.py
@@ -1149,9 +1149,8 @@
     stream.late(j, out)
     if phases == 3:
         pl.when(j == 0)(lambda: end(loads))
-        pl.when(j < 8)(lambda: spread(j, 8, 16, first.tick))
-        pl.when(j >= 8)(lambda: down.tick(j - 8))
-        pl.when(j == 15)(lambda: down.result(out_down))
+        pl.when(j <= tiles + 1)(lambda: spread(j, tiles + 2, 16, first.tick))
+        pl.when(j > tiles + 1)(lambda: down.tick(j - tiles - 2))
 
     @pl.when(j == stream.last_step())
     def _():
@@ -1161,6 +1160,7 @@
             stream.drain()
             end(saves)
         else:
+            down.result(out_down)
             stream.drain()
             first.drain()
             down.drain()
@@ -1195,14 +1195,14 @@
     )(at, dgu, dgu, *sum_down)
 
 
-def gate_up_first_kernel(tiles, cols, at, ahead, behind, sum_down, out, half0, half1, *rest):
+def gate_up_first_kernel(tiles, cols, at, ahead, behind, sum_down, out, out_down, *rest):
     j = pl.program_id(0)
     place = Place()
     core = place.core
     pair = PairSum(place, tiles, *rest[:4])
     first = First.of(place, DOWN_WINDOW, cols, rest[4:9])
-    load_sem, save_sem = rest[9:11]
-    loads = loads_down(sum_down, first, load_sem)
+    down = Rest.of(place, DOWN_WINDOW, cols, first.results(), rest[9:17])
+    loads = loads_down(sum_down, first, rest[17])
 
     @pl.when(j == 0)
     def _():
@@ -1221,14 +1221,14 @@
     pl.when(j < tiles)(lambda: pair.copy(j).start())
 
     pl.when(j == 0)(lambda: end(loads))
-    spread(j, tiles + 2, 16, first.tick)
+    pl.when(j <= tiles - 5)(lambda: spread(j, tiles - 4, 16, first.tick))
+    pl.when(j >= tiles - 5)(lambda: down.tick(j - tiles + 5))
 
     @pl.when(j == tiles + 1)
     def _():
-        saves = copies(first.results(), (half0, half1), save_sem)
-        begin(saves)
+        down.result(out_down)
         first.drain()
-        end(saves)
+        down.drain()
 
 
 def gate_up_first_call(name, collective_id, at, dgu, sum_down):
@@ -1245,32 +1245,24 @@
             spec((1, 2, tokens, TILE), lambda j: (before(j), 0, 0, 0)),
             HBM,
         ],
-        out_specs=[spec((d, TILE), lambda j: (0, before(j))), HBM, HBM],
-        out_shape=[jax.ShapeDtypeStruct((d, tiles * TILE), BF16)]
-        + [jax.ShapeDtypeStruct(s, BF16) for s in half_sums(DOWN_WINDOW, cols)],
-        scratch_shapes=[*PairSum.scratch(tiles, d, TILE), *First.scratch(DOWN_WINDOW, cols), dma((SIDE,)), dma((2,))],
+        out_specs=[spec((d, TILE), lambda j: (0, before(j))), whole((DOWN_WINDOW, cols))],
+        out_shape=[jax.ShapeDtypeStruct(s, BF16) for s in ((d, tiles * TILE), (DOWN_WINDOW, cols))],
+        scratch_shapes=[
+            *PairSum.scratch(tiles, d, TILE),
+            *First.scratch(DOWN_WINDOW, cols),
+            *Rest.scratch(DOWN_WINDOW, cols),
+            dma((SIDE,)),
+        ],
         compiler_params=params(collective_id),
     )(at, dgu, dgu, sum_down)
 
 
-def column_halves(cols):
-    return ways_of(cols)
-
-
-def load_columns(source, first, part, sem):
-    start, width = part
-    return [pltpu.make_async_copy(source.at[:, :, :, :, pl.ds(start, width)], first.held, sem)]
-
-
-def middle_kernel(steps, ff, down_cols, dgu, wg, wu, h, dy, sum_gu, down0, down1, dh, out_down, half0, half1, acc_g, acc_u, *rest):
+def middle_kernel(steps, ff, dgu, wg, wu, h, dy, sum_gu, dh, half0, half1, acc_g, acc_u, *rest):
     j = pl.program_id(0)
     place = Place()
-    part = column_halves(ff)[0]
-    first = First.of(place, GATE_ROWS, part[1], rest[:5])
-    before = rest[5:7]
-    down = Rest.of(place, DOWN_WINDOW, down_cols, before, rest[7:15])
-    load_sem, save_sem = rest[15:17]
-    loads = copies((down0, down1), before, load_sem) + load_columns(sum_gu, first, part, load_sem.at[2])
+    first = First.of(place, GATE_ROWS, ff, rest[:5])
+    load_sem, save_sem = rest[5:7]
+    loads = [pltpu.make_async_copy(sum_gu.at[x], first.held.at[x], load_sem.at[x]) for x in range(SIDE)]
 
     @pl.when(j == 0)
     def _():
@@ -1290,15 +1282,12 @@
     pl.when(j == steps - 1)(lambda: in_rows(h.shape[0], ROWS, lambda r: add_up(r, False)))
 
     pl.when(j == 0)(lambda: end(loads))
-    down.tick(j)
     spread(j, steps, 16, first.tick)
 
     @pl.when(j == steps - 1)
     def _():
-        lax.fori_loop(steps, 7, lambda i, _: (down.tick(i), 0)[1], 0)
         saves = copies(first.results(), (half0, half1), save_sem)
         begin(saves)
-        down.result(out_down)
 
         def rows(r):
             wide = h[r, :].astype(F32)
@@ -1309,45 +1298,35 @@
 
         in_rows(h.shape[0], 32, rows)
         first.drain()
-        down.drain()
         end(saves)
 
 
-def middle_call(collective_id, dgu, wg, wu, h, dy, sum_gu, down_halves):
+def middle_call(collective_id, dgu, wg, wu, h, dy, sum_gu):
     tokens, d = h.shape
-    tiles, dma, down_cols = dgu.shape[0], pltpu.SemaphoreType.DMA, d // 2
+    tiles, dma = dgu.shape[0], pltpu.SemaphoreType.DMA
     ff = tiles * TILE
     steps = (tiles + 1) // 2
-    width = column_halves(ff)[0][1]
     w_in = spec((1, d, 2 * TILE), lambda j: (1, 0, j))
     return pl.pallas_call(
-        functools.partial(middle_kernel, steps, ff, down_cols),
+        functools.partial(middle_kernel, steps, ff),
         name="middle",
         grid=(steps,),
-        in_specs=[spec((2, 2, tokens, TILE), lambda j: (j, 0, 0, 0)), w_in, w_in, whole((tokens, d)), whole((tokens, d))] + [HBM] * 3,
-        out_specs=[whole((tokens, d)), whole((DOWN_WINDOW, down_cols)), HBM, HBM],
-        out_shape=[jax.ShapeDtypeStruct(s, BF16) for s in ((tokens, d), (DOWN_WINDOW, down_cols), *half_sums(GATE_ROWS, width))],
-        scratch_shapes=[pltpu.VMEM((tokens, d), F32)] * 2
-        + First.scratch(GATE_ROWS, width)
-        + [pltpu.VMEM(t.shape, BF16) for t in down_halves]
-        + Rest.scratch(DOWN_WINDOW, down_cols)
-        + [dma((3,)), dma((2,))],
+        in_specs=[spec((2, 2, tokens, TILE), lambda j: (j, 0, 0, 0)), w_in, w_in, whole((tokens, d)), whole((tokens, d)), HBM],
+        out_specs=[whole((tokens, d)), HBM, HBM],
+        out_shape=[jax.ShapeDtypeStruct(s, BF16) for s in ((tokens, d), *half_sums(GATE_ROWS, ff))],
+        scratch_shapes=[pltpu.VMEM((tokens, d), F32)] * 2 + First.scratch(GATE_ROWS, ff) + [dma((SIDE,)), dma((2,))],
         compiler_params=params(collective_id),
-    )(dgu, wg, wu, h, dy, sum_gu, *down_halves)
-
-
-def back_kernel(tiles, ff, dh, gate, up, wd, gate0, gate1, sum_gu, dgu, out, out_gu, p, dps, *rest):
+    )(dgu, wg, wu, h, dy, sum_gu)
+
+
+def back_kernel(tiles, ff, dh, gate, up, wd, gate0, gate1, dgu, out, out_gu, p, dps, *rest):
     j = pl.program_id(0)
     place = Place()
     core, half = place.core, dh.shape[1] // 2
-    parts = column_halves(ff)
     pair = PairSum(place, tiles, *rest[:4])
     before = rest[4:6]
-    rest_a = Rest.of(place, GATE_ROWS, parts[0][1], before, rest[6:14])
-    first = First.of(place, GATE_ROWS, parts[1][1], rest[14:19])
-    rest_b = Rest.of(place, GATE_ROWS, parts[1][1], first.results(), rest[19:27])
-    load_sem = rest[27]
-    loads = copies((gate0, gate1), before, load_sem) + load_columns(sum_gu, first, parts[1], load_sem.at[2])
+    sums = Rest.of(place, GATE_ROWS, ff, before, rest[6:14])
+    loads = copies((gate0, gate1), before, rest[14])
 
     @pl.when(j == 0)
     def _():
@@ -1371,31 +1350,26 @@
         pair.copy(j).start()
 
     pl.when(j == 0)(lambda: end(loads))
-    rest_a.tick(j)
-    pl.when(j < 6)(lambda: spread(j, 6, 16, first.tick))
-    pl.when(j >= 5)(lambda: rest_b.tick(j - 5))
+    sums.tick(j)
 
     @pl.when(j == tiles + 1)
     def _():
-        for sums, (start, width) in ((rest_a, parts[0]), (rest_b, parts[1])):
-            sums.result(out_gu.at[:, pl.ds(start, width)])
+        sums.result(out_gu)
         pair.drain()
-        for sums in (rest_a, first, rest_b):
-            sums.drain()
-
-
-def back_call(collective_id, dh, gate, up, wd, sum_gu, gate_halves):
+        sums.drain()
+
+
+def back_call(collective_id, dh, gate, up, wd, gate_halves):
     tokens, d = dh.shape
     tiles, half, dma = gate.shape[0], d // 2, pltpu.SemaphoreType.DMA
     ff = tiles * TILE
     now, before = clip(tiles), clip(tiles, 2)
     tile = spec((1, tokens, TILE), lambda j: (now(j), 0, 0))
-    parts = column_halves(ff)
     return pl.pallas_call(
         functools.partial(back_kernel, tiles, ff),
         name="back_0",
         grid=(tiles + 2,),
-        in_specs=[whole((tokens, d)), tile, tile, spec((1, 2 * TILE, d), lambda j: (0, lax.div(now(j), 2), 0)), HBM, HBM, HBM],
+        in_specs=[whole((tokens, d)), tile, tile, spec((1, 2 * TILE, d), lambda j: (0, lax.div(now(j), 2), 0)), HBM, HBM],
         out_specs=[
             spec((1, 2, tokens, TILE), lambda j: (now(j), 0, 0, 0)),
             spec((TILE, half), lambda j: (before(j), 0)),
@@ -1405,12 +1379,10 @@
         scratch_shapes=[pltpu.VMEM((3, tokens, TILE), BF16), pltpu.VMEM((2, tokens, TILE), BF16)]
         + PairSum.scratch(tiles, TILE, half)
         + [pltpu.VMEM(t.shape, BF16) for t in gate_halves]
-        + Rest.scratch(GATE_ROWS, parts[0][1])
-        + First.scratch(GATE_ROWS, parts[1][1])
-        + Rest.scratch(GATE_ROWS, parts[1][1])
-        + [dma((3,))],
+        + Rest.scratch(GATE_ROWS, ff)
+        + [dma((2,))],
         compiler_params=params(collective_id),
-    )(dh, gate, up, wd, *gate_halves, sum_gu)
+    )(dh, gate, up, wd, *gate_halves)
 
 
 def flat(m):
@@ -1433,10 +1405,9 @@
         gate0, up0, h1, a1, a0t = forward_call(x, wg, wu, wd)
         dgu1, a1t, down1 = layer_call(1, a1, dy, wg, wu, wd)
         blocks = (SIDE, SIDE, SIDE, GATE_ROWS, ff)
-        gu1, *down_halves = gate_up_first_call("gate_up_1", 2, a1t, dgu1, down1.reshape(windows))
-        gu1 = gu1.reshape(blocks)
-        dh1, sum_down1, *gate_halves = middle_call(3, dgu1, wg, wu, h1, dy, gu1, down_halves)
-        dgu0, down0, sum_gu1 = back_call(4, dh1, gate0, up0, wd, gu1, gate_halves)
+        gu1, sum_down1 = gate_up_first_call("gate_up_1", 2, a1t, dgu1, down1.reshape(windows))
+        dh1, *gate_halves = middle_call(3, dgu1, wg, wu, h1, dy, gu1.reshape(blocks))
+        dgu0, down0, sum_gu1 = back_call(4, dh1, gate0, up0, wd, gate_halves)
         sum_gu0, sum_down0 = gate_up_call("gate_up_0", 5, 3, a0t, dgu0, down0.reshape(windows))
 
         views = [(2, SIDE, SIDE, SIDE, GATE_ROWS, ff)] * 2 + [(2, SIDE, SIDE, 4 * 66, d)]

time: 652 us -> 655 us (level)
    pallas_call x1, Pallas kernels: 49.3 us -> 58.8 us  [gate_up_first_call(): pl.pallas_call(functools.partial(gate_up_first_kernel, tiles, cols), name...]
    pallas_call x1, Pallas kernels: 75.7 us -> 68.7 us  [back_call(): pl.pallas_call(functools.partial(back_kernel, tiles, ff), name='back_0',...]
where the time goes in v8:
time: 655 us; the launch traced here: 654 us
  Pallas kernels  647 us (99%)
    pallas_call x1, Pallas kernels, finish_call(): pl.pallas_call(functools.partial(finish_kernel, count), name='finish', ou...  182 us
    pallas_call x1, Pallas kernels, gate_up_call(): pl.pallas_call(functools.partial(gate_up_kernel, tiles, phases, cols), na...  96 us
    pallas_call x1, Pallas kernels, layer_call(): pl.pallas_call(functools.partial(layer_kernel, tiles), name='layer_1', gr...  76.2 us
    pallas_call x1, Pallas kernels, back_call(): pl.pallas_call(functools.partial(back_kernel, tiles, ff), name='back_0',...  68.7 us
    pallas_call x1, Pallas kernels, forward_call(): pl.pallas_call(functools.partial(forward_kernel, tiles), name='forward_0'...  63 us
    pallas_call x1, Pallas kernels, middle_call(): pl.pallas_call(functools.partial(middle_kernel, steps, ff), name='middle'...  59 us
    pallas_call x1, Pallas kernels, gate_up_first_call(): pl.pallas_call(functools.partial(gate_up_first_kernel, tiles, cols), name...  58.8 us
    pallas_call x1, Pallas kernels, write_call(): pl.pallas_call(lambda *refs: write_kernel(bounces, *refs[:6], refs[6:8],...  43.2 us

profile of v8, /device:TPU:1, one launch (start us, length us, event | category | flops | bytes accessed | tf_op | source)
XLA Modules:
  0.0 654.4 jit_solution(8356724024384056189)
XLA Ops:
  0.6 63.0 %forward_0.1 = (f32[11,1024,384]{2,1,0:T(8,128)}, f32[11,1024,384]{2,1,0:T(8,128)}, bf16[1024,1536]{1,0:T(8,128)(2,1)}, bf16[1024,1536]{1,0:T(8,128)(2,1)}, bf16[1536,1024]{1,0:T(8,128)(2,1)}) custom-call(bf16[1024,1536]{1,0:T(8,128)(2,1)} %bitcast.109, bf16[2,1536,4224]{2,1,0:T(8,128)(2,1)} %wg.5, bf16[2,1536,4224]{2,1,0:T(8,128)(2,1)} %wu.5, ...), custom_call_target="tpu_custom_call" | custom-call | tf_op jit(solution)/shard_map/forward_0/pallas_call | solution.py:765
  63.6 76.2 %layer_1.1 = (bf16[11,2,1024,384]{3,2,1,0:T(8,128)(2,1)}, bf16[1536,1024]{1,0:T(8,128)(2,1)}, bf16[4224,768]{1,0:T(8,128)(2,1)}) custom-call(bf16[1024,1536]{1,0:T(8,128)(2,1)} %get-tuple-element.40.a, bf16[1024,1536]{1,0:T(8,128)(2,1)} %bitcast.105, bf16[2,1536,4224]{2,1,0:T(8,128)(2,1)} %wg.5, bf16[2,1536,4224]{2,1,0:T(8,128)(2,1)} %wu.5, ...), custom_call_target="tpu_custom_call" | custom-call | tf_op jit(solution)/shard_map/layer_1/pallas_call | solution.py:876
  139.8 58.8 %gate_up_1.1 = (bf16[1536,4224]{1,0:T(8,128)(2,1)}, bf16[72,768]{1,0:T(8,128)(2,1)}) custom-call(bf16[1536,1024]{1,0:T(8,128)(2,1)} %get-tuple-element.43.at, bf16[11,2,1024,384]{3,2,1,0:T(8,128)(2,1)} %get-tuple-element.41.ahead.behind.dgu, bf16[11,2,1024,384]{3,2,1,0:T(8,128)(2,1)} %get-tuple-element.41.ahead.behind.dgu, bf16[4,4,264,768]{3,2,1,0:T(8,128)(2,1)} %bitcast.108), custom_call_target="tpu_custom_call" | custom-call | tf_op jit(solution)/shard_map/gate_up_1/pallas_call | solution.py:1238
  198.6 59.0 %middle.1 = (bf16[1024,1536]{1,0:T(8,128)(2,1)}, bf16[3,4,4,8,2176]{4,3,2,1,0:T(8,128)(2,1)}, bf16[3,4,4,8,2048]{4,3,2,1,0:T(8,128)(2,1)}) custom-call(bf16[11,2,1024,384]{3,2,1,0:T(8,128)(2,1)} %get-tuple-element.41.ahead.behind.dgu, bf16[2,1536,4224]{2,1,0:T(8,128)(2,1)} %wg.5, bf16[2,1536,4224]{2,1,0:T(8,128)(2,1)} %wu.5, ...), custom_call_target="tpu_custom_call" | custom-call | tf_op jit(solution)/shard_map/middle/pallas_call | solution.py:1310
  257.6 68.7 %back_0.1 = (bf16[11,2,1024,384]{3,2,1,0:T(8,128)(2,1)}, bf16[4224,768]{1,0:T(8,128)(2,1)}, bf16[24,4224]{1,0:T(8,128)(2,1)}) custom-call(bf16[1024,1536]{1,0:T(8,128)(2,1)} %get-tuple-element.46.dh, f32[11,1024,384]{2,1,0:T(8,128)} %get-tuple-element.47.gate, f32[11,1024,384]{2,1,0:T(8,128)} %get-tuple-element.48.up, bf16[2,4224,1536]{2,1,0:T(8,128)(2,1)} %wd.5, ...), custom_call_target="tpu_custom_call" | custom-call | tf_op jit(solution)/shard_map/back_0/pallas_call | solution.py:1368
  326.3 0.0 copy-start
  326.3 0.0 copy-start.2
  326.3 96.0 %gate_up_0.1 = (bf16[24,4224]{1,0:T(8,128)(2,1)}, bf16[72,768]{1,0:T(8,128)(2,1)}) custom-call(bf16[1536,1024]{1,0:T(8,128)(2,1)} %get-tuple-element.39.at, bf16[11,2,1024,384]{3,2,1,0:T(8,128)(2,1)} %get-tuple-element.51.ahead.behind, bf16[11,2,1024,384]{3,2,1,0:T(8,128)(2,1)} %get-tuple-element.51.ahead.behind, bf16[4,4,264,768]{3,2,1,0:T(8,128)(2,1)} %bitcast.107), custom_call_target="tpu_custom_call" | custom-call | tf_op jit(solution)/shard_map/gate_up_0/pallas_call | solution.py:1181
  422.3 0.0 copy-done
  422.3 0.0 copy-done.2
  422.4 0.0 copy-start.1
  422.4 0.9 copy-done.1
  423.3 0.0 copy-start.3
  423.3 0.9 copy-done.3
  424.2 182.5 %finish.1 = (bf16[2,4,4,4,24,4224]{5,4,3,2,1,0:T(8,128)(2,1)S(1)}, bf16[2,4,4,4,24,4224]{5,4,3,2,1,0:T(8,128)(2,1)}, bf16[2,4,4,264,1536]{4,3,2,1,0:T(8,128)(2,1...) custom-call(bf16[24,4224]{1,0:T(8,128)(2,1)S(1)} %copy-done.1, ...), custom_call_target="tpu_custom_call" | custom-call | flops 1000000000 | bytes 100000000 | tf_op jit(solution)/shard_map/finish/pallas_call | solution.py:592
  606.7 43.2 %write.1 = (bf16[2,4,4,4,24,4224]{5,4,3,2,1,0:T(8,128)(2,1)}, bf16[2,4,4,4,24,4224]{5,4,3,2,1,0:T(8,128)(2,1)}, bf16[2,4,4,264,1536]{4,3,2,1,0:T(8,128)(2,1)}) custom-call(bf16[2,4,4,4,24,4224]{5,4,3,2,1,0:T(8,128)(2,1)S(1)} %get-tuple-element.57.refs_0_, bf16[2,4,4,4,24,4224]{5,4,3,2,1,0:T(8,128)(2,1)} %get-tuple-element.58.refs_1_, ...), custom_call_target="tpu_custom_call" | custom-call | tf_op jit(solution)/shard_map/write/pallas_call | solution.py:644
  649.9 0.8 copy.26
  650.6 0.7 copy.27
  651.4 0.7 copy.28
  652.1 0.7 copy.29
  652.9 0.7 copy.30
  653.6 0.7 copy.31
Async XLA Ops:
  326.3 96.1 %copy-start = (bf16[24,4224]{1,0:T(8,128)(2,1)S(1)}, bf16[24,4224]{1,0:T(8,128)(2,1)}, u32[]{:S(2)}) copy-start(bf16[24,4224]{1,0:T(8,128)(2,1)} %get-tuple-element.54.refs_1_) | copy-start | bytes 608260
  326.3 96.1 %copy-start.2 = (bf16[72,768]{1,0:T(8,128)(2,1)S(1)}, bf16[72,768]{1,0:T(8,128)(2,1)}, u32[]{:S(2)}) copy-start(bf16[72,768]{1,0:T(8,128)(2,1)} %get-tuple-element.56.refs_3_) | copy-start | bytes 331780
  422.4 0.9 copy-start.1
  423.3 0.9 copy-start.3

commit v9 on v8

--- a/solution.py
+++ b/solution.py
@@ -1195,14 +1195,14 @@
     )(at, dgu, dgu, *sum_down)
 
 
-def gate_up_first_kernel(tiles, cols, at, ahead, behind, sum_down, out, out_down, *rest):
+def gate_up_first_kernel(tiles, cols, at, ahead, behind, sum_down, out, half0, half1, *rest):
     j = pl.program_id(0)
     place = Place()
     core = place.core
     pair = PairSum(place, tiles, *rest[:4])
     first = First.of(place, DOWN_WINDOW, cols, rest[4:9])
-    down = Rest.of(place, DOWN_WINDOW, cols, first.results(), rest[9:17])
-    loads = loads_down(sum_down, first, rest[17])
+    load_sem, save_sem = rest[9:11]
+    loads = loads_down(sum_down, first, load_sem)
 
     @pl.when(j == 0)
     def _():
@@ -1221,14 +1221,14 @@
     pl.when(j < tiles)(lambda: pair.copy(j).start())
 
     pl.when(j == 0)(lambda: end(loads))
-    pl.when(j <= tiles - 5)(lambda: spread(j, tiles - 4, 16, first.tick))
-    pl.when(j >= tiles - 5)(lambda: down.tick(j - tiles + 5))
+    spread(j, tiles + 2, 16, first.tick)
 
     @pl.when(j == tiles + 1)
     def _():
-        down.result(out_down)
+        saves = copies(first.results(), (half0, half1), save_sem)
+        begin(saves)
         first.drain()
-        down.drain()
+        end(saves)
 
 
 def gate_up_first_call(name, collective_id, at, dgu, sum_down):
@@ -1245,14 +1245,10 @@
             spec((1, 2, tokens, TILE), lambda j: (before(j), 0, 0, 0)),
             HBM,
         ],
-        out_specs=[spec((d, TILE), lambda j: (0, before(j))), whole((DOWN_WINDOW, cols))],
-        out_shape=[jax.ShapeDtypeStruct(s, BF16) for s in ((d, tiles * TILE), (DOWN_WINDOW, cols))],
-        scratch_shapes=[
-            *PairSum.scratch(tiles, d, TILE),
-            *First.scratch(DOWN_WINDOW, cols),
-            *Rest.scratch(DOWN_WINDOW, cols),
-            dma((SIDE,)),
-        ],
+        out_specs=[spec((d, TILE), lambda j: (0, before(j))), HBM, HBM],
+        out_shape=[jax.ShapeDtypeStruct((d, tiles * TILE), BF16)]
+        + [jax.ShapeDtypeStruct(s, BF16) for s in half_sums(DOWN_WINDOW, cols)],
+        scratch_shapes=[*PairSum.scratch(tiles, d, TILE), *First.scratch(DOWN_WINDOW, cols), dma((SIDE,)), dma((2,))],
         compiler_params=params(collective_id),
     )(at, dgu, dgu, sum_down)
 
@@ -1319,70 +1315,67 @@
     )(dgu, wg, wu, h, dy, sum_gu)
 
 
-def back_kernel(tiles, ff, dh, gate, up, wd, gate0, gate1, dgu, out, out_gu, p, dps, *rest):
+def back_kernel(tiles, ff, dh, gate, up, wd, gate0, gate1, down0, down1, dgu, out, out_gu, out_down, p, *rest):
     j = pl.program_id(0)
     place = Place()
-    core, half = place.core, dh.shape[1] // 2
+    half = dh.shape[1] // 2
     pair = PairSum(place, tiles, *rest[:4])
-    before = rest[4:6]
-    sums = Rest.of(place, GATE_ROWS, ff, before, rest[6:14])
-    loads = copies((gate0, gate1), before, rest[14])
+    before = rest[4:8]
+    gate_up = Rest.of(place, GATE_ROWS, ff, before[:2], rest[8:16])
+    down = Rest.of(place, DOWN_WINDOW, half, before[2:], rest[16:24])
+    loads = copies((gate0, gate1, down0, down1), before, rest[24])
 
     @pl.when(j == 0)
     def _():
         signal_all(near(place))
         begin(loads)
 
-    two_tiles_of_dp(j, tiles, dh, wd, dps)
-    pl.when(j >= 2)(lambda: pair.copy(j - 2).wait_recv())
-    tile = jnp.minimum(j, tiles - 1)
-    ours = p[lax.rem(j + 1, 3)]
-    for m in range(dh.shape[0] // ROWS):
-        r = pl.ds(m * ROWS, ROWS)
-        p[lax.rem(tile, 3), r, :], dgu[0, 0, r, :], dgu[0, 1, r, :] = hidden_back(gate[0, r, :], up[0, r, :], dps[lax.rem(tile, 2), r, :])
-    own = dot(ours, dh[:, pl.ds(pl.multiple_of(core * half, LANES), half)], TN)
-    out[...] = (own + pair.landing[lax.rem(j + tiles - 2, tiles)].astype(F32)).astype(BF16)
-
     @pl.when(j < tiles)
     def _():
-        slot = pair.reserve(j)
-        slot[...] = dot(p[lax.rem(j, 3)], dh[:, pl.ds(pl.multiple_of((1 - core) * half, LANES), half)], TN).astype(BF16)
-        pair.copy(j).start()
-
+        slot = lax.rem(j, 2)
+        for m in range(dh.shape[0] // ROWS):
+            r = pl.ds(m * ROWS, ROWS)
+            dp = dot(dh[r, :], wd[0], NT).astype(BF16)
+            p[slot, r, :], dgu[0, 0, r, :], dgu[0, 1, r, :] = hidden_back(gate[0, r, :], up[0, r, :], dp)
+
+    down_gradient(j, tiles, pair, p, dh, half, out)
     pl.when(j == 0)(lambda: end(loads))
-    sums.tick(j)
-
-    @pl.when(j == tiles + 1)
-    def _():
-        sums.result(out_gu)
-        pair.drain()
-        sums.drain()
-
-
-def back_call(collective_id, dh, gate, up, wd, gate_halves):
+    gate_up.tick(j)
+    pl.when(j >= tiles - 6)(lambda: down.tick(j - tiles + 6))
+
+    @pl.when(j == tiles)
+    def _():
+        gate_up.result(out_gu)
+        down.result(out_down)
+        gate_up.drain()
+        down.drain()
+
+
+def back_call(collective_id, dh, gate, up, wd, gate_halves, down_halves):
     tokens, d = dh.shape
     tiles, half, dma = gate.shape[0], d // 2, pltpu.SemaphoreType.DMA
     ff = tiles * TILE
-    now, before = clip(tiles), clip(tiles, 2)
+    now, before = clip(tiles), clip(tiles, 1)
     tile = spec((1, tokens, TILE), lambda j: (now(j), 0, 0))
+    sums = [(GATE_ROWS, ff), (DOWN_WINDOW, half)]
     return pl.pallas_call(
         functools.partial(back_kernel, tiles, ff),
         name="back_0",
-        grid=(tiles + 2,),
-        in_specs=[whole((tokens, d)), tile, tile, spec((1, 2 * TILE, d), lambda j: (0, lax.div(now(j), 2), 0)), HBM, HBM],
+        grid=(tiles + 1,),
+        in_specs=[whole((tokens, d)), tile, tile, spec((1, TILE, d), lambda j: (0, now(j), 0))] + [HBM] * 4,
         out_specs=[
             spec((1, 2, tokens, TILE), lambda j: (now(j), 0, 0, 0)),
             spec((TILE, half), lambda j: (before(j), 0)),
-            whole((GATE_ROWS, ff)),
+            *[whole(s) for s in sums],
         ],
-        out_shape=[jax.ShapeDtypeStruct(s, BF16) for s in ((tiles, 2, tokens, TILE), (ff, half), (GATE_ROWS, ff))],
-        scratch_shapes=[pltpu.VMEM((3, tokens, TILE), BF16), pltpu.VMEM((2, tokens, TILE), BF16)]
-        + PairSum.scratch(tiles, TILE, half)
-        + [pltpu.VMEM(t.shape, BF16) for t in gate_halves]
+        out_shape=[jax.ShapeDtypeStruct(s, BF16) for s in ((tiles, 2, tokens, TILE), (ff, half), *sums)],
+        scratch_shapes=[pltpu.VMEM((2, tokens, TILE), BF16), *PairSum.scratch(tiles, TILE, half)]
+        + [pltpu.VMEM(t.shape, BF16) for t in (*gate_halves, *down_halves)]
         + Rest.scratch(GATE_ROWS, ff)
-        + [dma((2,))],
+        + Rest.scratch(DOWN_WINDOW, half)
+        + [dma((4,))],
         compiler_params=params(collective_id),
-    )(dh, gate, up, wd, *gate_halves)
+    )(dh, gate, up, wd, *gate_halves, *down_halves)
 
 
 def flat(m):
@@ -1405,9 +1398,9 @@
         gate0, up0, h1, a1, a0t = forward_call(x, wg, wu, wd)
         dgu1, a1t, down1 = layer_call(1, a1, dy, wg, wu, wd)
         blocks = (SIDE, SIDE, SIDE, GATE_ROWS, ff)
-        gu1, sum_down1 = gate_up_first_call("gate_up_1", 2, a1t, dgu1, down1.reshape(windows))
+        gu1, *down_halves = gate_up_first_call("gate_up_1", 2, a1t, dgu1, down1.reshape(windows))
         dh1, *gate_halves = middle_call(3, dgu1, wg, wu, h1, dy, gu1.reshape(blocks))
-        dgu0, down0, sum_gu1 = back_call(4, dh1, gate0, up0, wd, gate_halves)
+        dgu0, down0, sum_gu1, sum_down1 = back_call(4, dh1, gate0, up0, wd, gate_halves, down_halves)
         sum_gu0, sum_down0 = gate_up_call("gate_up_0", 5, 3, a0t, dgu0, down0.reshape(windows))
 
         views = [(2, SIDE, SIDE, SIDE, GATE_ROWS, ff)] * 2 + [(2, SIDE, SIDE, 4 * 66, d)]

time: 655 us -> 638 us (0.974)
  Pallas kernels: 647 us -> 631 us
    pallas_call x1, Pallas kernels: 68.7 us -> 59.2 us  [back_call(): pl.pallas_call(functools.partial(back_kernel, tiles, ff), name='back_0',...]
    pallas_call x1, Pallas kernels: 58.8 us -> 49.3 us  [gate_up_first_call(): pl.pallas_call(functools.partial(gate_up_first_kernel, tiles, cols), name...]
where the time goes in v9:
time: 638 us
  Pallas kernels  631 us (99%)
    pallas_call x1, Pallas kernels, finish_call(): pl.pallas_call(functools.partial(finish_kernel, count), name='finish', ou...  182 us
    pallas_call x1, Pallas kernels, gate_up_call(): pl.pallas_call(functools.partial(gate_up_kernel, tiles, phases, cols), na...  97.2 us
    pallas_call x1, Pallas kernels, layer_call(): pl.pallas_call(functools.partial(layer_kernel, tiles), name='layer_1', gr...  76.2 us
    pallas_call x1, Pallas kernels, forward_call(): pl.pallas_call(functools.partial(forward_kernel, tiles), name='forward_0'...  63 us
    pallas_call x1, Pallas kernels, middle_call(): pl.pallas_call(functools.partial(middle_kernel, steps, ff), name='middle'...  61.2 us
    pallas_call x1, Pallas kernels, back_call(): pl.pallas_call(functools.partial(back_kernel, tiles, ff), name='back_0',...  59.2 us
    pallas_call x1, Pallas kernels, gate_up_first_call(): pl.pallas_call(functools.partial(gate_up_first_kernel, tiles, cols), name...  49.3 us
    pallas_call x1, Pallas kernels, write_call(): pl.pallas_call(lambda *refs: write_kernel(bounces, *refs[:6], refs[6:8],...  43.2 us

profile of v9, /device:TPU:1, one launch (start us, length us, event | category | flops | bytes accessed | tf_op | source)
XLA Modules:
  0.0 638.1 jit_solution(9127279083453803205)
XLA Ops:
  0.6 63.0 %forward_0.1 = (f32[11,1024,384]{2,1,0:T(8,128)}, f32[11,1024,384]{2,1,0:T(8,128)}, bf16[1024,1536]{1,0:T(8,128)(2,1)}, bf16[1024,1536]{1,0:T(8,128)(2,1)}, bf16[1536,1024]{1,0:T(8,128)(2,1)}) custom-call(bf16[1024,1536]{1,0:T(8,128)(2,1)} %bitcast.109, bf16[2,1536,4224]{2,1,0:T(8,128)(2,1)} %wg.5, bf16[2,1536,4224]{2,1,0:T(8,128)(2,1)} %wu.5, ...), custom_call_target="tpu_custom_call" | custom-call | tf_op jit(solution)/shard_map/forward_0/pallas_call | solution.py:765
  63.6 76.2 %layer_1.1 = (bf16[11,2,1024,384]{3,2,1,0:T(8,128)(2,1)}, bf16[1536,1024]{1,0:T(8,128)(2,1)}, bf16[4224,768]{1,0:T(8,128)(2,1)}) custom-call(bf16[1024,1536]{1,0:T(8,128)(2,1)} %get-tuple-element.42.a, bf16[1024,1536]{1,0:T(8,128)(2,1)} %bitcast.105, bf16[2,1536,4224]{2,1,0:T(8,128)(2,1)} %wg.5, bf16[2,1536,4224]{2,1,0:T(8,128)(2,1)} %wu.5, ...), custom_call_target="tpu_custom_call" | custom-call | tf_op jit(solution)/shard_map/layer_1/pallas_call | solution.py:876
  139.8 49.3 %gate_up_1.1 = (bf16[1536,4224]{1,0:T(8,128)(2,1)}, bf16[3,4,4,24,384]{4,3,2,1,0:T(8,128)(2,1)}, bf16[3,4,4,24,384]{4,3,2,1,0:T(8,128)(2,1)}) custom-call(bf16[1536,1024]{1,0:T(8,128)(2,1)} %get-tuple-element.45.at, bf16[11,2,1024,384]{3,2,1,0:T(8,128)(2,1)} %get-tuple-element.43.ahead.behind.dgu, ...), custom_call_target="tpu_custom_call" | custom-call | tf_op jit(solution)/shard_map/gate_up_1/pallas_call | solution.py:1238
  189.1 61.2 %middle.1 = (bf16[1024,1536]{1,0:T(8,128)(2,1)}, bf16[3,4,4,8,2176]{4,3,2,1,0:T(8,128)(2,1)}, bf16[3,4,4,8,2048]{4,3,2,1,0:T(8,128)(2,1)}) custom-call(bf16[11,2,1024,384]{3,2,1,0:T(8,128)(2,1)} %get-tuple-element.43.ahead.behind.dgu, bf16[2,1536,4224]{2,1,0:T(8,128)(2,1)} %wg.5, bf16[2,1536,4224]{2,1,0:T(8,128)(2,1)} %wu.5, ...), custom_call_target="tpu_custom_call" | custom-call | tf_op jit(solution)/shard_map/middle/pallas_call | solution.py:1306
  250.3 59.2 %back_0.1 = (bf16[11,2,1024,384]{3,2,1,0:T(8,128)(2,1)}, bf16[4224,768]{1,0:T(8,128)(2,1)}, bf16[24,4224]{1,0:T(8,128)(2,1)}, bf16[72,768]{1,0:T(8,128)(2,1)}) custom-call(bf16[1024,1536]{1,0:T(8,128)(2,1)} %get-tuple-element.48.dh, f32[11,1024,384]{2,1,0:T(8,128)} %get-tuple-element.49.gate, f32[11,1024,384]{2,1,0:T(8,128)} %get-tuple-element.50.up, ...), custom_call_target="tpu_custom_call" | custom-call | tf_op jit(solution)/shard_map/back_0/pallas_call | solution.py:1361
  309.5 0.0 copy-start
  309.5 0.0 copy-start.2
  309.5 97.2 %gate_up_0.1 = (bf16[24,4224]{1,0:T(8,128)(2,1)}, bf16[72,768]{1,0:T(8,128)(2,1)}) custom-call(bf16[1536,1024]{1,0:T(8,128)(2,1)} %get-tuple-element.41.at, bf16[11,2,1024,384]{3,2,1,0:T(8,128)(2,1)} %get-tuple-element.55.ahead.behind, bf16[11,2,1024,384]{3,2,1,0:T(8,128)(2,1)} %get-tuple-element.55.ahead.behind, bf16[4,4,264,768]{3,2,1,0:T(8,128)(2,1)} %bitcast.107), custom_call_target="tpu_custom_call" | custom-call | tf_op jit(solution)/shard_map/gate_up_0/pallas_call | solution.py:1181
  406.7 0.0 copy-done
  406.7 0.0 copy-done.2
  406.7 0.0 copy-start.1
  406.7 0.9 copy-done.1
  407.6 0.0 copy-start.3
  407.6 0.9 copy-done.3
  408.5 181.8 %finish.1 = (bf16[2,4,4,4,24,4224]{5,4,3,2,1,0:T(8,128)(2,1)S(1)}, bf16[2,4,4,4,24,4224]{5,4,3,2,1,0:T(8,128)(2,1)}, bf16[2,4,4,264,1536]{4,3,2,1,0:T(8,128)(2,1...) custom-call(bf16[24,4224]{1,0:T(8,128)(2,1)S(1)} %copy-done.1, ...), custom_call_target="tpu_custom_call" | custom-call | flops 1000000000 | bytes 100000000 | tf_op jit(solution)/shard_map/finish/pallas_call | solution.py:592
  590.4 43.2 %write.1 = (bf16[2,4,4,4,24,4224]{5,4,3,2,1,0:T(8,128)(2,1)}, bf16[2,4,4,4,24,4224]{5,4,3,2,1,0:T(8,128)(2,1)}, bf16[2,4,4,264,1536]{4,3,2,1,0:T(8,128)(2,1)}) custom-call(bf16[2,4,4,4,24,4224]{5,4,3,2,1,0:T(8,128)(2,1)S(1)} %get-tuple-element.61.refs_0_, bf16[2,4,4,4,24,4224]{5,4,3,2,1,0:T(8,128)(2,1)} %get-tuple-element.62.refs_1_, ...), custom_call_target="tpu_custom_call" | custom-call | tf_op jit(solution)/shard_map/write/pallas_call | solution.py:644
  633.6 0.8 copy.26
  634.3 0.7 copy.27
  635.1 0.7 copy.28
  635.8 0.7 copy.29
  636.6 0.7 copy.30
  637.3 0.7 copy.31
Async XLA Ops:
  309.5 97.2 %copy-start = (bf16[24,4224]{1,0:T(8,128)(2,1)S(1)}, bf16[24,4224]{1,0:T(8,128)(2,1)}, u32[]{:S(2)}) copy-start(bf16[24,4224]{1,0:T(8,128)(2,1)} %get-tuple-element.58.refs_1_) | copy-start | bytes 608260
  309.5 97.2 %copy-start.2 = (bf16[72,768]{1,0:T(8,128)(2,1)S(1)}, bf16[72,768]{1,0:T(8,128)(2,1)}, u32[]{:S(2)}) copy-start(bf16[72,768]{1,0:T(8,128)(2,1)} %get-tuple-element.60.refs_3_) | copy-start | bytes 331780
  406.7 0.9 copy-start.1
  407.6 0.9 copy-start.3
